TPU v7x, 32 devices: a whole 2x2x4 slice. The times are simulated.
32 devices in a mesh: rep: 8 (over y, x, core), grp: 4 (over z).
Axes of the slice: x: 2, y: 2, z: 4, core: 2. Of those that a mesh axis runs over, the one named last changes fastest.
Arguments:
- frames: bfloat16 [8192, 768], P(('rep', 'grp')), may hold values from -6 to 6
- cotangent: bfloat16 [8192, 768], P(('rep', 'grp')), may hold values from -6 to 6
- params: bfloat16 [4, 1771776], P('grp'), may hold values from -8 to 8, as said below
- first_moment: float32 [4, 1771776], P('grp'), as said below
- second_moment: float32 [4, 1771776], P('grp'), as said below
Outputs:
- out_frames: bfloat16 [8192, 768], P(('rep', 'grp'))
- frames_grad: bfloat16 [8192, 768], P(('rep', 'grp'))
- param_grad: float32 [4, 1771776], P('grp')
- new_params: float32 [4, 1771776], P('grp')
- new_first: float32 [4, 1771776], P('grp')
- new_second: float32 [4, 1771776], P('grp')
Inputs may be any that keep to these rules, and one draw needn't show every extreme that they name: `params`: laid out as the first step says; gains lie between 0.5 and 1.5. `first_moment`: laid out as the first step says. `second_moment`: Positive; laid out as the first step says.
All inputs are finite; a program needn't handle non-finite values.
Results may differ from a plain program's by a relative error of at most 0.012.
The roundings to bfloat16 on the way count: a program that leaves them out, or rounds other values in their place, can miss the bound.
Values may be sent and summed in bfloat16 or wider, within the bound.
A program may use at most 256 MiB of HBM per device.

v0:
```python
import jax
import jax.numpy as jnp
from jax import lax
from jax.sharding import PartitionSpec as P

D = 768
FF = 3072
HDIM = 64


EPS_NORM = 1e-05
BETA_ONE = 0.9
BETA_TWO = 0.98
ADAM_EPS = 1e-06
LEARN_RATE = 0.006
DECAY = 0.01
adam_step = 4


def tensor_shapes():
    return [
        (D, 1),
        (D, 1),
        (D, 3 * D),
        (2 * D, 1),
        (D, D),
        (D, 1),
        (D, 1),
        (D, 1),
        (D, FF),
        (FF, 1),
        (FF, D),
        (D, 1),
    ]


def unpack(flat):
    groups = flat.shape[0]
    result = []
    offset = 0
    for height, breadth in tensor_shapes():
        length = height * breadth // groups
        block = flat[:, offset : offset + length]
        if breadth > 1:
            result.append(block.reshape(height, breadth))
        else:
            result.append(block.reshape(height))
        offset += length
    return tuple(result)


def pack(tensors, groups):
    return jnp.concatenate([item.reshape(groups, -1) for item in tensors], axis=1)


def norm_forward(values):
    center = values - jnp.mean(values, axis=-1, keepdims=True)
    inverse = lax.rsqrt(jnp.mean(center * center, axis=-1, keepdims=True) + EPS_NORM)
    return (center * inverse, inverse)


def norm_backward(upstream, normalized, inverse, gain):
    scaled = upstream * gain
    return inverse * (
        scaled
        - jnp.mean(scaled, axis=-1, keepdims=True)
        - normalized * jnp.mean(scaled * normalized, axis=-1, keepdims=True)
    )


def gelu(values):
    return 0.5 * values * (1.0 + lax.erf(values * 0.7071067811865476))


def gelu_slope(values):
    return (
        0.5 * (1.0 + lax.erf(values * 0.7071067811865476))
        + values * jnp.exp(-0.5 * values * values) * 0.3989422804014327
    )


def to_pairs(matrix):
    heads = matrix.shape[1] // HDIM
    return matrix.reshape(matrix.shape[0], heads // 2, 2, HDIM).transpose(1, 0, 2, 3)


def from_pairs(stacked):
    return stacked.transpose(1, 0, 2, 3).reshape(stacked.shape[1], -1)


def attend(query, keys, values):
    scale = HDIM ** (-0.5)

    def attend_one_pair(items):
        query_pair, key_pair, value_pair = items
        scores = (
            jnp.einsum("qhd,khd->hqk", query_pair, key_pair, preferred_element_type=jnp.float32)
            * scale
        )
        highest = jnp.max(scores, axis=-1, keepdims=True)
        log_total = highest + jnp.log(jnp.sum(jnp.exp(scores - highest), axis=-1, keepdims=True))
        shares = jnp.exp(scores - log_total).astype(jnp.bfloat16)
        mixed = jnp.einsum("hqk,khd->qhd", shares, value_pair, preferred_element_type=jnp.float32)
        return (mixed, log_total[..., 0])

    mixed, log_total = lax.map(attend_one_pair, (to_pairs(query), to_pairs(keys), to_pairs(values)))
    return (from_pairs(mixed).astype(jnp.bfloat16), log_total)


def row_centre(upstream, attended):
    product = to_pairs(upstream).astype(jnp.float32) * to_pairs(attended).astype(jnp.float32)
    return jnp.sum(product, axis=-1).transpose(0, 2, 1)


def back_blocks(query, keys, values, upstream, log_total, centre):
    scale = HDIM ** (-0.5)

    def back_one_pair(items):
        query_pair, key_pair, value_pair, upstream_pair, log_pair, centre_pair = items
        scores = (
            jnp.einsum("qhd,khd->hqk", query_pair, key_pair, preferred_element_type=jnp.float32)
            * scale
        )
        shares = jnp.exp(scores - log_pair[..., None])
        share_grad = jnp.einsum(
            "qhd,khd->hqk", upstream_pair, value_pair, preferred_element_type=jnp.float32
        )
        score_grad = (shares * (share_grad - centre_pair[..., None]) * scale).astype(jnp.bfloat16)
        result = []
        result.append(
            jnp.einsum("hqk,khd->qhd", score_grad, key_pair, preferred_element_type=jnp.float32)
        )
        result.append(
            jnp.einsum("hqk,qhd->khd", score_grad, query_pair, preferred_element_type=jnp.float32)
        )
        result.append(
            jnp.einsum(
                "hqk,qhd->khd",
                shares.astype(jnp.bfloat16),
                upstream_pair,
                preferred_element_type=jnp.float32,
            )
        )
        return tuple(result)

    stacked = (
        to_pairs(query),
        to_pairs(keys),
        to_pairs(values),
        to_pairs(upstream),
        log_total,
        centre,
    )
    outputs = lax.map(back_one_pair, stacked)
    return tuple((from_pairs(item) for item in outputs))


def adam_update(params, grad, first, second):
    new_first = BETA_ONE * first + (1.0 - BETA_ONE) * grad
    new_second = BETA_TWO * second + (1.0 - BETA_TWO) * grad * grad
    first_hat = new_first / (1.0 - BETA_ONE**adam_step)
    second_hat = new_second / (1.0 - BETA_TWO**adam_step)
    current = params.astype(jnp.float32)
    new_params = current - LEARN_RATE * (
        first_hat / (jnp.sqrt(second_hat) + ADAM_EPS) + DECAY * current
    )
    return (new_first, new_second, new_params)


def on_device(frames, cotangent, params, first_moment, second_moment):
    gathered = lax.all_gather(params, "grp", axis=0, tiled=True)
    (
        gain_one,
        shift_one,
        qkv_weight,
        qv_bias,
        out_weight,
        out_bias,
        gain_two,
        shift_two,
        up_weight,
        up_bias,
        down_weight,
        down_bias,
    ) = unpack(gathered)
    width = frames.shape[1]
    inputs = frames.astype(jnp.float32)
    normal_one, inverse_one = norm_forward(inputs)
    normed_one = (normal_one * gain_one.astype(jnp.float32) + shift_one.astype(jnp.float32)).astype(
        jnp.bfloat16
    )
    bias_three = jnp.concatenate(
        [
            qv_bias[:width].astype(jnp.float32),
            jnp.zeros((width,), jnp.float32),
            qv_bias[width:].astype(jnp.float32),
        ]
    )
    projected = (
        jnp.dot(normed_one, qkv_weight, preferred_element_type=jnp.float32) + bias_three
    ).astype(jnp.bfloat16)
    query = projected[:, :width]
    key_value = lax.all_gather(projected[:, width:], "grp", axis=0, tiled=True)
    keys = key_value[:, :width]
    values = key_value[:, width:]
    attended, log_total = attend(query, keys, values)
    middle = (
        jnp.dot(attended, out_weight, preferred_element_type=jnp.float32)
        + out_bias.astype(jnp.float32)
        + inputs
    )
    normal_two, inverse_two = norm_forward(middle)
    normed_two = (normal_two * gain_two.astype(jnp.float32) + shift_two.astype(jnp.float32)).astype(
        jnp.bfloat16
    )
    hidden_pre = jnp.dot(
        normed_two, up_weight, preferred_element_type=jnp.float32
    ) + up_bias.astype(jnp.float32)
    activated = gelu(hidden_pre).astype(jnp.bfloat16)
    out_frames = (
        jnp.dot(activated, down_weight, preferred_element_type=jnp.float32)
        + down_bias.astype(jnp.float32)
        + middle
    ).astype(jnp.bfloat16)
    (
        gain_one,
        shift_one,
        qkv_weight,
        qv_bias,
        out_weight,
        out_bias,
        gain_two,
        shift_two,
        up_weight,
        up_bias,
        down_weight,
        down_bias,
    ) = unpack(lax.all_gather(params, "grp", axis=0, tiled=True))
    upstream = cotangent.astype(jnp.float32)
    pre_grad = jnp.dot(cotangent, down_weight.T, preferred_element_type=jnp.float32) * gelu_slope(
        hidden_pre
    )
    pre_grad_half = pre_grad.astype(jnp.bfloat16)
    normed_two_grad = jnp.dot(pre_grad_half, up_weight.T, preferred_element_type=jnp.float32)
    middle_grad = upstream + norm_backward(
        normed_two_grad, normal_two, inverse_two, gain_two.astype(jnp.float32)
    )
    middle_half = middle_grad.astype(jnp.bfloat16)
    attended_grad = jnp.dot(middle_half, out_weight.T, preferred_element_type=jnp.float32).astype(
        jnp.bfloat16
    )
    centre = row_centre(attended_grad, attended)
    query_grad, key_grad, value_grad = back_blocks(
        query, keys, values, attended_grad, log_total, centre
    )
    owned = lax.psum_scatter(
        jnp.concatenate([key_grad, value_grad], axis=1), "grp", scatter_dimension=0, tiled=True
    )
    projected_grad = jnp.concatenate([query_grad, owned], axis=1).astype(jnp.bfloat16)
    normed_one_grad = jnp.dot(projected_grad, qkv_weight.T, preferred_element_type=jnp.float32)
    frames_grad = (
        middle_grad
        + norm_backward(normed_one_grad, normal_one, inverse_one, gain_one.astype(jnp.float32))
    ).astype(jnp.bfloat16)
    grads = (
        jnp.sum(normed_one_grad * normal_one, axis=0),
        jnp.sum(normed_one_grad, axis=0),
        jnp.dot(normed_one.T, projected_grad, preferred_element_type=jnp.float32),
        jnp.concatenate([jnp.sum(query_grad, axis=0), jnp.sum(owned[:, width:], axis=0)]),
        jnp.dot(attended.T, middle_half, preferred_element_type=jnp.float32),
        jnp.sum(middle_grad, axis=0),
        jnp.sum(normed_two_grad * normal_two, axis=0),
        jnp.sum(normed_two_grad, axis=0),
        jnp.dot(normed_two.T, pre_grad_half, preferred_element_type=jnp.float32),
        jnp.sum(pre_grad, axis=0),
        jnp.dot(activated.T, cotangent, preferred_element_type=jnp.float32),
        jnp.sum(upstream, axis=0),
    )
    groups = gathered.shape[0]
    full = pack(grads, groups)
    replicas = lax.axis_size("rep")
    owned_sum = lax.psum_scatter(full, "grp", scatter_dimension=0, tiled=True)
    total = lax.psum(owned_sum, "rep")
    param_grad = total / replicas
    new_first, new_second, new_params = adam_update(params, param_grad, first_moment, second_moment)
    return (out_frames, frames_grad, param_grad, new_params, new_first, new_second)


def solution(mesh):
    in_specs = (
        P(("rep", "grp"), None),
        P(("rep", "grp"), None),
        P("grp", None),
        P("grp", None),
        P("grp", None),
    )
    out_specs = (
        P(("rep", "grp"), None),
        P(("rep", "grp"), None),
        P("grp", None),
        P("grp", None),
        P("grp", None),
        P("grp", None),
    )
    return jax.shard_map(
        on_device, mesh=mesh, in_specs=in_specs, out_specs=out_specs, check_vma=False
    )
```

profile of v0, /device:TPU:28, one launch (start us, length us, event | category | flops | bytes accessed | tf_op | source)
XLA Modules:
  0.0 2067.2 jit_solution(2643180612140104417)
XLA Ops:
  9.2 475.2 %all-gather.6.cloned.1.call-done = bf16[4,1,1771776]{2,1,0:T(2,128)(2,1)} async-done(((bf16[1,1,1771776]{2,1,0:T(2,128)(2,1)}), bf16[4,1,1771776]{2,1,0:T(2,128)(2,1)}) %all-gather.6.cloned.1.call-update) | async-done | bytes 14174224 | tf_op jit(solution)/shard_map/all_gather | solution.py:171
  484.4 20.3 copy.25
  505.5 4.5 slice.85
  510.9 7.3 reshape.232
  518.3 3.2 fusion.43
  522.7 11.2 fusion.80
  534.0 1.5 slice.92
  537.1 2.1 reshape.236
  540.6 8.9 reshape.237
  549.6 9.0 reshape.238
  558.6 26.1 %all-gather.4.cloned.1.call-done = bf16[1024,1536]{1,0:T(8,128)(2,1)} async-done(((bf16[256,1536]{1,0:T(8,128)(2,1)}), bf16[1024,1536]{1,0:T(8,128)(2,1)}) %all-gather.4.cloned.1.call-update) | async-done | bytes 3145744 | tf_op jit(solution)/shard_map/all_gather | solution.py:203
  584.7 3.2 fusion.81
  588.7 2.1 copy.21
  590.8 22.2 %while.28 = (s32[]{:T(128)}, bf16[6,256,2,64]{1,3,2,0:T(8,128)(2,1)}, f32[6,2,256]{2,1,0:T(2,128)}, bf16[6,1024,2,64]{1,3,2,0:T(8,128)(2,1)S(1)}, bf16[6,256,2,6...) while((s32[]{:T(128)}, bf16[6,256,2,64]{1,3,2,0:T(8,128)(2,1)}, ...), condition=%wide.region_5.6_spmd.clone, body=%wide.region_2.5_spmd.sunk.clone | while | flops 138411520 | bytes 7030865 | solution.py:106
  590.8 1.4 multiply_reduce_fusion.9
  614.1 1.9 fusion.82
  616.4 5.4 multiply_convert_fusion.1
  621.9 3.0 fusion.83
  624.9 2.2 multiply_reduce_fusion.1
  629.6 1.9 copy.22
  631.5 1.8 multiply_reduce_fusion.2
  633.3 54.1 %while.29 = (s32[]{:T(128)}, f32[6,256,2,64]{1,3,2,0:T(8,128)}, f32[6,1024,2,64]{1,3,2,0:T(8,128)}, f32[6,1024,2,64]{1,3,2,0:T(8,128)}, bf16[6,1024,2,64]{1,3,2,...) while((s32[]{:T(128)}, f32[6,256,2,64]{1,3,2,0:T(8,128)}, ...), condition=%wide.region_12.13_spmd.clone, body=%wide.region_11.12_spmd.sunk.clone | while | flops 340262912 | bytes 11684977 | solution.py:154
  635.3 1.7 multiply_convert_fusion.4
  638.2 1.9 fusion.152
  640.1 2.2 fusion.153
  644.3 1.7 multiply_convert_fusion.4
  647.2 1.9 fusion.152
  649.1 2.2 fusion.153
  653.3 1.7 multiply_convert_fusion.4
  656.2 2.0 fusion.152
  658.1 2.2 fusion.153
  662.4 1.7 multiply_convert_fusion.4
  665.2 2.0 fusion.152
  667.2 2.2 fusion.153
  671.4 1.7 multiply_convert_fusion.4
  674.2 1.9 fusion.152
  676.2 2.2 fusion.153
  680.4 1.7 multiply_convert_fusion.4
  683.3 1.9 fusion.152
  685.2 2.2 fusion.153
  687.4 6.7 pad_maximum_fusion
  696.1 1.9 fusion.72
  698.0 4.4 reshape.246
  704.4 6.6 fusion.66
  711.1 13.9 reshape.250
  725.6 6.4 fusion.84
  732.0 12.3 reshape.252
  744.4 61.2 %reduce-scatter.2.cloned.1.call-done = f32[256,1536]{0,1:T(8,128)} async-done(((f32[1024,1536]{0,1:T(8,128)}), f32[256,1536]{0,1:T(8,128)}) %reduce-scatter.2.cloned.1.call-update) | async-done | bytes 1572880 | tf_op jit(solution)/shard_map/reduce_scatter | solution.py:256
  805.6 1.5 convert.17
  807.1 4.8 fusion.64
  811.9 4.3 fusion.70
  817.5 9.6 reshape.245
  828.7 1.5 dynamic-update-slice.1
  830.2 6.5 constant_dynamic-update-slice_fusion.1
  837.3 1.5 constant_dynamic-update-slice_fusion
  840.2 1.4 dynamic-update-slice.6
  842.9 49.6 %dynamic-update-slice.8 = f32[4,1771776]{1,0:T(4,128)} dynamic-update-slice(f32[4,1771776]{1,0:T(4,128)} %dynamic-update-slice.7, f32[4,589824]{1,0:T(4,128)} %reshape.250, s32[]{} %constant.100, s32[]{} %constant.109) | dynamic-update-slice | bytes 18874372
  892.5 1.5 dynamic-update-slice.9
  894.1 49.2 %dynamic-update-slice.10 = f32[4,1771776]{1,0:T(4,128)} dynamic-update-slice(f32[4,1771776]{1,0:T(4,128)} %dynamic-update-slice.9, f32[4,589824]{1,0:T(4,128)} %reshape.252, s32[]{} %constant.100, s32[]{} %constant.111) | dynamic-update-slice | bytes 18874372
  945.9 933.0 %all-reduce.6.cloned.1.call-done = f32[4,1771776]{1,0:T(4,128)} async-done(((f32[4,1771776]{1,0:T(4,128)}), f32[4,1771776]{1,0:T(4,128)}) %all-reduce.6.cloned.1.call-update) | async-done | bytes 28348432
  1878.9 13.2 constant_dynamic-slice_fusion.2
  1893.6 4.5 fusion.50
  1899.2 108.2 %all-reduce.4.cloned.1.call-done = f32[1,1771776]{1,0:T(1,128)} async-done(((f32[1,1771776]{1,0:T(1,128)}), f32[1,1771776]{1,0:T(1,128)}) %all-reduce.4.cloned.1.call-update) | async-done | bytes 7087120 | tf_op jit(solution)/shard_map/psum | solution.py:283
  2007.5 52.7 %multiply_subtract_fusion = (f32[1,1771776]{1,0:T(1,128)}, f32[1,1771776]{1,0:T(1,128)}, f32[1,1771776]{1,0:T(1,128)}, f32[1,1771776]{1,0:T(1,128)}) fusion(bf16[1,1771776]{1,0:T(2,128)(2,1)} %param.11, f32[1,1771776]{1,0:T(1,128)} %all-reduce.4.cloned.1.call-done, f32[1,1771776]{1,0:T(1,128)} %param.12, f32[1,1771776]{1,0:T(1,128)} %param.13), kind=kLoop, calls=%fused_computation.56 | loop fusion | flops 30120192 | bytes 53153280 | tf_op jit(solution)/shard_map/sub | solution.py:164
  (190 shorter events, 68.2 us)
Async XLA Ops:
  7.2 477.2 %all-gather.6.cloned.1.call-start = ((), (), s32[]{:S(2)}) async-start(), calls=%async_computation.4 | async-start | bytes 35435520 | tf_op jit(solution)/shard_map/all_gather | solution.py:171
  7.2 1.6 copy-start.3
  7.9 576.8 %all-gather.4.cloned.1.call-start = ((), (), s32[]{:S(2)}) async-start(), calls=%async_computation.1 | async-start | bytes 3932160 | tf_op jit(solution)/shard_map/all_gather | solution.py:203
  8.9 509.4 %copy-start.14 = (f32[256]{0:T(256)}, f32[256]{0:T(256)S(1)}, u32[]{:S(2)}) copy-start(f32[256]{0:T(256)S(1)} %broadcast_multiply_fusion.6) | copy-start | bytes 3076
  9.2 509.1 %copy-start.24 = (f32[256]{0:T(256)}, f32[256]{0:T(256)S(1)}, u32[]{:S(2)}) copy-start(f32[256]{0:T(256)S(1)} %add_rsqrt_fusion.1) | copy-start | bytes 3076
  504.7 6.1 copy-start
  522.5 283.1 %reduce-scatter.2.cloned.1.call-start = ((), (), s32[]{:S(2)}) async-start(), calls=%async_computation.2 | async-start | bytes 7864320 | tf_op jit(solution)/shard_map/reduce_scatter | solution.py:256
  613.0 1.1 copy-start.1
  613.0 3.3 copy-start.30
  616.1 11.0 copy-start.16
  616.1 5.7 slice-start
  616.3 10.7 copy-start.27
  616.4 5.5 slice-start.1
  616.4 5.5 copy-start.9
  616.4 8.5 slice-start.2
  621.8 3.0 slice-start.3
  624.9 2.2 copy-start.11
  627.0 1.3 copy-start.2
  694.1 1.1 copy-start.7
  694.1 2.0 copy-start.5
  694.1 1184.8 %all-reduce.6.cloned.1.call-start = ((), (), s32[]{:S(2)}) async-start(), calls=%async_computation.5 | async-start | bytes 56696832
  698.0 4.4 copy-start.19
  698.0 5.1 copy-start.33
  698.0 5.8 copy-start.32
  698.0 6.4 copy-start.17
  698.0 6.4 copy-start.28
  711.1 13.9 copy-start.29
  711.1 14.6 copy-start.10
  732.0 12.3 copy-start.18
  744.3 62.8 %copy-start.15 = (f32[256]{0:T(256)S(1)}, f32[256]{0:T(256)}, u32[]{:S(2)}) copy-start(f32[256]{0:T(256)} %copy-done.14) | copy-start | bytes 3076
  744.3 62.8 %copy-start.25 = (f32[256]{0:T(256)S(1)}, f32[256]{0:T(256)}, u32[]{:S(2)}) copy-start(f32[256]{0:T(256)} %copy-done.24) | copy-start | bytes 3076
  817.5 9.6 copy-start.6
  830.1 6.6 copy-start.31
  830.1 7.2 copy-start.4
  836.7 2.2 copy-start.23
  836.7 3.5 copy-start.22
  836.7 4.9 copy-start.21
  842.9 49.6 %copy-start.13 = (f32[4,768]{1,0:T(4,128)S(1)}, f32[4,768]{1,0:T(4,128)}, u32[]{:S(2)}) copy-start(f32[4,768]{1,0:T(4,128)} %reshape.251) | copy-start | bytes 36868
  944.7 0.7 copy-start.36
  944.7 1062.8 %all-reduce.4.cloned.1.call-start = ((), (), s32[]{:S(2)}) async-start(), calls=%async_computation.3 | async-start | bytes 14174208 | tf_op jit(solution)/shard_map/psum | solution.py:283
  1892.1 0.7 copy-start.20
  1892.1 1.4 copy-start.8
  1893.6 4.6 copy-start.35
  1893.6 4.6 copy-start.34
  1893.6 4.6 copy-start.12
  1893.6 4.6 copy-start.26
Sparse Core Ops, SparseCore 0:
  9.6 474.7 all-gather.5
  522.6 62.0 all-gather.3
  694.2 111.2 reduce-scatter.1
  944.8 934.0 all-reduce.5
  1892.3 115.1 all-reduce.3
where the time goes:
time: 2080 us; the launch traced here: 2070 us
  waiting for transfers between devices  1600 us (77%)
  local copies, waits for them, and re-layouts  261 us (13%)
  matrix products  111 us (5%)
  other arithmetic  75.3 us (4%)
    unnamed x6, waiting for transfers between devices  934 us
    all_gather x1, waiting for transfers between devices, on_device(): gathered = lax.all_gather(params, 'grp', axis=0, tiled=True)  475 us
    unnamed x95, local copies, waits for them, and re-layouts  154 us
    psum x1, waiting for transfers between devices, on_device(): total = lax.psum(owned_sum, 'rep')  108 us
    reduce_scatter x1, waiting for transfers between devices, on_device(): lax.psum_scatter(jnp.concatenate([key_grad, value_grad], axis=1), 'grp',...  61.2 us
    sub x1, other arithmetic, adam_update(): current - LEARN_RATE * (first_hat / (jnp.sqrt(second_hat) + ADAM_EPS) + D...  52.7 us
    reshape x11, local copies, waits for them, and re-layouts, pack(): item.reshape(groups, -1)  44.3 us
  transfers between devices with their start and end apart: 5, of which 5 were waited for; matrix products, arithmetic and copies ran while one was open for 4% of the time, Pallas kernels for 0%

commit v1 on v0

v1 whole, which is shorter than its diff:
```python
import functools
import jax
import jax.numpy as jnp
from jax import lax
from jax.sharding import PartitionSpec as P
from jax.experimental import pallas as pl
from jax.experimental.pallas import tpu as pltpu

MESH = pl.DeviceIdType.MESH
BF = jnp.bfloat16
F32 = jnp.float32
D = 768
FF = 3072
HDIM = 64
LANE = 128
FLAT = 1771776
FROWS = FLAT // LANE


class Mat:
    def __init__(self, offset, block, cols, suba, subb):
        self.offset, self.block, self.cols = offset, block, cols
        self.tiles = cols // LANE
        self.row0 = offset // LANE
        self.shifted = offset % LANE != 0
        self.quarter = block // 4
        self.half = cols // 2
        self.sub = (suba, subb)


QKV = Mat(384, 192, 2304, (0, 48, 0, 640), (0, 48, 640, 512))
OUT = Mat(443136, 192, 768, (0, 48, 0, 128), (0, 48, 128, 256))
UP = Mat(591168, 192, 3072, (0, 48, 0, 768), (0, 48, 768, 768))
DOWN = Mat(1181760, 768, 768, (0, 96, 0, 384), (96, 96, 0, 384))
MATS = (QKV, OUT, UP, DOWN)
SMALL = ((0, 3), (3459, 3), (4614, 5), (9226, 7), (13840, 2))
SROWS = 24


def flip(index, bit):
    return index + bit - 2 * bit * ((index // bit) % 2)


def mo(value, by):
    return pl.multiple_of(value, by)


def part(ref, m, r, k, h, sub=None):
    r0, rn, c0, cn = m.sub[sub] if sub is not None else (0, m.quarter, 0, m.half)
    row = mo(r * m.block + k * m.quarter + r0, 16)
    col = mo(h * m.half + c0, LANE)
    return ref.at[pl.ds(row, rn), pl.ds(col, cn)]


def slab(ref, m, r, h):
    return ref.at[pl.ds(mo(r * m.block, 16), m.block), pl.ds(mo(h * m.half, LANE), m.half)]


def remote(src, dst, send, recv, rep, grp):
    return pltpu.make_async_remote_copy(
        src_ref=src, dst_ref=dst, send_sem=send, recv_sem=recv,
        device_id={"rep": rep, "grp": grp}, device_id_type=MESH)


def greet(rep, g, groups, everyone=False):
    barrier = pltpu.get_barrier_semaphore()
    peers = [(flip(rep, b), g) for b in (1, 2, 4)]
    peers += [(rep, lax.rem(g + i, groups)) for i in range(1, groups)]
    return barrier, peers


def do_barrier(barrier, peers):
    for r, gg in peers:
        pl.semaphore_signal(barrier, inc=1, device_id={"rep": r, "grp": gg}, device_id_type=MESH)
    pl.semaphore_wait(barrier, len(peers))


def relayout(m, k, pbuf, fbuf, out):
    nrows = m.quarter * m.tiles
    extra = 8 if m.shifted else 0
    start = mo((m.row0 + k * nrows) * LANE, LANE)
    piece = pbuf[:, pl.ds(start, (nrows + extra) * LANE)]
    fbuf[0:nrows + extra, :] = piece.astype(F32).reshape(nrows + extra, LANE)
    low = lax.broadcasted_iota(jnp.int32, (m.quarter, LANE), 1) < 64
    for c in range(m.tiles):
        a = fbuf[pl.ds(c, m.quarter, stride=m.tiles), :]
        if m.shifted:
            b = fbuf[pl.ds(c + 1, m.quarter, stride=m.tiles), :]
            a = pltpu.roll(jnp.where(low, b, a), 64, 1)
        out[pl.ds(mo(k * m.quarter, 16), m.quarter), c * LANE:(c + 1) * LANE] = a.astype(BF)


def gather_kernel(groups, p_ref, fr_ref, wq, wo, wu, wd, fa, sm, pbuf, fbuf, sq, so, su, sd, smb,
                  lsem, osem, zs, zr, xs, xr, ys, yr, fas, far, fbs, fbr, cs, cr, ms, mr):
    rep, g = lax.axis_index("rep"), lax.axis_index("grp")
    s = lax.rem(rep, 8)
    h = lax.rem(s, 2)
    k = s // 2
    kx, ky, kd = flip(k, 1), flip(k, 2), 3 - k
    full = (wq, wo, wu, wd)
    blocks = (sq, so, su, sd)
    tokens = fr_ref.shape[0]
    barrier, peers = greet(rep, g, groups)
    bounds = [0]
    for m in MATS[1:]:
        bounds.append(m.offset // LANE * LANE)
    bounds.append(FLAT)
    loads = []
    for i in range(4):
        view = (slice(None), pl.ds(bounds[i], bounds[i + 1] - bounds[i]))
        cp = pltpu.make_async_copy(p_ref.at[view], pbuf.at[view], lsem.at[i])
        cp.start()
        loads.append(cp)
    do_barrier(barrier, peers)

    def zcopy(t, d, step, src, dst):
        target = lax.rem(g + (1 if d == 0 else groups - 1), groups)
        return remote(src, dst, zs.at[t, d, step], zr.at[t, d, step], rep, target)

    def has_next(d):
        return g < groups - 1 if d == 0 else g > 0

    def own_send(t):
        for d in range(2):
            @pl.when(has_next(d))
            def _():
                if t == 4:
                    zcopy(t, d, 0, fr_ref, fa.at[pl.ds(mo(g * tokens, 16), tokens), :]).start()
                else:
                    m = MATS[t]
                    src = blocks[t].at[pl.ds(mo(k * m.quarter, 16), m.quarter), pl.ds(mo(h * m.half, LANE), m.half)]
                    zcopy(t, d, 0, src, part(full[t], m, g, k, h)).start()

    def rest(t):
        def body(i, c):
            relayout(MATS[t], lax.rem(k + i, 4), pbuf, fbuf, blocks[t])
            return c
        lax.fori_loop(1, 4, body, 0)
        pltpu.make_async_copy(blocks[t], full[t].at[pl.ds(mo(g * MATS[t].block, 16), MATS[t].block), :], osem.at[t]).start()

    def row_of(d, step):
        return g - 1 - step if d == 0 else g + 1 + step

    def valid(d, step):
        return g - 1 - step >= 0 if d == 0 else g + 1 + step <= groups - 1

    slots = [(d, step) for step in range(groups - 1) for d in range(2)]

    def zregion(t, r):
        if t == 4:
            return fa.at[pl.ds(mo(r * tokens, 16), tokens), :]
        return part(full[t], MATS[t], r, k, h)

    def stage0(t, d, step):
        @pl.when(valid(d, step))
        def _():
            r = row_of(d, step)
            reg = zregion(t, r)
            zcopy(t, d, step, reg, reg).wait_recv()
            if step < groups - 2:
                @pl.when(has_next(d))
                def _():
                    zcopy(t, d, step + 1, reg, reg).start()
            if t < 4:
                i = d * (groups - 1) + step
                remote(reg, reg, xs.at[t, i], xr.at[t, i], flip(rep, 2), g).start()
                remote(reg, reg, ys.at[t, i], yr.at[t, i], flip(rep, 4), g).start()

    def stage1(t, d, step):
        @pl.when(valid(d, step))
        def _():
            r, i, m = row_of(d, step), d * (groups - 1) + step, MATS[t]
            reg = part(full[t], m, r, kx, h)
            remote(reg, reg, xs.at[t, i], xr.at[t, i], flip(rep, 2), g).wait_recv()
            a = part(full[t], m, r, kx, h, 0)
            remote(a, a, fas.at[t, i], far.at[t, i], flip(rep, 4), g).start()
            reg = part(full[t], m, r, ky, h)
            remote(reg, reg, ys.at[t, i], yr.at[t, i], flip(rep, 4), g).wait_recv()
            b = part(full[t], m, r, ky, h, 1)
            remote(b, b, fbs.at[t, i], fbr.at[t, i], flip(rep, 2), g).start()

    def stage2(t, d, step):
        @pl.when(valid(d, step))
        def _():
            r, i, m = row_of(d, step), d * (groups - 1) + step, MATS[t]
            a, b = part(full[t], m, r, kd, h, 0), part(full[t], m, r, kd, h, 1)
            remote(a, a, fas.at[t, i], far.at[t, i], flip(rep, 4), g).wait_recv()
            remote(b, b, fbs.at[t, i], fbr.at[t, i], flip(rep, 2), g).wait_recv()
            c = slab(full[t], m, r, h)
            remote(c, c, cs.at[t, i], cr.at[t, i], flip(rep, 1), g).start()

    def stage3(t, d, step):
        @pl.when(valid(d, step))
        def _():
            r, i, m = row_of(d, step), d * (groups - 1) + step, MATS[t]
            c = slab(full[t], m, r, 1 - h)
            remote(c, c, cs.at[t, i], cr.at[t, i], flip(rep, 1), g).wait_recv()

    loads[0].wait()
    relayout(QKV, k, pbuf, fbuf, sq)
    own_send(0)
    own_send(4)
    loads[1].wait()
    relayout(OUT, k, pbuf, fbuf, so)
    own_send(1)
    loads[2].wait()
    loads[3].wait()
    relayout(UP, k, pbuf, fbuf, su)
    own_send(2)
    relayout(DOWN, k, pbuf, fbuf, sd)
    own_send(3)
    row = 0
    for first, count in SMALL:
        smb[row:row + count, :] = pbuf[:, first * LANE:(first + count) * LANE].astype(F32).reshape(count, LANE)
        row += count
    smb[row:SROWS, :] = jnp.zeros((SROWS - row, LANE), F32)
    for i in range(1, groups):
        remote(smb, sm.at[g], ms.at[i - 1], mr.at[i - 1], rep, lax.rem(g + i, groups)).start()
    pltpu.make_async_copy(smb, sm.at[g], osem.at[4]).start()
    pltpu.make_async_copy(fr_ref, fa.at[pl.ds(mo(g * tokens, 16), tokens), :], osem.at[5]).start()

    items = [(t, d, step) for step in range(groups - 1) for t in (0, 4, 1, 2, 3) for d in range(2)]
    mats = [it for it in items if it[0] < 4]
    fillers = {1: 0, 3: 1, 5: 2, 7: 3}
    lag = 2
    n1 = n2 = n3 = 0
    count = 0
    for n, it in enumerate(items):
        stage0(*it)
        if it[0] < 4:
            count += 1
        if n in fillers:
            rest(fillers[n])
        while n1 < count - lag:
            stage1(*mats[n1])
            n1 += 1
        while n2 < n1 - lag:
            stage2(*mats[n2])
            n2 += 1
    while n1 < len(mats):
        stage1(*mats[n1])
        n1 += 1
        if n2 < n1 - lag:
            stage2(*mats[n2])
            n2 += 1
    while n2 < len(mats):
        stage2(*mats[n2])
        n2 += 1
    for it in mats:
        stage3(*it)
    for t in (0, 4, 1, 2, 3):
        reg = zregion(t, g)
        for d in range(2):
            @pl.when(has_next(d))
            def _():
                zcopy(t, d, 0, reg, reg).wait_send()
        for (d, step) in slots:
            i = d * (groups - 1) + step

            @pl.when(valid(d, step))
            def _():
                r = row_of(d, step)
                if step < groups - 2:
                    @pl.when(has_next(d))
                    def _():
                        zcopy(t, d, step + 1, reg, reg).wait_send()
                if t < 4:
                    m = MATS[t]
                    remote(reg, reg, xs.at[t, i], xr.at[t, i], flip(rep, 2), g).wait_send()
                    remote(reg, reg, ys.at[t, i], yr.at[t, i], flip(rep, 4), g).wait_send()
                    a, b = part(full[t], m, r, kx, h, 0), part(full[t], m, r, ky, h, 1)
                    remote(a, a, fas.at[t, i], far.at[t, i], flip(rep, 4), g).wait_send()
                    remote(b, b, fbs.at[t, i], fbr.at[t, i], flip(rep, 2), g).wait_send()
                    c = slab(full[t], m, r, h)
                    remote(c, c, cs.at[t, i], cr.at[t, i], flip(rep, 1), g).wait_send()
        if t < 4:
            pltpu.make_async_copy(blocks[t], full[t].at[pl.ds(mo(g * MATS[t].block, 16), MATS[t].block), :], osem.at[t]).wait()
    for i in range(1, groups):
        cp = remote(smb, sm.at[lax.rem(g + groups - i, groups)], ms.at[i - 1], mr.at[i - 1], rep, lax.rem(g + i, groups))
        cp.wait_send()
        cp.wait_recv()
    pltpu.make_async_copy(smb, sm.at[g], osem.at[4]).wait()
    pltpu.make_async_copy(fr_ref, fa.at[pl.ds(mo(g * tokens, 16), tokens), :], osem.at[5]).wait()


def gather(params, frames, groups):
    dma = pltpu.SemaphoreType.DMA
    n = 2 * (groups - 1)
    tokens = frames.shape[0]
    shapes = [jax.ShapeDtypeStruct((m.block * groups, m.cols), BF) for m in MATS]
    shapes += [jax.ShapeDtypeStruct((tokens * groups, D), BF), jax.ShapeDtypeStruct((groups, SROWS, LANE), F32)]
    return pl.pallas_call(
        functools.partial(gather_kernel, groups),
        out_shape=shapes,
        in_specs=[pl.BlockSpec(memory_space=pl.ANY), pl.BlockSpec(memory_space=pltpu.VMEM)],
        out_specs=[pl.BlockSpec(memory_space=pl.ANY)] * 6,
        scratch_shapes=[
            pltpu.VMEM((1, FLAT + 8 * LANE), BF),
            pltpu.VMEM((48 * 24 + 16, LANE), F32),
        ] + [pltpu.VMEM((m.block, m.cols), BF) for m in MATS] + [
            pltpu.VMEM((SROWS, LANE), F32),
            dma((4,)), dma((6,)), dma((5, 2, groups)), dma((5, 2, groups)),
            dma((4, n)), dma((4, n)), dma((4, n)), dma((4, n)), dma((4, n)), dma((4, n)), dma((4, n)), dma((4, n)),
            dma((4, n)), dma((4, n)), dma((groups,)), dma((groups,)),
        ],
        compiler_params=pltpu.CompilerParams(collective_id=0, has_side_effects=True, vmem_limit_bytes=40 << 20),
        name="gather",
    )(params, frames)


def add_rows(dst, a, b, rows, step=16):
    def body(i, c):
        at = pl.ds(mo(i * step, 16), step)
        dst[at, :] = (a[at, :].astype(F32) + b[at, :].astype(F32)).astype(dst.dtype)
        return c
    lax.fori_loop(0, rows // step, body, 0)


def cell(ref, m, r, kk, sub=None):
    r0, rn, c0, cn = m.sub[sub] if sub is not None else (0, m.quarter, 0, m.half)
    return ref.at[pl.ds(mo(r * m.block + kk * m.quarter + r0, 16), rn), pl.ds(c0, cn)]


ORDER = (2, 3, 0, 1)


def reduce_kernel(groups, highs, gq, go, gu, gd, sm_ref, oq, oo, ou, od, osm, *scratch):
    own, scratch = scratch[:4], scratch[4:]
    buf1, scratch = scratch[:4], scratch[4:]
    buf2, scratch = scratch[:4], scratch[4:]
    buf3, scratch = scratch[:4], scratch[4:]
    zbuf, scratch = scratch[:4], scratch[4:]
    fin, scratch = scratch[:4], scratch[4:]
    (smacc, smin, lsem, c1s, c1r, a1s, a1r, b1s, b1r, a2s, a2r, b2s, b2r, zs, zr, fxs, fxr, os, xs, xr, ys, yr,
     fas, far, fbs, fbr, cs, cr, sms, smr) = scratch
    rep, g = lax.axis_index("rep"), lax.axis_index("grp")
    s = lax.rem(rep, 8)
    h = lax.rem(s, 2)
    k = s // 2
    x, y = lax.rem(k, 2), k // 2
    kx, ky, kd = flip(k, 1), flip(k, 2), 3 - k
    core, xn, yn = flip(rep, 1), flip(rep, 2), flip(rep, 4)
    grads = (gq, go, gu, gd)
    outs = (oq, oo, ou, od)
    barrier, peers = greet(rep, g, groups)
    peers += [(flip(rep, 8 << b), g) for b in range(highs)]
    do_barrier(barrier, peers)

    def row(i):
        return lax.rem(g + 1 + i, groups)

    def load(t, i):
        m = MATS[t]
        at = pl.ds(mo(row(i) * m.block, 16), m.block)
        return pltpu.make_async_copy(grads[t].at[at, pl.ds(mo(h * m.half, LANE), m.half)], own[t].at[at, :], lsem.at[t, i])

    def first(t, i):
        m = MATS[t]
        at = pl.ds(mo(row(i) * m.block, 16), m.block)
        return remote(grads[t].at[at, pl.ds(mo((1 - h) * m.half, LANE), m.half)], buf1[t].at[at, :],
                      c1s.at[t, i], c1r.at[t, i], core, g)

    def acopy(t, i, j, kk):
        return remote(cell(buf1[t], MATS[t], row(i), kk, 0), cell(buf2[t], MATS[t], row(i), kk, 0),
                      a1s.at[t, i, j], a1r.at[t, i, j], xn, g)

    def bcopy(t, i, j, kk):
        return remote(cell(buf1[t], MATS[t], row(i), kk, 1), cell(buf2[t], MATS[t], row(i), kk, 1),
                      b1s.at[t, i, j], b1r.at[t, i, j], yn, g)

    def a2copy(t, i, kk):
        return remote(cell(buf2[t], MATS[t], row(i), kk, 0), cell(buf3[t], MATS[t], row(i), kk, 0),
                      a2s.at[t, i], a2r.at[t, i], yn, g)

    def b2copy(t, i, kk):
        return remote(cell(buf2[t], MATS[t], row(i), kk, 1), cell(buf3[t], MATS[t], row(i), kk, 1),
                      b2s.at[t, i], b2r.at[t, i], xn, g)

    def zcopy(t, i):
        return remote(cell(buf3[t], MATS[t], row(i), k), zbuf[t].at[i], zs.at[t, i], zr.at[t, i], rep, row(i))

    def r1(t, i):
        m = MATS[t]
        load(t, i).wait()
        first(t, i).wait_recv()
        at = pl.ds(mo(row(i) * m.block, 16), m.block)
        add_rows(buf1[t].at[at, :], own[t].at[at, :], buf1[t].at[at, :], m.block)
        for j in range(2):
            acopy(t, i, j, 2 * j + (1 - x)).start()
            bcopy(t, i, j, 2 * (1 - y) + j).start()

    def r2(t, i):
        m = MATS[t]
        for j in range(2):
            acopy(t, i, j, 2 * j + x).wait_recv()
            kk = 2 * j + x
            add_rows(cell(buf2[t], m, row(i), kk, 0), cell(buf1[t], m, row(i), kk, 0), cell(buf2[t], m, row(i), kk, 0), m.sub[0][1])
        a2copy(t, i, 2 * (1 - y) + x).start()
        for j in range(2):
            bcopy(t, i, j, 2 * y + j).wait_recv()
            kk = 2 * y + j
            add_rows(cell(buf2[t], m, row(i), kk, 1), cell(buf1[t], m, row(i), kk, 1), cell(buf2[t], m, row(i), kk, 1), m.sub[1][1])
        b2copy(t, i, 2 * y + (1 - x)).start()

    def r3(t, i):
        m = MATS[t]
        a2copy(t, i, k).wait_recv()
        b2copy(t, i, k).wait_recv()
        whole = (cell(buf3[t], m, row(i), k), cell(buf2[t], m, row(i), k))
        add_rows(whole[0], whole[1], whole[0], m.quarter)
        if i < groups - 1:
            zcopy(t, i).start()

    def fpart(t, kk, hh, sub=None):
        return part(outs[t], MATS[t], 0, kk, hh, sub)

    def fslab(t, hh):
        return slab(outs[t], MATS[t], 0, hh)

    def keep(t):
        return pltpu.make_async_copy(fin[t].at[highs], fpart(t, k, h), os.at[t])

    def xsend(t):
        return remote(fin[t].at[highs], fpart(t, k, h), xs.at[t], xr.at[t], xn, g)

    def ysend(t):
        return remote(fin[t].at[highs], fpart(t, k, h), ys.at[t], yr.at[t], yn, g)

    def xgot(t):
        return remote(fpart(t, kx, h), fpart(t, kx, h), xs.at[t], xr.at[t], xn, g)

    def ygot(t):
        return remote(fpart(t, ky, h), fpart(t, ky, h), ys.at[t], yr.at[t], yn, g)

    def fwd(t, sub, kk):
        reg = fpart(t, kk, h, sub)
        return remote(reg, reg, (fas, fbs)[sub].at[t], (far, fbr)[sub].at[t], (yn, xn)[sub], g)

    def cross(t, hh):
        return remote(fslab(t, hh), fslab(t, hh), cs.at[t], cr.at[t], core, g)

    def r4(t):
        m = MATS[t]
        for i in range(groups - 1):
            zcopy(t, i).wait_recv()
        mine = cell(buf3[t], m, g, k)

        def body(n, c):
            at = pl.ds(mo(n * 16, 16), 16)
            total = mine[at, :].astype(F32)
            for i in range(groups - 1):
                total = total + zbuf[t][i, at, :].astype(F32)
            fin[t][0, at, :] = total.astype(BF)
            return c
        lax.fori_loop(0, m.quarter // 16, body, 0)
        for b in range(highs):
            cp = remote(fin[t].at[b], fin[t].at[highs + 1 + b], fxs.at[t, b], fxr.at[t, b], flip(rep, 8 << b), g)
            cp.start()
            cp.wait()
            add_rows(fin[t].at[b + 1], fin[t].at[b], fin[t].at[highs + 1 + b], m.quarter)
        keep(t).start()
        xsend(t).start()
        ysend(t).start()

    def r5(t):
        xgot(t).wait_recv()
        fwd(t, 0, kx).start()
        ygot(t).wait_recv()
        fwd(t, 1, ky).start()

    def r6(t):
        fwd(t, 0, kd).wait_recv()
        fwd(t, 1, kd).wait_recv()
        keep(t).wait()
        cross(t, h).start()

    def r7(t):
        cross(t, 1 - h).wait_recv()

    partners = [(core, g), (xn, g), (yn, g)] + [(flip(rep, 8 << b), g) for b in range(highs)]
    bit = 1
    while bit < groups:
        partners.append((rep, flip(g, bit)))
        bit *= 2

    def smcopy(j):
        return remote(smacc.at[j], smin.at[j], sms.at[j], smr.at[j], *partners[j])

    def small(j):
        if j:
            smcopy(j - 1).wait_recv()
            smacc[j] = smacc[j - 1] + smin[j - 1]
        else:
            smacc[0] = sm_ref[...]
        if j < len(partners):
            smcopy(j).start()
        else:
            osm[...] = smacc[j, g]

    chunks = [(t, i) for t in ORDER for i in range(groups)]
    small(0)
    for t, i in chunks:
        first(t, i).start()
        load(t, i).start()
    done4 = {}
    total = len(chunks)
    smalls = 1
    for n in range(total + 16):
        if n < total:
            r1(*chunks[n])
        if 0 <= n - 2 < total:
            r2(*chunks[n - 2])
        if n % 2 and smalls <= len(partners):
            small(smalls)
            smalls += 1
        if 0 <= n - 4 < total:
            r3(*chunks[n - 4])
        for q, t in enumerate(ORDER):
            last = groups * q + groups - 1 + 4
            if n == last + 2:
                r4(t)
            if n == last + 4:
                r5(t)
            if n == last + 6:
                r6(t)
    for t in ORDER:
        r7(t)
    for t, i in chunks:
        first(t, i).wait_send()
        for j in range(2):
            acopy(t, i, j, 2 * j + x).wait_send()
            bcopy(t, i, j, 2 * y + j).wait_send()
        a2copy(t, i, k).wait_send()
        b2copy(t, i, k).wait_send()
        if i < groups - 1:
            zcopy(t, i).wait_send()
    for t in ORDER:
        xsend(t).wait_send()
        ysend(t).wait_send()
        fwd(t, 0, kx).wait_send()
        fwd(t, 1, ky).wait_send()
        cross(t, h).wait_send()
    for j in range(len(partners)):
        smcopy(j).wait_send()


def reduce_grads(grads, smalls, groups, reps):
    dma = pltpu.SemaphoreType.DMA
    highs = (reps // 8).bit_length() - 1
    steps = 3 + highs + groups.bit_length() - 1
    wide = [pltpu.VMEM((m.block * groups, m.half), BF) for m in MATS]
    scratch = wide * 4
    scratch += [pltpu.VMEM((groups, m.quarter, m.half), BF) for m in MATS]
    scratch += [pltpu.VMEM((2 * highs + 1, m.quarter, m.half), BF) for m in MATS]
    scratch += [pltpu.VMEM((steps + 1, groups, SROWS, LANE), F32), pltpu.VMEM((steps, groups, SROWS, LANE), F32)]
    scratch += [dma((4, groups))] * 3 + [dma((4, groups, 2))] * 4 + [dma((4, groups))] * 6
    scratch += [dma((4, max(highs, 1)))] * 2 + [dma((4,))] * 11 + [dma((steps,))] * 2
    return pl.pallas_call(
        functools.partial(reduce_kernel, groups, highs),
        out_shape=[jax.ShapeDtypeStruct((m.block, m.cols), BF) for m in MATS] + [jax.ShapeDtypeStruct((SROWS, LANE), F32)],
        in_specs=[pl.BlockSpec(memory_space=pl.ANY)] * 4 + [pl.BlockSpec(memory_space=pltpu.VMEM)],
        out_specs=[pl.BlockSpec(memory_space=pl.ANY)] * 4 + [pl.BlockSpec(memory_space=pltpu.VMEM)],
        scratch_shapes=scratch,
        compiler_params=pltpu.CompilerParams(collective_id=1, has_side_effects=True, vmem_limit_bytes=44 << 20),
        name="reduce",
    )(*grads, smalls)


BETA_ONE = 0.9
BETA_TWO = 0.98
ADAM_EPS = 1e-06
LEARN_RATE = 0.006
DECAY = 0.01
ADAM_STEP = 4
ROWS = 1736
STEPS = -(-FROWS // ROWS)


def flatten(m, block, flat, late):
    def body(i, carry):
        base = m.row0 + i * (48 * m.tiles)
        for c in range(m.tiles):
            tile = block[pl.ds(mo(i * 48, 16), 48), c * LANE:(c + 1) * LANE].astype(F32)
            if m.shifted:
                tile = pltpu.roll(tile, 64, 1)
                late[pl.ds(base + c + 1, 48, stride=m.tiles), :] = tile
            flat[pl.ds(base + c, 48, stride=m.tiles), :] = tile
        return carry
    lax.fori_loop(0, m.block // 48, body, 0)


def adam_kernel(scale, gq, go, gu, gd, sm, p_ref, m_ref, v_ref, o_g, o_p, o_m, o_v, flat, late):
    step = pl.program_id(0)

    @pl.when(step == 0)
    def _():
        flatten(QKV, gq, flat, late)
        flatten(OUT, go, flat, late)
        flatten(UP, gu, flat, late)
        flatten(DOWN, gd, flat, late)
        flat[0:3, :] = sm[0:3, :]
        flat[3459:3462, :] = sm[3:6, :]
        flat[4614:4618, :] = sm[6:10, :]
        flat[4618:4619, 0:64] = sm[10:11, 0:64]
        flat[9226:9227, 64:128] = sm[11:12, 64:128]
        flat[9227:9232, :] = sm[12:17, :]
        flat[9232:9233, 0:64] = sm[17:18, 0:64]
        flat[13840:13841, 64:128] = sm[18:19, 64:128]
        flat[13841:13842, :] = sm[19:20, :]
        late[9227:9232, :] = sm[12:17, :]
        late[9232:9233, 0:64] = sm[17:18, 0:64]
        late[13841:13842, :] = sm[19:20, :]

    at = pl.ds(mo(step * ROWS, 8), ROWS)
    number = step * ROWS + lax.broadcasted_iota(jnp.int32, (ROWS, LANE), 0)
    low = lax.broadcasted_iota(jnp.int32, (ROWS, LANE), 1) < 64
    grad = jnp.where(jnp.logical_and(number > UP.row0, low), late[at, :], flat[at, :]).reshape(1, ROWS * LANE) * scale
    first = BETA_ONE * m_ref[...] + (1.0 - BETA_ONE) * grad
    second = BETA_TWO * v_ref[...] + (1.0 - BETA_TWO) * grad * grad
    o_g[...] = grad
    o_m[...] = first
    o_v[...] = second
    first_hat = first * (1.0 / (1.0 - BETA_ONE**ADAM_STEP))
    second_hat = second * (1.0 / (1.0 - BETA_TWO**ADAM_STEP))
    current = p_ref[...].astype(F32)
    o_p[...] = current - LEARN_RATE * (first_hat / (jnp.sqrt(second_hat) + ADAM_EPS) + DECAY * current)


def adam(blocks, smalls, params, first, second, reps):
    spec = pl.BlockSpec((1, ROWS * LANE), lambda i: (0, i))
    vmem = pl.BlockSpec(memory_space=pltpu.VMEM)
    return pl.pallas_call(
        functools.partial(adam_kernel, 1.0 / reps),
        grid=(STEPS,),
        out_shape=[jax.ShapeDtypeStruct((1, FLAT), F32)] * 4,
        in_specs=[vmem] * 5 + [spec] * 3,
        out_specs=[spec] * 4,
        scratch_shapes=[pltpu.VMEM((STEPS * ROWS, LANE), F32)] * 2,
        compiler_params=pltpu.CompilerParams(vmem_limit_bytes=50 << 20),
        name="adam",
    )(*blocks, smalls, params, first, second)


EPS_NORM = 1e-05


def norm_forward(values):
    center = values - jnp.mean(values, axis=-1, keepdims=True)
    inverse = lax.rsqrt(jnp.mean(center * center, axis=-1, keepdims=True) + EPS_NORM)
    return (center * inverse, inverse)


def norm_backward(upstream, normalized, inverse, gain):
    scaled = upstream * gain
    return inverse * (
        scaled
        - jnp.mean(scaled, axis=-1, keepdims=True)
        - normalized * jnp.mean(scaled * normalized, axis=-1, keepdims=True)
    )


def gelu(values):
    return 0.5 * values * (1.0 + lax.erf(values * 0.7071067811865476))


def gelu_slope(values):
    return (
        0.5 * (1.0 + lax.erf(values * 0.7071067811865476))
        + values * jnp.exp(-0.5 * values * values) * 0.3989422804014327
    )


def to_pairs(matrix):
    heads = matrix.shape[1] // HDIM
    return matrix.reshape(matrix.shape[0], heads // 2, 2, HDIM).transpose(1, 0, 2, 3)


def from_pairs(stacked):
    return stacked.transpose(1, 0, 2, 3).reshape(stacked.shape[1], -1)


def attend(query, keys, values):
    scale = HDIM ** (-0.5)

    def attend_one_pair(items):
        query_pair, key_pair, value_pair = items
        scores = (
            jnp.einsum("qhd,khd->hqk", query_pair, key_pair, preferred_element_type=jnp.float32)
            * scale
        )
        highest = jnp.max(scores, axis=-1, keepdims=True)
        log_total = highest + jnp.log(jnp.sum(jnp.exp(scores - highest), axis=-1, keepdims=True))
        shares = jnp.exp(scores - log_total).astype(jnp.bfloat16)
        mixed = jnp.einsum("hqk,khd->qhd", shares, value_pair, preferred_element_type=jnp.float32)
        return (mixed, log_total[..., 0])

    mixed, log_total = lax.map(attend_one_pair, (to_pairs(query), to_pairs(keys), to_pairs(values)))
    return (from_pairs(mixed).astype(jnp.bfloat16), log_total)


def row_centre(upstream, attended):
    product = to_pairs(upstream).astype(jnp.float32) * to_pairs(attended).astype(jnp.float32)
    return jnp.sum(product, axis=-1).transpose(0, 2, 1)


def back_blocks(query, keys, values, upstream, log_total, centre):
    scale = HDIM ** (-0.5)

    def back_one_pair(items):
        query_pair, key_pair, value_pair, upstream_pair, log_pair, centre_pair = items
        scores = (
            jnp.einsum("qhd,khd->hqk", query_pair, key_pair, preferred_element_type=jnp.float32)
            * scale
        )
        shares = jnp.exp(scores - log_pair[..., None])
        share_grad = jnp.einsum(
            "qhd,khd->hqk", upstream_pair, value_pair, preferred_element_type=jnp.float32
        )
        score_grad = (shares * (share_grad - centre_pair[..., None]) * scale).astype(jnp.bfloat16)
        result = []
        result.append(
            jnp.einsum("hqk,khd->qhd", score_grad, key_pair, preferred_element_type=jnp.float32)
        )
        result.append(
            jnp.einsum("hqk,qhd->khd", score_grad, query_pair, preferred_element_type=jnp.float32)
        )
        result.append(
            jnp.einsum(
                "hqk,qhd->khd",
                shares.astype(jnp.bfloat16),
                upstream_pair,
                preferred_element_type=jnp.float32,
            )
        )
        return tuple(result)

    stacked = (
        to_pairs(query),
        to_pairs(keys),
        to_pairs(values),
        to_pairs(upstream),
        log_total,
        centre,
    )
    outputs = lax.map(back_one_pair, stacked)
    return tuple((from_pairs(item) for item in outputs))


def vectors(smalls, groups):
    rows = smalls.reshape(groups, SROWS * LANE)

    def pick(first, count):
        return rows[:, first:first + count].reshape(1, groups * count)
    qv = pick(384, 384)
    return (pick(0, 192), pick(192, 192), qv, pick(768, 192), pick(960, 192), pick(1152, 192), pick(1472, 768), pick(2368, 192))


def small_image(gain_one, shift_one, qv, out_bias, gain_two, shift_two, up_bias, down_bias, groups):
    def rows(item):
        return item.reshape(groups, -1)
    gap = jnp.zeros((groups, 64), F32)
    pieces = [rows(gain_one), rows(shift_one), rows(qv), rows(out_bias), rows(gain_two), rows(shift_two), gap,
              gap, rows(up_bias), gap, gap, rows(down_bias), jnp.zeros((groups, 512), F32)]
    return jnp.concatenate(pieces, axis=1).reshape(groups, SROWS, LANE)


def on_device(frames, cotangent, params, first_moment, second_moment):
    groups, reps = lax.axis_size("grp"), lax.axis_size("rep")
    qkv_weight, out_weight, up_weight, down_weight, clip, smalls = gather(params, frames, groups)
    gain_one, shift_one, qv_bias, out_bias, gain_two, shift_two, up_bias, down_bias = vectors(smalls, groups)
    width = frames.shape[1]
    tokens = frames.shape[0]
    wide = clip.astype(F32)
    normal_all, inverse_all = norm_forward(wide)
    normed_all = (normal_all * gain_one + shift_one).astype(BF)
    start = lax.axis_index("grp") * tokens
    inputs = frames.astype(F32)
    normal_one, inverse_one = norm_forward(inputs)
    normed_one = (normal_one * gain_one + shift_one).astype(BF)
    query = (jnp.dot(normed_one, qkv_weight[:, :width], preferred_element_type=F32) + qv_bias[:, :width]).astype(BF)
    kv_bias = jnp.concatenate([jnp.zeros((1, width), F32), qv_bias[:, width:]], axis=1)
    key_value = (jnp.dot(normed_all, qkv_weight[:, width:], preferred_element_type=F32) + kv_bias).astype(BF)
    keys = key_value[:, :width]
    values = key_value[:, width:]
    attended, log_total = attend(query, keys, values)
    middle = jnp.dot(attended, out_weight, preferred_element_type=F32) + out_bias + inputs
    normal_two, inverse_two = norm_forward(middle)
    normed_two = (normal_two * gain_two + shift_two).astype(BF)
    hidden_pre = jnp.dot(normed_two, up_weight, preferred_element_type=F32) + up_bias
    activated = gelu(hidden_pre).astype(BF)
    out_frames = (jnp.dot(activated, down_weight, preferred_element_type=F32) + down_bias + middle).astype(BF)
    upstream = cotangent.astype(F32)
    pre_grad = jnp.dot(cotangent, down_weight.T, preferred_element_type=F32) * gelu_slope(hidden_pre)
    pre_grad_half = pre_grad.astype(BF)
    normed_two_grad = jnp.dot(pre_grad_half, up_weight.T, preferred_element_type=F32)
    middle_grad = upstream + norm_backward(normed_two_grad, normal_two, inverse_two, gain_two)
    middle_half = middle_grad.astype(BF)
    attended_grad = jnp.dot(middle_half, out_weight.T, preferred_element_type=F32).astype(BF)
    centre = row_centre(attended_grad, attended)
    query_grad, key_grad, value_grad = back_blocks(query, keys, values, attended_grad, log_total, centre)
    owned = lax.psum_scatter(jnp.concatenate([key_grad, value_grad], axis=1), "grp", scatter_dimension=0, tiled=True)
    projected_grad = jnp.concatenate([query_grad, owned], axis=1).astype(BF)
    normed_one_grad = jnp.dot(projected_grad, qkv_weight.T, preferred_element_type=F32)
    frames_grad = (middle_grad + norm_backward(normed_one_grad, normal_one, inverse_one, gain_one)).astype(BF)
    grads = [jnp.dot(a.T, b, preferred_element_type=F32).astype(BF) for a, b in (
        (normed_one, projected_grad), (attended, middle_half), (normed_two, pre_grad_half), (activated, cotangent))]
    image = small_image(
        jnp.sum(normed_one_grad * normal_one, axis=0), jnp.sum(normed_one_grad, axis=0),
        jnp.concatenate([jnp.sum(query_grad, axis=0), jnp.sum(owned[:, width:], axis=0)]),
        jnp.sum(middle_grad, axis=0), jnp.sum(normed_two_grad * normal_two, axis=0), jnp.sum(normed_two_grad, axis=0),
        jnp.sum(pre_grad, axis=0), jnp.sum(upstream, axis=0), groups)
    *blocks, small = reduce_grads(grads, image, groups, reps)
    param_grad, new_params, new_first, new_second = adam(blocks, small, params, first_moment, second_moment, reps)
    return (out_frames, frames_grad, param_grad, new_params, new_first, new_second)


def solution(mesh):
    in_specs = (
        P(("rep", "grp"), None),
        P(("rep", "grp"), None),
        P("grp", None),
        P("grp", None),
        P("grp", None),
    )
    out_specs = (
        P(("rep", "grp"), None),
        P(("rep", "grp"), None),
        P("grp", None),
        P("grp", None),
        P("grp", None),
        P("grp", None),
    )
    return jax.shard_map(
        on_device, mesh=mesh, in_specs=in_specs, out_specs=out_specs, check_vma=False
    )
```

time: 2080 us -> 472 us (0.23)
  waiting for transfers between devices: 1600 us -> 88 us
  local copies, waits for them, and re-layouts: 261 us -> 40.4 us
  Pallas kernels: 0 us -> 188 us
  other arithmetic: 75.3 us -> 29.7 us
    unnamed x6 -> x1, waiting for transfers between devices: 934 us -> 0.02 us
    all_gather x2 -> x0, waiting for transfers between devices: 501 us -> none  [the longest x1 475 us: on_device(): gathered = lax.all_gather(params, 'grp', axis=0, tiled=True)]
    pallas_call x0 -> x3, Pallas kernels: none -> 188 us  [the longest x1 91.1 us: reduce_grads(): pl.pallas_call(functools.partial(reduce_kernel, groups, highs), out_shape...]
    unnamed x95 -> x68, local copies, waits for them, and re-layouts: 154 us -> 6.58 us
    psum x1 -> x0, waiting for transfers between devices: 108 us -> none  [on_device(): total = lax.psum(owned_sum, 'rep')]
    reshape x15 -> x7, local copies, waits for them, and re-layouts: 71.5 us -> 9.37 us  [rows(): return item.reshape(groups, -1)]
    sub x1 -> x0, other arithmetic: 52.7 us -> none  [adam_update(): current - LEARN_RATE * (first_hat / (jnp.sqrt(second_hat) + ADAM_EPS) + D...]
    reduce_scatter x1, waiting for transfers between devices: 61.2 us -> 88 us  [on_device(): lax.psum_scatter(jnp.concatenate([key_grad, value_grad], axis=1), 'grp',...]
  transfers between devices with their start and end apart: 5 -> 1, of which waited for: 5 -> 1; matrix products, arithmetic and copies ran while one was open for 4% -> 5% of each run, Pallas kernels for 0% -> 0%
where the time goes in v1:
time: 472 us; the launch traced here: 466 us
  Pallas kernels  188 us (40%)
  matrix products  105 us (22%)
  waiting for transfers between devices  88 us (19%)
  local copies, waits for them, and re-layouts  40.4 us (9%)
  other arithmetic  29.7 us (6%)
  between operations  14.4 us (3%)
    pallas_call x1, Pallas kernels, reduce_grads(): pl.pallas_call(functools.partial(reduce_kernel, groups, highs), out_shape...  91.1 us
    reduce_scatter x1, waiting for transfers between devices, on_device(): lax.psum_scatter(jnp.concatenate([key_grad, value_grad], axis=1), 'grp',...  88 us
    pallas_call x1, Pallas kernels, gather(): pl.pallas_call(functools.partial(gather_kernel, groups), out_shape=shapes...  72.1 us
    pallas_call x1, Pallas kernels, adam(): pl.pallas_call(functools.partial(adam_kernel, 1.0 / reps), grid=(STEPS,),...  24.6 us
    dot_general x6, matrix products, back_one_pair(): jnp.einsum('hqk,qhd->khd', score_grad, query_pair, preferred_element_type...  11.6 us
    dot_general x4, matrix products, on_device(): jnp.dot(a.T, b, preferred_element_type=F32).astype(BF)  11.5 us
    dot_general x6, matrix products, back_one_pair(): jnp.einsum('qhd,khd->hqk', upstream_pair, value_pair, preferred_element_t...  10.2 us
  transfers between devices with their start and end apart: 1, of which 1 were waited for; matrix products, arithmetic and copies ran while one was open for 5% of the time, Pallas kernels for 0%

profile of v1, /device:TPU:28, one launch (start us, length us, event | category | flops | bytes accessed | tf_op | source)
XLA Modules:
  0.0 466.0 jit_solution(16402757942180617982)
XLA Ops:
  7.3 1.7 convert_reduce_fusion.1
  10.0 72.1 %gather.1 = (bf16[768,2304]{1,0:T(8,128)(2,1)S(1)}, bf16[768,768]{1,0:T(8,128)(2,1)S(1)}, bf16[768,3072]{1,0:T(8,128)(2,1)S(1)}, bf16[3072,768]{1,0:T(8,128)(2,1...) custom-call(bf16[1,1771776]{1,0:T(2,128)(2,1)} %p_ref.3, bf16[256,768]{1,0:T(8,128)(2,1)S(1)} %copy-done), custom_call_target="tpu_custom_call" | custom-call | tf_op jit(solution)/shard_map/gather/pallas_call | solution.py:292
  82.2 2.1 copy-done.4
  94.5 1.3 add.166
  95.9 2.6 fusion.63
  98.5 1.9 copy.16
  100.4 4.8 %add_convert_fusion = bf16[1024,1536]{1,0:T(8,128)(2,1)S(1)} fusion(f32[1536]{0:T(1024)} %pad_reduce_fusion, bf16[768,2304]{1,0:T(8,128)(2,1)} %copy-done.5, bf16[1024,768]{1,0:T(8,128)(2,1)S(1)} %get-tuple-element.108, f32[768]{0:T(1024)S(1)} %add.154, f32[768]{0:T(1024)S(1)} %mul.165, f32[1024]{0:T(1024)} %add_rsqrt_fusion, f32[1024]{0:T(1024)} %copy-done.23), kind=kOutput, calls=%fused_computation.56 | convolution fusion | flops 2423783424 | bytes 7100416 | tf_op jit(solution)/shard_map/dot_general | solution.py:782
  105.1 1.9 fusion.91
  107.0 1.7 copy.17
  108.7 2.6 copy.15
  111.4 24.2 %while.28 = (s32[]{:T(128)}, bf16[6,256,2,64]{1,3,2,0:T(8,128)(2,1)S(1)}, f32[6,2,256]{2,1,0:T(2,128)}, bf16[6,1024,2,64]{1,3,2,0:T(8,128)(2,1)}, bf16[6,256,2,6...) while((s32[]{:T(128)}, bf16[6,256,2,64]{1,3,2,0:T(8,128)(2,1)S(1)}, ...), condition=%wide.region_7.8_spmd.clone, body=%wide.region_4.7_spmd.sunk.clone | while | flops 138411520 | bytes 7030865 | solution.py:697
  111.4 1.4 multiply_reduce_fusion.9
  113.8 1.5 fusion.147
  115.4 1.4 multiply_reduce_fusion.9
  117.9 1.5 fusion.147
  119.4 1.4 multiply_reduce_fusion.9
  121.9 1.5 fusion.147
  123.4 1.4 multiply_reduce_fusion.9
  125.9 1.5 fusion.147
  127.5 1.4 multiply_reduce_fusion.9
  130.0 1.5 fusion.147
  131.5 1.4 multiply_reduce_fusion.9
  134.0 1.5 fusion.147
  137.1 5.4 %multiply_convert_fusion.1 = (bf16[256,3072]{1,0:T(8,128)(2,1)}, f32[256,3072]{1,0:T(8,128)S(1)}) fusion(f32[3072]{0:T(1024)S(1)} %copy-done.26, bf16[768,3072]{1,0:T(8,128)(2,1)} %copy-done.4, f32[256,768]{1,0:T(8,128)S(1)} %get-tuple-element.188, f32[768]{0:T(1024)S(1)} %add.171, f32[768]{0:T(1024)S(1)} %mul.176, f32[256]{0:T(256)S(1)} %add_rsqrt_fusion.1, ...), kind=kOutput, calls=%fused_computation.76 | convolution fusion | flops 1213661184 | bytes 10244096 | tf_op jit(solution)/shard_map/dot_general | solution.py:789
  142.6 6.5 %fusion.94 = (f32[3072]{0:T(1024)}, bf16[256,3072]{1,0:T(8,128)(2,1)S(1)}) fusion(f32[256,3072]{1,0:T(8,128)S(1)} %get-tuple-element.190, bf16[3072,768]{1,0:T(8,128)(2,1)} %get-tuple-element.114, bf16[256,768]{1,0:T(8,128)(2,1)S(1)} %copy-done.11), kind=kOutput, calls=%fused_computation.152 | convolution fusion | flops 1216607232 | bytes 9842688 | tf_op jit(solution)/shard_map/dot_general | solution.py:793
  149.1 2.1 multiply_reduce_fusion.1
  151.2 1.8 fusion.90
  153.1 2.4 convolution_convert_fusion.4
  156.8 48.5 %while.29 = (s32[]{:T(128)}, f32[6,256,2,64]{1,3,2,0:T(8,128)}, f32[6,1024,2,64]{1,3,2,0:T(8,128)}, f32[6,1024,2,64]{1,3,2,0:T(8,128)}, bf16[6,1024,2,64]{1,3,2,...) while((s32[]{:T(128)}, f32[6,256,2,64]{1,3,2,0:T(8,128)}, ...), condition=%wide.region_14.15_spmd.clone, body=%wide.region_13.14_spmd.sunk.clone | while | flops 340262912 | bytes 11684977 | solution.py:745
  158.7 1.7 multiply_convert_fusion.4
  161.6 1.4 fusion.162
  162.9 1.9 fusion.161
  166.8 1.7 multiply_convert_fusion.4
  169.6 1.4 fusion.162
  171.0 1.9 fusion.161
  174.9 1.7 multiply_convert_fusion.4
  177.7 1.4 fusion.162
  179.1 1.9 fusion.161
  183.0 1.7 multiply_convert_fusion.4
  185.8 1.4 fusion.162
  187.2 1.9 fusion.161
  191.1 1.7 multiply_convert_fusion.4
  193.9 1.4 fusion.162
  195.3 1.9 fusion.161
  199.1 1.7 multiply_convert_fusion.4
  202.0 1.4 fusion.162
  203.3 1.9 fusion.161
  205.3 6.7 %pad_maximum_fusion = f32[1024,1536]{0,1:T(8,128)} fusion(f32[1024,768]{0,1:T(8,128)} %bitcast.185, f32[1024,768]{0,1:T(8,128)} %bitcast.186), kind=kLoop, calls=%fused_computation.55 | loop fusion | flops 1572864 | bytes 12582912 | tf_op jit(solution)/shard_map/concatenate | solution.py:801
  212.0 1.5 add.178
  214.8 1.3 reshape.184
  217.5 1.3 reshape.183
  218.8 1.3 reshape.187
  220.9 1.4 concatenate.24
  223.1 2.8 convolution_convert_fusion.3.go
  225.9 3.6 convolution_convert_fusion.gd
  229.6 3.8 convolution_convert_fusion.1.gu
  233.4 2.1 fusion.62
  235.5 88.0 %reduce-scatter.2.cloned.1.call-done = f32[256,1536]{0,1:T(8,128)} async-done(((f32[1024,1536]{0,1:T(8,128)}), f32[256,1536]{0,1:T(8,128)}) %reduce-scatter.2.cloned.1.call-update) | async-done | bytes 1572880 | tf_op jit(solution)/shard_map/reduce_scatter | solution.py:801
  323.5 1.5 convert.8
  325.0 4.8 %fusion.78 = (f32[768]{0:T(1024)}, f32[256]{0:T(256)}, f32[256]{0:T(256)}, f32[768]{0:T(1024)}, f32[256,768]{1,0:T(8,128)}) fusion(bf16[256,768]{1,0:T(8,128)(2,1)S(1)} %copy-done.1, f32[256]{0:T(256)S(1)} %copy-done.22, f32[256]{0:T(256)S(1)} %copy-done.18, f32[768]{0:T(1024)S(1)} %mul.165, bf16[768,2304]{1,0:T(8,128)(2,1)} %copy-done.5, ...), kind=kOutput, calls=%fused_computation.111 | convolution fusion | flops 910292992 | bytes 5911552 | tf_op jit(solution)/shard_map/dot_general | solution.py:803
  338.5 1.5 concatenate.27
  340.9 2.6 fusion.77
  343.4 91.1 %reduce.6 = (bf16[192,2304]{1,0:T(8,128)(2,1)S(1)}, bf16[192,768]{1,0:T(8,128)(2,1)S(1)}, bf16[192,3072]{1,0:T(8,128)(2,1)S(1)}, bf16[768,768]{1,0:T(8,128)(2,1)S(1)}, f32[24,128]{1,0:T(8,128)S(1)}) custom-call(bf16[768,2304]{1,0:T(8,128)(2,1)S(1)} %convolution_convert_fusion.2.gq, bf16[768,768]{1,0:T(8,128)(2,1)S(1)} %copy-done.3, ...), custom_call_target="tpu_custom_call" | custom-call | tf_op jit(solution)/shard_map/reduce/pallas_call | solution.py:558
  434.5 24.6 %adam.1 = (f32[1,1771776]{1,0:T(1,128)}, f32[1,1771776]{1,0:T(1,128)}, f32[1,1771776]{1,0:T(1,128)}, f32[1,1771776]{1,0:T(1,128)}) custom-call(bf16[192,2304]{1,0:T(8,128)(2,1)S(1)} %get-tuple-element.119.gq, bf16[192,768]{1,0:T(8,128)(2,1)S(1)} %get-tuple-element.120.go, bf16[192,3072]{1,0:T(8,128)(2,1)S(1)} %get-tuple-element.121.gu, ...), custom_call_target="tpu_custom_call" | custom-call | tf_op jit(solution)/shard_map/adam/pallas_call | solution.py:632
  (143 shorter events, 53.0 us)
Async XLA Ops:
  7.2 316.3 %reduce-scatter.2.cloned.1.call-start = ((), (), s32[]{:S(2)}) async-start(), calls=%async_computation.1 | async-start | bytes 7864320 | tf_op jit(solution)/shard_map/reduce_scatter | solution.py:801
  9.0 1.0 copy-start
  10.0 78.1 %copy-start.1 = (bf16[256,768]{1,0:T(8,128)(2,1)S(1)}, bf16[256,768]{1,0:T(8,128)(2,1)}, u32[]{:S(2)}) copy-start(bf16[256,768]{1,0:T(8,128)(2,1)} %fr_ref.1) | copy-start | bytes 1179652
  82.1 2.2 copy-start.4
  82.1 3.3 copy-start.5
  86.8 3.5 copy-start.21
  87.5 0.5 copy-start.17
  89.1 1.8 copy-start.23
  135.5 1.6 copy-start.26
  136.8 14.4 %copy-start.6 = (f32[256,768]{1,0:T(8,128)}, f32[256,768]{1,0:T(8,128)S(1)}, u32[]{:S(2)}) copy-start(f32[256,768]{1,0:T(8,128)S(1)} %get-tuple-element.188) | copy-start | bytes 2359300
  136.8 14.4 %copy-start.19 = (f32[256]{0:T(256)}, f32[256]{0:T(256)S(1)}, u32[]{:S(2)}) copy-start(f32[256]{0:T(256)S(1)} %broadcast_multiply_fusion.5) | copy-start | bytes 3076
  137.1 14.2 %copy-start.24 = (f32[256]{0:T(256)}, f32[256]{0:T(256)S(1)}, u32[]{:S(2)}) copy-start(f32[256]{0:T(256)S(1)} %add_rsqrt_fusion.1) | copy-start | bytes 3076
  137.1 5.5 %copy-start.11 = (bf16[256,768]{1,0:T(8,128)(2,1)S(1)}, bf16[256,768]{1,0:T(8,128)(2,1)}, u32[]{:S(2)}) copy-start(bf16[256,768]{1,0:T(8,128)(2,1)} %param.10) | copy-start | bytes 1179652
  137.1 11.9 %slice-start = ((s8[4718592]{0:T(1024)(128)(4,1)}), s8[4194304]{0:T(1024)(128)(4,1)S(1)}, s32[]{:S(2)}) async-start(s8[4718592]{0:T(1024)(128)(4,1)} %bitcast.176), calls=%async_computation.2 | async-start | bytes 8388608
  142.6 6.5 %slice-start.1 = ((s8[4718592]{0:T(1024)(128)(4,1)}), s8[524288]{0:T(1024)(128)(4,1)S(1)}, s32[]{:S(2)}) async-start(s8[4718592]{0:T(1024)(128)(4,1)} %bitcast.176), calls=%async_computation.3 | async-start | bytes 1048576
  149.1 2.2 copy-start.15
  211.9 8.2 %copy-start.10 = (f32[6,256,2,64]{1,3,2,0:T(8,128)S(1)}, f32[6,256,2,64]{1,3,2,0:T(8,128)}, u32[]{:S(2)}) copy-start(f32[6,256,2,64]{1,3,2,0:T(8,128)} %get-tuple-element.116) | copy-start | bytes 2359300
  212.0 13.9 %copy-start.9 = (bf16[256,3072]{1,0:T(8,128)(2,1)S(1)}, bf16[256,3072]{1,0:T(8,128)(2,1)}, u32[]{:S(2)}) copy-start(bf16[256,3072]{1,0:T(8,128)(2,1)} %get-tuple-element.189) | copy-start | bytes 4718596
  212.0 13.9 %copy-start.12 = (bf16[256,768]{1,0:T(8,128)(2,1)S(1)}, bf16[256,768]{1,0:T(8,128)(2,1)}, u32[]{:S(2)}) copy-start(bf16[256,768]{1,0:T(8,128)(2,1)} %param.10) | copy-start | bytes 1179652
  223.1 10.2 %slice-start.2 = ((s8[4718592]{0:T(1024)(128)(4,1)}), s8[4194304]{0:T(1024)(128)(4,1)S(1)}, s32[]{:S(2)}) async-start(s8[4718592]{0:T(1024)(128)(4,1)} %bitcast.195), calls=%async_computation.4 | async-start | bytes 8388608
  225.9 3.7 copy-start.7
  225.9 3.7 copy-start.16
  225.9 3.7 copy-start.20
  225.9 3.7 copy-start.25
  225.9 7.4 %slice-start.3 = ((s8[4718592]{0:T(1024)(128)(4,1)}), s8[524288]{0:T(1024)(128)(4,1)S(1)}, s32[]{:S(2)}) async-start(s8[4718592]{0:T(1024)(128)(4,1)} %bitcast.195), calls=%async_computation.5 | async-start | bytes 1048576
  229.6 3.8 copy-start.27
  233.3 91.6 %copy-start.13 = (bf16[256,6,2,64]{0,3,2,1:T(8,128)(2,1)S(1)}, bf16[256,6,2,64]{0,3,2,1:T(8,128)(2,1)}, u32[]{:S(2)}) copy-start(bf16[256,6,2,64]{0,3,2,1:T(8,128)(2,1)} %bitcast_convert_fusion) | copy-start | bytes 1179652
  233.3 91.6 %copy-start.18 = (f32[256]{0:T(256)S(1)}, f32[256]{0:T(256)}, u32[]{:S(2)}) copy-start(f32[256]{0:T(256)} %copy-done.17) | copy-start | bytes 3076
  233.4 91.6 %copy-start.22 = (f32[256]{0:T(256)S(1)}, f32[256]{0:T(256)}, u32[]{:S(2)}) copy-start(f32[256]{0:T(256)} %add_rsqrt_fusion.2) | copy-start | bytes 3076
  325.0 4.8 %copy-start.2 = (bf16[256,768]{1,0:T(8,128)(2,1)S(1)}, bf16[256,768]{1,0:T(8,128)(2,1)}, u32[]{:S(2)}) copy-start(bf16[256,768]{1,0:T(8,128)(2,1)} %fr_ref.1) | copy-start | bytes 1179652
  325.0 4.8 %copy-start.14 = (bf16[256,6,2,64]{0,3,2,1:T(8,128)(2,1)S(1)}, bf16[256,6,2,64]{0,3,2,1:T(8,128)(2,1)}, u32[]{:S(2)}) copy-start(bf16[256,6,2,64]{0,3,2,1:T(8,128)(2,1)} %bitcast_convert_fusion) | copy-start | bytes 1179652
  329.8 1.4 copy-start.8
  340.0 3.5 copy-start.3
Sparse Core Ops, SparseCore 0:
  212.1 111.3 reduce-scatter.1

commit v2 on v1

--- a/solution.py
+++ b/solution.py
@@ -642,174 +642,418 @@
 
 
 EPS_NORM = 1e-05
-
-
-def norm_forward(values):
-    center = values - jnp.mean(values, axis=-1, keepdims=True)
-    inverse = lax.rsqrt(jnp.mean(center * center, axis=-1, keepdims=True) + EPS_NORM)
-    return (center * inverse, inverse)
-
-
-def norm_backward(upstream, normalized, inverse, gain):
-    scaled = upstream * gain
-    return inverse * (
-        scaled
-        - jnp.mean(scaled, axis=-1, keepdims=True)
-        - normalized * jnp.mean(scaled * normalized, axis=-1, keepdims=True)
-    )
-
-
-def gelu(values):
-    return 0.5 * values * (1.0 + lax.erf(values * 0.7071067811865476))
-
-
-def gelu_slope(values):
-    return (
-        0.5 * (1.0 + lax.erf(values * 0.7071067811865476))
-        + values * jnp.exp(-0.5 * values * values) * 0.3989422804014327
-    )
-
-
-def to_pairs(matrix):
-    heads = matrix.shape[1] // HDIM
-    return matrix.reshape(matrix.shape[0], heads // 2, 2, HDIM).transpose(1, 0, 2, 3)
-
-
-def from_pairs(stacked):
-    return stacked.transpose(1, 0, 2, 3).reshape(stacked.shape[1], -1)
-
-
-def attend(query, keys, values):
-    scale = HDIM ** (-0.5)
-
-    def attend_one_pair(items):
-        query_pair, key_pair, value_pair = items
-        scores = (
-            jnp.einsum("qhd,khd->hqk", query_pair, key_pair, preferred_element_type=jnp.float32)
-            * scale
-        )
+ROOT_HALF = 0.7071067811865476
+ROOT_TWO_PI = 0.3989422804014327
+HEADS = D // HDIM
+GAIN_ONE, SHIFT_ONE, QV_BIAS, OUT_BIAS, GAIN_TWO, SHIFT_TWO, UP_BIAS, DOWN_BIAS = (
+    (0, 3), (3, 3), (6, 6), (12, 3), (15, 3), (18, 3), (23, 12), (37, 3))
+
+
+def low_lanes():
+    return lax.broadcasted_iota(jnp.int32, (1, LANE), 1) < 64
+
+
+def assemble(sm, place, out):
+    first, count = place
+    halves = [(gi, first + i) for gi in range(sm.shape[0]) for i in range(count)]
+    for t in range(len(halves) // 2):
+        (g0, h0), (g1, h1) = halves[2 * t], halves[2 * t + 1]
+        a = sm[g0, h0 // 2:h0 // 2 + 1, :]
+        b = sm[g1, h1 // 2:h1 // 2 + 1, :]
+        a = pltpu.roll(a, 64, 1) if h0 % 2 else a
+        b = b if h1 % 2 else pltpu.roll(b, 64, 1)
+        out[0:1, t * LANE:(t + 1) * LANE] = jnp.where(low_lanes(), a, b)
+
+
+def fill_image(image, rows, vectors):
+    where = {}
+    for place, ref in vectors:
+        for i in range(place[1]):
+            where[place[0] + i] = (place[1], i, ref)
+    for gi in range(image.shape[0]):
+        for r in rows:
+            parts = []
+            for side in range(2):
+                spot = where.get(2 * r + side)
+                if spot is None:
+                    parts.append(jnp.zeros((1, LANE), F32))
+                    continue
+                count, i, ref = spot
+                q = gi * count + i
+                v = ref[0:1, q // 2 * LANE:(q // 2 + 1) * LANE]
+                parts.append(v if q % 2 == side else pltpu.roll(v, 64, 1))
+            image[gi, r:r + 1, :] = jnp.where(low_lanes(), parts[0], parts[1])
+
+
+def mean(v):
+    return jnp.sum(v, axis=-1, keepdims=True) * (1.0 / D)
+
+
+def normalize(v):
+    centered = v - mean(v)
+    inverse = lax.rsqrt(mean(centered * centered) + EPS_NORM)
+    return centered * inverse, inverse
+
+
+def norm_back(upstream, normal, inverse, gain):
+    s = upstream * gain
+    return inverse * (s - mean(s) - normal * mean(s * normal))
+
+
+def nn(a, b):
+    return lax.dot_general(a, b, (((1,), (0,)), ((), ())), preferred_element_type=F32)
+
+
+def nt(a, b):
+    return lax.dot_general(a, b, (((1,), (1,)), ((), ())), preferred_element_type=F32)
+
+
+def loop(count, body):
+    def step(i, c):
+        body(i)
+        return c
+    lax.fori_loop(0, count, step, 0)
+
+
+def head_mask(rows):
+    return lax.broadcasted_iota(jnp.int32, (rows, LANE), 1) < HDIM
+
+
+def project_block(j, fa, gain, shift, bias, wq, q_all, k_all, v_all, normed, tokens):
+    at = pl.ds(mo(j * tokens, 16), tokens)
+    normal, _ = normalize(fa[at, :].astype(F32))
+    normed[...] = (normal * gain[...] + shift[...]).astype(BF)
+    for third, out in enumerate((q_all, k_all, v_all)):
+        def body(n):
+            col = pl.ds(mo(n * 256, 256), 256)
+            wide = nn(normed[...], wq[:, pl.ds(mo(third * D + n * 256, 256), 256)])
+            if third != 1:
+                wide = wide + bias[0:1, pl.ds(mo((third // 2) * D + n * 256, 256), 256)]
+            out[at, col] = wide.astype(BF)
+        loop(D // 256, body)
+
+
+def attend_pair(p, g, q_all, k_all, v_all, attended, stats, tokens):
+    col = pl.ds(mo(p * LANE, LANE), LANE)
+    query = q_all[pl.ds(mo(g * tokens, 16), tokens), col] * jnp.asarray(HDIM**-0.5, BF)
+    keys, values = k_all[:, col], v_all[:, col]
+    mask = head_mask(tokens)
+    zero = jnp.zeros_like(query)
+    lanes = lax.broadcasted_iota(jnp.int32, (tokens, LANE), 1)
+    results = []
+    for side in range(2):
+        scores = nt(jnp.where(mask, query, zero) if side == 0 else jnp.where(mask, zero, query), keys)
         highest = jnp.max(scores, axis=-1, keepdims=True)
-        log_total = highest + jnp.log(jnp.sum(jnp.exp(scores - highest), axis=-1, keepdims=True))
-        shares = jnp.exp(scores - log_total).astype(jnp.bfloat16)
-        mixed = jnp.einsum("hqk,khd->qhd", shares, value_pair, preferred_element_type=jnp.float32)
-        return (mixed, log_total[..., 0])
-
-    mixed, log_total = lax.map(attend_one_pair, (to_pairs(query), to_pairs(keys), to_pairs(values)))
-    return (from_pairs(mixed).astype(jnp.bfloat16), log_total)
-
-
-def row_centre(upstream, attended):
-    product = to_pairs(upstream).astype(jnp.float32) * to_pairs(attended).astype(jnp.float32)
-    return jnp.sum(product, axis=-1).transpose(0, 2, 1)
-
-
-def back_blocks(query, keys, values, upstream, log_total, centre):
-    scale = HDIM ** (-0.5)
-
-    def back_one_pair(items):
-        query_pair, key_pair, value_pair, upstream_pair, log_pair, centre_pair = items
-        scores = (
-            jnp.einsum("qhd,khd->hqk", query_pair, key_pair, preferred_element_type=jnp.float32)
-            * scale
-        )
-        shares = jnp.exp(scores - log_pair[..., None])
-        share_grad = jnp.einsum(
-            "qhd,khd->hqk", upstream_pair, value_pair, preferred_element_type=jnp.float32
-        )
-        score_grad = (shares * (share_grad - centre_pair[..., None]) * scale).astype(jnp.bfloat16)
-        result = []
-        result.append(
-            jnp.einsum("hqk,khd->qhd", score_grad, key_pair, preferred_element_type=jnp.float32)
-        )
-        result.append(
-            jnp.einsum("hqk,qhd->khd", score_grad, query_pair, preferred_element_type=jnp.float32)
-        )
-        result.append(
-            jnp.einsum(
-                "hqk,qhd->khd",
-                shares.astype(jnp.bfloat16),
-                upstream_pair,
-                preferred_element_type=jnp.float32,
-            )
-        )
-        return tuple(result)
-
-    stacked = (
-        to_pairs(query),
-        to_pairs(keys),
-        to_pairs(values),
-        to_pairs(upstream),
-        log_total,
-        centre,
-    )
-    outputs = lax.map(back_one_pair, stacked)
-    return tuple((from_pairs(item) for item in outputs))
-
-
-def vectors(smalls, groups):
-    rows = smalls.reshape(groups, SROWS * LANE)
-
-    def pick(first, count):
-        return rows[:, first:first + count].reshape(1, groups * count)
-    qv = pick(384, 384)
-    return (pick(0, 192), pick(192, 192), qv, pick(768, 192), pick(960, 192), pick(1152, 192), pick(1472, 768), pick(2368, 192))
-
-
-def small_image(gain_one, shift_one, qv, out_bias, gain_two, shift_two, up_bias, down_bias, groups):
-    def rows(item):
-        return item.reshape(groups, -1)
-    gap = jnp.zeros((groups, 64), F32)
-    pieces = [rows(gain_one), rows(shift_one), rows(qv), rows(out_bias), rows(gain_two), rows(shift_two), gap,
-              gap, rows(up_bias), gap, gap, rows(down_bias), jnp.zeros((groups, 512), F32)]
-    return jnp.concatenate(pieces, axis=1).reshape(groups, SROWS, LANE)
+        shares = jnp.exp(scores - highest)
+        total = jnp.sum(shares, axis=-1, keepdims=True)
+        results.append(nn(shares.astype(BF), values) * (1.0 / total))
+        stats[...] = jnp.where(lanes == 2 * p + side, highest + jnp.log(total), stats[...])
+    attended[:, col] = jnp.where(mask, results[0], results[1]).astype(BF)
+
+
+def fwd_kernel(fa, wq, sm, q_all, k_all, v_all, attended, stats, normed, gain, shift, bias):
+    g = lax.axis_index("grp")
+    tokens = attended.shape[0]
+    assemble(sm, GAIN_ONE, gain)
+    assemble(sm, SHIFT_ONE, shift)
+    assemble(sm, QV_BIAS, bias)
+    loop(fa.shape[0] // tokens, lambda j: project_block(j, fa, gain, shift, bias, wq, q_all, k_all, v_all, normed, tokens))
+    stats[...] = jnp.zeros_like(stats)
+    loop(HEADS // 2, lambda p: attend_pair(p, g, q_all, k_all, v_all, attended, stats, tokens))
+
+
+def forward(clip, wq, smalls, tokens):
+    vmem = pl.BlockSpec(memory_space=pltpu.VMEM)
+    wide = jax.ShapeDtypeStruct(clip.shape, BF)
+    return pl.pallas_call(
+        fwd_kernel,
+        out_shape=[wide] * 3 + [jax.ShapeDtypeStruct((tokens, D), BF), jax.ShapeDtypeStruct((tokens, LANE), F32)],
+        in_specs=[vmem] * 3, out_specs=[vmem] * 5,
+        scratch_shapes=[pltpu.VMEM((tokens, D), BF), pltpu.VMEM((1, D), F32), pltpu.VMEM((1, D), F32), pltpu.VMEM((1, 2 * D), F32)],
+        compiler_params=pltpu.CompilerParams(vmem_limit_bytes=40 << 20),
+        name="forward",
+    )(clip, wq, smalls)
+
+
+def mid_kernel(attended, fr, ct, wo_h, wu_h, wd_h, sm, lse, out_frames, agrad, mgrad, stats, rows, go, gu, gd, image,
+               wo, wu, wd, middle, normal, normed, act, pre, half, turned, wide, gain, shift, obias, ubias, dbias,
+               v_gain, v_shift, v_out, v_up, v_down, sem):
+    tokens = attended.shape[0]
+    loads = [pltpu.make_async_copy(a, b, sem.at[i]) for i, (a, b) in enumerate(((wo_h, wo), (wu_h, wu), (wd_h, wd)))]
+    for cp in loads:
+        cp.start()
+    assemble(sm, GAIN_TWO, gain)
+    assemble(sm, SHIFT_TWO, shift)
+    assemble(sm, OUT_BIAS, obias)
+    assemble(sm, UP_BIAS, ubias)
+    assemble(sm, DOWN_BIAS, dbias)
+    loads[0].wait()
+
+    def out_block(n):
+        col = pl.ds(mo(n * 256, 256), 256)
+        middle[:, col] = nn(attended[...], wo[:, col]) + obias[0:1, col] + fr[:, col].astype(F32)
+    loop(D // 256, out_block)
+    value, inverse = normalize(middle[...])
+    normal[...] = value
+    normed[...] = (value * gain[...] + shift[...]).astype(BF)
+    loads[1].wait()
+    loads[2].wait()
+
+    def hidden_block(n):
+        col = pl.ds(mo(n * 256, 256), 256)
+        hidden = nn(normed[...], wu[:, col]) + ubias[0:1, col]
+        bell = 0.5 * (1.0 + lax.erf(hidden * ROOT_HALF))
+        act[:, col] = (hidden * bell).astype(BF)
+        slope = bell + hidden * jnp.exp(-0.5 * hidden * hidden) * ROOT_TWO_PI
+        grad = nt(ct[...], wd[pl.ds(mo(n * 256, 256), 256), :]) * slope
+        v_up[0:1, col] = jnp.sum(grad, axis=0, keepdims=True)
+        pre[:, col] = grad.astype(BF)
+    loop(FF // 256, hidden_block)
+
+    def down_block(n):
+        col = pl.ds(mo(n * 256, 256), 256)
+        out_frames[:, col] = (nn(act[...], wd[:, col]) + dbias[0:1, col] + middle[:, col]).astype(BF)
+    loop(D // 256, down_block)
+
+    def back_block(n):
+        col = pl.ds(mo(n * 256, 256), 256)
+        wide[:, col] = nt(pre[...], wu[pl.ds(mo(n * 256, 256), 256), :])
+    loop(D // 256, back_block)
+    upstream = wide[...]
+    v_gain[...] = jnp.sum(upstream * normal[...], axis=0, keepdims=True)
+    v_shift[...] = jnp.sum(upstream, axis=0, keepdims=True)
+    total = ct[...].astype(F32) + norm_back(upstream, normal[...], inverse, gain[...])
+    mgrad[...] = total
+    half[...] = total.astype(BF)
+    v_out[...] = jnp.sum(total, axis=0, keepdims=True)
+    v_down[...] = jnp.sum(ct[...].astype(F32), axis=0, keepdims=True)
+
+    def attended_block(n):
+        col = pl.ds(mo(n * 256, 256), 256)
+        agrad[:, col] = nt(half[...], wo[pl.ds(mo(n * 256, 256), 256), :]).astype(BF)
+    loop(D // 256, attended_block)
+    lanes = lax.broadcasted_iota(jnp.int32, (tokens, LANE), 1)
+    mask = head_mask(tokens)
+    both = lse[...]
+    for p in range(HEADS // 2):
+        product = agrad[:, p * LANE:(p + 1) * LANE].astype(F32) * attended[:, p * LANE:(p + 1) * LANE].astype(F32)
+        for side in range(2):
+            mine = jnp.where(mask if side == 0 else jnp.logical_not(mask), product, 0.0)
+            both = jnp.where(lanes == HEADS + 2 * p + side, jnp.sum(mine, axis=-1, keepdims=True), both)
+    stats[...] = both
+    rows[...] = both.T[0:2 * HEADS, :]
+
+    def weight(left, right, out):
+        count = left.shape[1]
+        turned[0:count, :] = left[...].T
+
+        def block(i):
+            def inner(n):
+                r, c = pl.ds(mo(i * 256, 256), 256), pl.ds(mo(n * 256, 256), 256)
+                out[r, c] = nn(turned[r, :], right[:, c]).astype(BF)
+            loop(right.shape[1] // 256, inner)
+        loop(count // 256, block)
+    weight(act, ct, gd)
+    weight(normed, pre, gu)
+    weight(attended, half, go)
+    fill_image(image, range(6, SROWS), ((OUT_BIAS, v_out), (GAIN_TWO, v_gain), (SHIFT_TWO, v_shift), (UP_BIAS, v_up), (DOWN_BIAS, v_down)))
+
+
+def middle_step(attended, frames, cotangent, weights, smalls, lse):
+    vmem, hbm = pl.BlockSpec(memory_space=pltpu.VMEM), pl.BlockSpec(memory_space=pl.ANY)
+    tokens = frames.shape[0]
+    groups = smalls.shape[0]
+    sds = jax.ShapeDtypeStruct
+    vec = [pltpu.VMEM((1, n), F32) for n in (D, D, D, FF, D)]
+    return pl.pallas_call(
+        mid_kernel,
+        out_shape=[sds((tokens, D), BF), sds((tokens, D), BF), sds((tokens, D), F32), sds((tokens, LANE), F32),
+                   sds((2 * HEADS, tokens), F32), sds((D, D), BF), sds((D, FF), BF), sds((FF, D), BF),
+                   sds((groups, SROWS, LANE), F32)],
+        in_specs=[vmem] * 3 + [hbm] * 3 + [vmem] * 2, out_specs=[vmem] * 9,
+        scratch_shapes=[pltpu.VMEM((D, D), BF), pltpu.VMEM((D, FF), BF), pltpu.VMEM((FF, D), BF),
+                        pltpu.VMEM((tokens, D), F32), pltpu.VMEM((tokens, D), F32), pltpu.VMEM((tokens, D), BF),
+                        pltpu.VMEM((tokens, FF), BF), pltpu.VMEM((tokens, FF), BF), pltpu.VMEM((tokens, D), BF),
+                        pltpu.VMEM((FF, tokens), BF), pltpu.VMEM((tokens, D), F32)] + vec + vec[:3] + [vec[3], vec[4]]
+                       + [pltpu.SemaphoreType.DMA((3,))],
+        compiler_params=pltpu.CompilerParams(vmem_limit_bytes=56 << 20),
+        name="middle",
+    )(attended, frames, cotangent, *weights, smalls, lse)
+
+
+def share_kernel(groups, a_ref, r_ref, a_all, r_all, osem, zs, zr, rs, rr):
+    rep, g = lax.axis_index("rep"), lax.axis_index("grp")
+    tokens = a_ref.shape[0]
+    do_barrier(pltpu.get_barrier_semaphore(), [(rep, lax.rem(g + i, groups)) for i in range(1, groups)])
+
+    def place(r):
+        return a_all.at[pl.ds(mo(r * tokens, 16), tokens), :]
+
+    def zcopy(d, step, src, dst):
+        target = lax.rem(g + (1 if d == 0 else groups - 1), groups)
+        return remote(src, dst, zs.at[d, step], zr.at[d, step], rep, target)
+
+    def has_next(d):
+        return g < groups - 1 if d == 0 else g > 0
+
+    keep = pltpu.make_async_copy(a_ref, place(g), osem.at[0])
+    keep.start()
+    for i in range(1, groups):
+        remote(r_ref, r_all.at[g], rs.at[i - 1], rr.at[i - 1], rep, lax.rem(g + i, groups)).start()
+    for d in range(2):
+        @pl.when(has_next(d))
+        def _():
+            zcopy(d, 0, a_ref, place(g)).start()
+    r_all[g] = r_ref[...]
+    for step in range(groups - 1):
+        for d in range(2):
+            r = g - 1 - step if d == 0 else g + 1 + step
+
+            @pl.when(r >= 0 if d == 0 else r <= groups - 1)
+            def _():
+                zcopy(d, step, place(r), place(r)).wait_recv()
+                if step < groups - 2:
+                    @pl.when(has_next(d))
+                    def _():
+                        zcopy(d, step + 1, place(r), place(r)).start()
+    for step in range(groups - 1):
+        for d in range(2):
+            r = g - step if d == 0 else g + step
+
+            @pl.when(jnp.logical_and(r >= 0 if d == 0 else r <= groups - 1, has_next(d)))
+            def _():
+                zcopy(d, step, place(g), place(g)).wait_send()
+    for i in range(1, groups):
+        cp = remote(r_ref, r_all.at[lax.rem(g + groups - i, groups)], rs.at[i - 1], rr.at[i - 1], rep, lax.rem(g + i, groups))
+        cp.wait_send()
+        cp.wait_recv()
+    keep.wait()
+
+
+def share(agrad, rows, groups):
+    dma = pltpu.SemaphoreType.DMA
+    vmem, hbm = pl.BlockSpec(memory_space=pltpu.VMEM), pl.BlockSpec(memory_space=pl.ANY)
+    return pl.pallas_call(
+        functools.partial(share_kernel, groups),
+        out_shape=[jax.ShapeDtypeStruct((groups * agrad.shape[0], D), BF), jax.ShapeDtypeStruct((groups,) + rows.shape, F32)],
+        in_specs=[vmem] * 2, out_specs=[hbm, vmem],
+        scratch_shapes=[dma((1,)), dma((2, groups)), dma((2, groups)), dma((groups,)), dma((groups,))],
+        compiler_params=pltpu.CompilerParams(collective_id=2, has_side_effects=True),
+        name="share",
+    )(agrad, rows)
+
+
+def query_back(p, g, q_all, k_all, v_all, a_all, stats, grad, tokens):
+    col = pl.ds(mo(p * LANE, LANE), LANE)
+    own = pl.ds(mo(g * tokens, 16), tokens)
+    scale = jnp.asarray(HDIM**-0.5, BF)
+    query, upstream = q_all[own, col] * scale, a_all[own, col]
+    keys, values = k_all[:, col], v_all[:, col]
+    mask = head_mask(tokens)
+    zero = jnp.zeros_like(query)
+    lanes = lax.broadcasted_iota(jnp.int32, (tokens, LANE), 1)
+    results = []
+    for side in range(2):
+        def pick(v):
+            return jnp.where(mask, v, zero) if side == 0 else jnp.where(mask, zero, v)
+        total = jnp.sum(jnp.where(lanes == 2 * p + side, stats[...], 0.0), axis=-1, keepdims=True)
+        centre = jnp.sum(jnp.where(lanes == HEADS + 2 * p + side, stats[...], 0.0), axis=-1, keepdims=True)
+        shares = jnp.exp(nt(pick(query), keys) - total)
+        back = (shares * (nt(pick(upstream), values) - centre)).astype(BF) * scale
+        results.append(nn(back, keys))
+    grad[:, col] = jnp.where(mask, results[0], results[1])
+
+
+def key_back(p, g, q_all, k_all, v_all, a_all, rows, kgrad, vgrad, tokens):
+    col = pl.ds(mo(p * LANE, LANE), LANE)
+    own = pl.ds(mo(g * tokens, 16), tokens)
+    scale = jnp.asarray(HDIM**-0.5, BF)
+    keys, values = k_all[own, col] * scale, v_all[own, col]
+    queries, upstream = q_all[:, col], a_all[:, col]
+    mask = head_mask(tokens)
+    zero = jnp.zeros_like(keys)
+    ks, vs = [], []
+    for side in range(2):
+        def pick(v):
+            return jnp.where(mask, v, zero) if side == 0 else jnp.where(mask, zero, v)
+        total = rows[pl.ds(2 * p + side, 1), :]
+        centre = rows[pl.ds(HEADS + 2 * p + side, 1), :]
+        shares = jnp.exp(nt(pick(keys), queries) - total)
+        vs.append(nn(shares.astype(BF), upstream))
+        back = (shares * (nt(pick(values), upstream) - centre)).astype(BF) * scale
+        ks.append(nn(back, queries))
+    kgrad[:, col] = jnp.where(mask, ks[0], ks[1])
+    vgrad[:, col] = jnp.where(mask, vs[0], vs[1])
+
+
+def input_back(wq, fr, mgrad, gain, shift, qg, kg, vg, pgrad, normed, turned, wide, frames_grad, gq, v_gain, v_shift, v_qv):
+    for i, ref in enumerate((qg, kg, vg)):
+        pgrad[:, i * D:(i + 1) * D] = ref[...].astype(BF)
+    v_qv[0:1, 0:D] = jnp.sum(qg[...], axis=0, keepdims=True)
+    v_qv[0:1, D:2 * D] = jnp.sum(vg[...], axis=0, keepdims=True)
+
+    def block(n):
+        col = pl.ds(mo(n * 256, 256), 256)
+        wide[:, col] = nt(pgrad[...], wq[pl.ds(mo(n * 256, 256), 256), :])
+    loop(D // 256, block)
+    normal, inverse = normalize(fr[...].astype(F32))
+    normed[...] = (normal * gain[...] + shift[...]).astype(BF)
+    upstream = wide[...]
+    v_gain[...] = jnp.sum(upstream * normal, axis=0, keepdims=True)
+    v_shift[...] = jnp.sum(upstream, axis=0, keepdims=True)
+    frames_grad[...] = (mgrad[...] + norm_back(upstream, normal, inverse, gain[...])).astype(BF)
+    turned[...] = normed[...].T
+
+    def outer(i):
+        def inner(n):
+            r, c = pl.ds(mo(i * 256, 256), 256), pl.ds(mo(n * 256, 256), 256)
+            gq[r, c] = nn(turned[r, :], pgrad[:, c]).astype(BF)
+        loop(3 * D // 256, inner)
+    loop(D // 256, outer)
+
+
+def back_kernel(q_all, k_all, v_all, a_all, rows3, stats, wq, fr, mgrad, sm, image_in, frames_grad, gq, image,
+                rows, gain, shift, qg, kg, vg, pgrad, normed, turned, wide, v_gain, v_shift, v_qv):
+    g = lax.axis_index("grp")
+    tokens = fr.shape[0]
+    assemble(sm, GAIN_ONE, gain)
+    assemble(sm, SHIFT_ONE, shift)
+    for i in range(rows3.shape[0]):
+        rows[:, i * tokens:(i + 1) * tokens] = rows3[i]
+    loop(HEADS // 2, lambda p: query_back(p, g, q_all, k_all, v_all, a_all, stats, qg, tokens))
+    loop(HEADS // 2, lambda p: key_back(p, g, q_all, k_all, v_all, a_all, rows, kg, vg, tokens))
+    input_back(wq, fr, mgrad, gain, shift, qg, kg, vg, pgrad, normed, turned, wide, frames_grad, gq, v_gain, v_shift, v_qv)
+    image[...] = image_in[...]
+    fill_image(image, range(6), ((GAIN_ONE, v_gain), (SHIFT_ONE, v_shift), (QV_BIAS, v_qv)))
+
+
+def backward(q_all, k_all, v_all, a_all, rows, stats, wq, frames, mgrad, smalls, image):
+    vmem = pl.BlockSpec(memory_space=pltpu.VMEM)
+    tokens = frames.shape[0]
+    clip = q_all.shape[0]
+    sds = jax.ShapeDtypeStruct
+    return pl.pallas_call(
+        back_kernel,
+        out_shape=[sds((tokens, D), BF), sds((D, 3 * D), BF), sds(image.shape, F32)],
+        in_specs=[vmem] * 11, out_specs=[vmem] * 3,
+        scratch_shapes=[pltpu.VMEM((2 * HEADS, clip), F32), pltpu.VMEM((1, D), F32), pltpu.VMEM((1, D), F32)]
+        + [pltpu.VMEM((tokens, D), F32)] * 3 + [pltpu.VMEM((tokens, 3 * D), BF), pltpu.VMEM((tokens, D), BF),
+           pltpu.VMEM((D, tokens), BF), pltpu.VMEM((tokens, D), F32), pltpu.VMEM((1, D), F32), pltpu.VMEM((1, D), F32),
+           pltpu.VMEM((1, 2 * D), F32)],
+        compiler_params=pltpu.CompilerParams(vmem_limit_bytes=50 << 20),
+        name="backward",
+    )(q_all, k_all, v_all, a_all, rows, stats, wq, frames, mgrad, smalls, image)
 
 
 def on_device(frames, cotangent, params, first_moment, second_moment):
     groups, reps = lax.axis_size("grp"), lax.axis_size("rep")
-    qkv_weight, out_weight, up_weight, down_weight, clip, smalls = gather(params, frames, groups)
-    gain_one, shift_one, qv_bias, out_bias, gain_two, shift_two, up_bias, down_bias = vectors(smalls, groups)
-    width = frames.shape[1]
-    tokens = frames.shape[0]
-    wide = clip.astype(F32)
-    normal_all, inverse_all = norm_forward(wide)
-    normed_all = (normal_all * gain_one + shift_one).astype(BF)
-    start = lax.axis_index("grp") * tokens
-    inputs = frames.astype(F32)
-    normal_one, inverse_one = norm_forward(inputs)
-    normed_one = (normal_one * gain_one + shift_one).astype(BF)
-    query = (jnp.dot(normed_one, qkv_weight[:, :width], preferred_element_type=F32) + qv_bias[:, :width]).astype(BF)
-    kv_bias = jnp.concatenate([jnp.zeros((1, width), F32), qv_bias[:, width:]], axis=1)
-    key_value = (jnp.dot(normed_all, qkv_weight[:, width:], preferred_element_type=F32) + kv_bias).astype(BF)
-    keys = key_value[:, :width]
-    values = key_value[:, width:]
-    attended, log_total = attend(query, keys, values)
-    middle = jnp.dot(attended, out_weight, preferred_element_type=F32) + out_bias + inputs
-    normal_two, inverse_two = norm_forward(middle)
-    normed_two = (normal_two * gain_two + shift_two).astype(BF)
-    hidden_pre = jnp.dot(normed_two, up_weight, preferred_element_type=F32) + up_bias
-    activated = gelu(hidden_pre).astype(BF)
-    out_frames = (jnp.dot(activated, down_weight, preferred_element_type=F32) + down_bias + middle).astype(BF)
-    upstream = cotangent.astype(F32)
-    pre_grad = jnp.dot(cotangent, down_weight.T, preferred_element_type=F32) * gelu_slope(hidden_pre)
-    pre_grad_half = pre_grad.astype(BF)
-    normed_two_grad = jnp.dot(pre_grad_half, up_weight.T, preferred_element_type=F32)
-    middle_grad = upstream + norm_backward(normed_two_grad, normal_two, inverse_two, gain_two)
-    middle_half = middle_grad.astype(BF)
-    attended_grad = jnp.dot(middle_half, out_weight.T, preferred_element_type=F32).astype(BF)
-    centre = row_centre(attended_grad, attended)
-    query_grad, key_grad, value_grad = back_blocks(query, keys, values, attended_grad, log_total, centre)
-    owned = lax.psum_scatter(jnp.concatenate([key_grad, value_grad], axis=1), "grp", scatter_dimension=0, tiled=True)
-    projected_grad = jnp.concatenate([query_grad, owned], axis=1).astype(BF)
-    normed_one_grad = jnp.dot(projected_grad, qkv_weight.T, preferred_element_type=F32)
-    frames_grad = (middle_grad + norm_backward(normed_one_grad, normal_one, inverse_one, gain_one)).astype(BF)
-    grads = [jnp.dot(a.T, b, preferred_element_type=F32).astype(BF) for a, b in (
-        (normed_one, projected_grad), (attended, middle_half), (normed_two, pre_grad_half), (activated, cotangent))]
-    image = small_image(
-        jnp.sum(normed_one_grad * normal_one, axis=0), jnp.sum(normed_one_grad, axis=0),
-        jnp.concatenate([jnp.sum(query_grad, axis=0), jnp.sum(owned[:, width:], axis=0)]),
-        jnp.sum(middle_grad, axis=0), jnp.sum(normed_two_grad * normal_two, axis=0), jnp.sum(normed_two_grad, axis=0),
-        jnp.sum(pre_grad, axis=0), jnp.sum(upstream, axis=0), groups)
-    *blocks, small = reduce_grads(grads, image, groups, reps)
+    wq, wo, wu, wd, clip, smalls = gather(params, frames, groups)
+    q_all, k_all, v_all, attended, lse = forward(clip, wq, smalls, frames.shape[0])
+    out_frames, agrad, mgrad, stats, rows, go, gu, gd, image = middle_step(
+        attended, frames, cotangent, (wo, wu, wd), smalls, lse)
+    a_all, rows_all = share(agrad, rows, groups)
+    frames_grad, gq, image = backward(q_all, k_all, v_all, a_all, rows_all, stats, wq, frames, mgrad, smalls, image)
+    *blocks, small = reduce_grads((gq, go, gu, gd), image, groups, reps)
     param_grad, new_params, new_first, new_second = adam(blocks, small, params, first_moment, second_moment, reps)
     return (out_frames, frames_grad, param_grad, new_params, new_first, new_second)
 

time: 472 us -> 330 us (0.70)
  Pallas kernels: 188 us -> 307 us
  matrix products: 105 us -> 0 us
  waiting for transfers between devices: 88 us -> 0 us
  other arithmetic: 29.7 us -> 0 us
  local copies, waits for them, and re-layouts: 40.4 us -> 18.1 us
  between operations: 14.4 us -> 0.72 us
    pallas_call x0 -> x4, Pallas kernels: none -> 119 us  [the longest x1 37.7 us: middle_step(): pl.pallas_call(mid_kernel, out_shape=[sds((tokens, D), BF), sds((tokens,...]
    dot_general x55 -> x0, matrix products: 105 us -> none  [the longest x6 11.6 us: back_one_pair(): jnp.einsum('hqk,qhd->khd', score_grad, query_pair, preferred_element_type...]
    reduce_scatter x1 -> x0, waiting for transfers between devices: 88 us -> none  [on_device(): lax.psum_scatter(jnp.concatenate([key_grad, value_grad], axis=1), 'grp',...]
    unnamed x68 -> x38, local copies, waits for them, and re-layouts: 6.58 us -> 18.1 us
    reshape x7 -> x0, local copies, waits for them, and re-layouts: 9.37 us -> none  [rows(): return item.reshape(groups, -1)]
    reduce_sum x15 -> x0, other arithmetic: 9.02 us -> none  [the longest x6 3.04 us: attend_one_pair(): jnp.sum(jnp.exp(scores - highest), axis=-1, keepdims=True)]
    concatenate x2 -> x0, other arithmetic: 7.94 us -> none  [the longest x1 6.67 us: on_device(): jnp.concatenate([key_grad, value_grad], axis=1)]
    slice x6 -> x0, local copies, waits for them, and re-layouts: 7.57 us -> none  [the longest x2 3.58 us: on_device(): keys = key_value[:, :width]]
  transfers between devices with their start and end apart: 1 -> 0, of which waited for: 1 -> 0; matrix products, arithmetic and copies ran while one was open for 5% -> 0% of each run, Pallas kernels for 0% -> 0%
where the time goes in v2:
time: 330 us; the launch traced here: 326 us
  Pallas kernels  307 us (93%)
  local copies, waits for them, and re-layouts  18.1 us (5%)
    pallas_call x1, Pallas kernels, reduce_grads(): pl.pallas_call(functools.partial(reduce_kernel, groups, highs), out_shape...  91.3 us
    pallas_call x1, Pallas kernels, gather(): pl.pallas_call(functools.partial(gather_kernel, groups), out_shape=shapes...  72.2 us
    pallas_call x1, Pallas kernels, middle_step(): pl.pallas_call(mid_kernel, out_shape=[sds((tokens, D), BF), sds((tokens,...  37.7 us
    pallas_call x1, Pallas kernels, share(): pl.pallas_call(functools.partial(share_kernel, groups), out_shape=[jax.Sh...  36 us
    pallas_call x1, Pallas kernels, backward(): pl.pallas_call(back_kernel, out_shape=[sds((tokens, D), BF), sds((D, 3 *...  27.1 us
    pallas_call x1, Pallas kernels, adam(): pl.pallas_call(functools.partial(adam_kernel, 1.0 / reps), grid=(STEPS,),...  24.6 us
    pallas_call x1, Pallas kernels, forward(): pl.pallas_call(fwd_kernel, out_shape=[wide] * 3 + [jax.ShapeDtypeStruct((...  18.2 us
    unnamed x38, local copies, waits for them, and re-layouts  18.1 us

profile of v2, /device:TPU:28, one launch (start us, length us, event | category | flops | bytes accessed | tf_op | source)
XLA Modules:
  0.0 326.0 jit_solution(6680771213342929146)
XLA Ops:
  0.6 0.0 copy-start.2
  0.6 1.0 copy-done.2
  1.6 72.2 %gather.1 = (bf16[768,2304]{1,0:T(8,128)(2,1)S(1)}, bf16[768,768]{1,0:T(8,128)(2,1)S(1)}, bf16[768,3072]{1,0:T(8,128)(2,1)S(1)}, bf16[3072,768]{1,0:T(8,128)(2,1...) custom-call(bf16[1,1771776]{1,0:T(2,128)(2,1)} %p_ref.3, bf16[256,768]{1,0:T(8,128)(2,1)S(1)} %copy-done.2), custom_call_target="tpu_custom_call" | custom-call | tf_op jit(solution)/shard_map/gather/pallas_call | solution.py:292
  73.8 0.0 copy-start.1
  73.8 2.2 copy-done.1
  76.0 0.0 copy-start.9
  76.0 1.0 copy-done.9
  77.0 0.0 copy-start.12
  77.0 0.0 copy-start
  77.0 18.2 %forward.1 = (bf16[1024,768]{1,0:T(8,128)(2,1)S(1)}, bf16[1024,768]{1,0:T(8,128)(2,1)S(1)}, bf16[1024,768]{1,0:T(8,128)(2,1)S(1)}, bf16[256,768]{1,0:T(8,128)(2,1)S(1)}, f32[256,128]{1,0:T(8,128)S(1)}) custom-call(bf16[1024,768]{1,0:T(8,128)(2,1)S(1)} %get-tuple-element.40.fa, bf16[768,2304]{1,0:T(8,128)(2,1)S(1)} %get-tuple-element.41.wq, ...), custom_call_target="tpu_custom_call" | custom-call | tf_op jit(solution)/shard_map/forward/pallas_call | solution.py:768
  95.2 0.0 copy-start.5
  95.3 1.3 copy-done.5
  96.5 0.0 copy-start.7
  96.5 1.2 copy-done.7
  97.7 0.0 copy-start.8
  97.7 1.1 copy-done.8
  98.9 0.0 copy-start.14
  98.9 0.7 copy-done.14
  99.6 0.0 copy-start.16
  99.6 0.6 copy-done.16
  100.3 0.0 copy-done.12
  100.3 37.7 %middle.1 = (bf16[256,768]{1,0:T(8,128)(2,1)}, bf16[256,768]{1,0:T(8,128)(2,1)}, f32[256,768]{1,0:T(8,128)}, f32[256,128]{1,0:T(8,128)}, f32[24,256]{1,0:T(8,128...) custom-call(bf16[256,768]{1,0:T(8,128)(2,1)} %copy-done.14, ...), custom_call_target="tpu_custom_call" | custom-call | tf_op jit(solution)/shard_map/middle/pallas_call | solution.py:868
  138.0 0.0 copy-done
  138.0 36.0 %share.1 = (bf16[1024,768]{1,0:T(8,128)(2,1)}, f32[4,24,256]{2,1,0:T(8,128)}) custom-call(bf16[256,768]{1,0:T(8,128)(2,1)} %get-tuple-element.52.a_ref, f32[24,256]{1,0:T(8,128)} %get-tuple-element.53.r_ref), custom_call_target="tpu_custom_call" | custom-call | tf_op jit(solution)/shard_map/share/pallas_call | solution.py:936
  174.0 0.0 copy-start.3
  174.0 1.0 copy-done.3
  175.0 0.0 copy-start.6
  175.0 1.4 copy-done.6
  176.4 0.0 copy-start.11
  176.4 1.1 copy-done.11
  177.6 0.0 copy-start.13
  177.6 0.8 copy-done.13
  178.4 0.0 copy-start.15
  178.4 0.9 copy-done.15
  179.3 0.0 copy-start.17
  179.3 0.9 copy-done.17
  180.2 0.0 copy-start.18
  180.2 0.8 copy-done.18
  181.0 0.0 copy-start.10
  181.0 27.1 %backward.1 = (bf16[256,768]{1,0:T(8,128)(2,1)}, bf16[768,2304]{1,0:T(8,128)(2,1)}, f32[4,24,128]{2,1,0:T(8,128)S(1)}) custom-call(bf16[1024,768]{1,0:T(8,128)(2,1)S(1)} %copy-done.6, bf16[1024,768]{1,0:T(8,128)(2,1)} %copy-done.7, bf16[1024,768]{1,0:T(8,128)(2,1)} %copy-done.8, bf16[1024,768]{1,0:T(8,128)(2,1)} %get-tuple-element.54.a_all, ...), custom_call_target="tpu_custom_call" | custom-call | tf_op jit(solution)/shard_map/backward/pallas_call | solution.py:1035
  208.1 0.0 copy-done.10
  208.1 0.0 copy-start.4
  208.1 2.0 copy-done.4
  210.1 91.3 %reduce.1 = (bf16[192,2304]{1,0:T(8,128)(2,1)S(1)}, bf16[192,768]{1,0:T(8,128)(2,1)S(1)}, bf16[192,3072]{1,0:T(8,128)(2,1)S(1)}, bf16[768,768]{1,0:T(8,128)(2,1)S(1)}, f32[24,128]{1,0:T(8,128)S(1)}) custom-call(bf16[768,2304]{1,0:T(8,128)(2,1)S(1)} %copy-done.4, bf16[768,768]{1,0:T(8,128)(2,1)S(1)} %copy-done.10, bf16[768,3072]{1,0:T(8,128)(2,1)} %get-tuple-element.62.gu, ...), custom_call_target="tpu_custom_call" | custom-call | tf_op jit(solution)/shard_map/reduce/pallas_call | solution.py:558
  301.4 24.6 %adam.1 = (f32[1,1771776]{1,0:T(1,128)}, f32[1,1771776]{1,0:T(1,128)}, f32[1,1771776]{1,0:T(1,128)}, f32[1,1771776]{1,0:T(1,128)}) custom-call(bf16[192,2304]{1,0:T(8,128)(2,1)S(1)} %get-tuple-element.65.gq, bf16[192,768]{1,0:T(8,128)(2,1)S(1)} %get-tuple-element.66.go, bf16[192,3072]{1,0:T(8,128)(2,1)S(1)} %get-tuple-element.67.gu, ...), custom_call_target="tpu_custom_call" | custom-call | tf_op jit(solution)/shard_map/adam/pallas_call | solution.py:632
Async XLA Ops:
  0.6 1.0 copy-start.2
  73.8 2.2 copy-start.1
  76.0 1.0 copy-start.9
  77.0 23.2 %copy-start.12 = (f32[4,24,128]{2,1,0:T(8,128)}, f32[4,24,128]{2,1,0:T(8,128)S(1)}, u32[]{:S(2)}) copy-start(f32[4,24,128]{2,1,0:T(8,128)S(1)} %get-tuple-element.42.sm) | copy-start | bytes 147460
  77.0 61.0 %copy-start = (bf16[768,2304]{1,0:T(8,128)(2,1)}, bf16[768,2304]{1,0:T(8,128)(2,1)S(1)}, u32[]{:S(2)}) copy-start(bf16[768,2304]{1,0:T(8,128)(2,1)S(1)} %get-tuple-element.41.wq) | copy-start | bytes 10616836
  95.2 1.3 copy-start.5
  96.5 1.2 copy-start.7
  97.7 1.2 copy-start.8
  98.9 0.7 copy-start.14
  99.6 0.6 copy-start.16
  174.0 1.0 copy-start.3
  175.0 1.4 copy-start.6
  176.4 1.1 copy-start.11
  177.6 0.8 copy-start.13
  178.4 0.9 copy-start.15
  179.3 0.9 copy-start.17
  180.2 0.8 copy-start.18
  181.0 27.1 %copy-start.10 = (bf16[768,768]{1,0:T(8,128)(2,1)S(1)}, bf16[768,768]{1,0:T(8,128)(2,1)}, u32[]{:S(2)}) copy-start(bf16[768,768]{1,0:T(8,128)(2,1)} %get-tuple-element.61.go) | copy-start | bytes 3538948
  208.1 2.0 copy-start.4

commit v3 on v1

--- a/solution.py
+++ b/solution.py
@@ -321,10 +321,322 @@
     return ref.at[pl.ds(mo(r * m.block + kk * m.quarter + r0, 16), rn), pl.ds(c0, cn)]
 
 
-ORDER = (2, 3, 0, 1)
-
-
-def reduce_kernel(groups, highs, gq, go, gu, gd, sm_ref, oq, oo, ou, od, osm, *scratch):
+EPS_NORM = 1e-05
+ROOT_HALF = 0.7071067811865476
+ROOT_TWO_PI = 0.3989422804014327
+HEADS = D // HDIM
+GAIN_ONE, SHIFT_ONE, QV_BIAS, OUT_BIAS, GAIN_TWO, SHIFT_TWO, UP_BIAS, DOWN_BIAS = (
+    (0, 3), (3, 3), (6, 6), (12, 3), (15, 3), (18, 3), (23, 12), (37, 3))
+
+
+def low_lanes():
+    return lax.broadcasted_iota(jnp.int32, (1, LANE), 1) < 64
+
+
+def assemble(sm, place, out):
+    first, count = place
+    halves = [(gi, first + i) for gi in range(sm.shape[0]) for i in range(count)]
+    for t in range(len(halves) // 2):
+        (g0, h0), (g1, h1) = halves[2 * t], halves[2 * t + 1]
+        a = sm[g0, h0 // 2:h0 // 2 + 1, :]
+        b = sm[g1, h1 // 2:h1 // 2 + 1, :]
+        a = pltpu.roll(a, 64, 1) if h0 % 2 else a
+        b = b if h1 % 2 else pltpu.roll(b, 64, 1)
+        out[0:1, t * LANE:(t + 1) * LANE] = jnp.where(low_lanes(), a, b)
+
+
+def fill_image(image, rows, vectors):
+    where = {}
+    for place, ref in vectors:
+        for i in range(place[1]):
+            where[place[0] + i] = (place[1], i, ref)
+    for gi in range(image.shape[0]):
+        for r in rows:
+            parts = []
+            for side in range(2):
+                spot = where.get(2 * r + side)
+                if spot is None:
+                    parts.append(jnp.zeros((1, LANE), F32))
+                    continue
+                count, i, ref = spot
+                q = gi * count + i
+                v = ref[0:1, q // 2 * LANE:(q // 2 + 1) * LANE]
+                parts.append(v if q % 2 == side else pltpu.roll(v, 64, 1))
+            image[gi, r:r + 1, :] = jnp.where(low_lanes(), parts[0], parts[1])
+
+
+def mean(v):
+    return jnp.sum(v, axis=-1, keepdims=True) * (1.0 / D)
+
+
+def normalize(v):
+    centered = v - mean(v)
+    inverse = lax.rsqrt(mean(centered * centered) + EPS_NORM)
+    return centered * inverse, inverse
+
+
+def norm_back(upstream, normal, inverse, gain):
+    s = upstream * gain
+    return inverse * (s - mean(s) - normal * mean(s * normal))
+
+
+def nn(a, b):
+    return lax.dot_general(a, b, (((1,), (0,)), ((), ())), preferred_element_type=F32)
+
+
+def nt(a, b):
+    return lax.dot_general(a, b, (((1,), (1,)), ((), ())), preferred_element_type=F32)
+
+
+def loop(count, body):
+    def step(i, c):
+        body(i)
+        return c
+    lax.fori_loop(0, count, step, 0)
+
+
+def head_mask(rows):
+    return lax.broadcasted_iota(jnp.int32, (rows, LANE), 1) < HDIM
+
+
+def project_block(j, fa, gain, shift, bias, wq, q_all, k_all, v_all, normed, tokens):
+    at = pl.ds(mo(j * tokens, 16), tokens)
+    normal, _ = normalize(fa[at, :].astype(F32))
+    normed[...] = (normal * gain[...] + shift[...]).astype(BF)
+    for third, out in enumerate((q_all, k_all, v_all)):
+        def body(n):
+            col = pl.ds(mo(n * 256, 256), 256)
+            wide = nn(normed[...], wq[:, pl.ds(mo(third * D + n * 256, 256), 256)])
+            if third != 1:
+                wide = wide + bias[0:1, pl.ds(mo((third // 2) * D + n * 256, 256), 256)]
+            out[at, col] = wide.astype(BF)
+        loop(D // 256, body)
+
+
+def attend_pair(p, g, q_all, k_all, v_all, attended, stats, tokens):
+    col = pl.ds(mo(p * LANE, LANE), LANE)
+    query = q_all[pl.ds(mo(g * tokens, 16), tokens), col] * jnp.asarray(HDIM**-0.5, BF)
+    keys, values = k_all[:, col], v_all[:, col]
+    mask = head_mask(tokens)
+    zero = jnp.zeros_like(query)
+    lanes = lax.broadcasted_iota(jnp.int32, (tokens, LANE), 1)
+    results = []
+    for side in range(2):
+        scores = nt(jnp.where(mask, query, zero) if side == 0 else jnp.where(mask, zero, query), keys)
+        highest = jnp.max(scores, axis=-1, keepdims=True)
+        shares = jnp.exp(scores - highest)
+        total = jnp.sum(shares, axis=-1, keepdims=True)
+        results.append(nn(shares.astype(BF), values) * (1.0 / total))
+        stats[...] = jnp.where(lanes == 2 * p + side, highest + jnp.log(total), stats[...])
+    attended[:, col] = jnp.where(mask, results[0], results[1]).astype(BF)
+
+
+def fwd_kernel(fa, wq, sm, q_all, k_all, v_all, attended, stats, normed, gain, shift, bias):
+    g = lax.axis_index("grp")
+    tokens = attended.shape[0]
+    assemble(sm, GAIN_ONE, gain)
+    assemble(sm, SHIFT_ONE, shift)
+    assemble(sm, QV_BIAS, bias)
+    loop(fa.shape[0] // tokens, lambda j: project_block(j, fa, gain, shift, bias, wq, q_all, k_all, v_all, normed, tokens))
+    stats[...] = jnp.zeros_like(stats)
+    loop(HEADS // 2, lambda p: attend_pair(p, g, q_all, k_all, v_all, attended, stats, tokens))
+
+
+def forward(clip, wq, smalls, tokens):
+    vmem = pl.BlockSpec(memory_space=pltpu.VMEM)
+    wide = jax.ShapeDtypeStruct(clip.shape, BF)
+    return pl.pallas_call(
+        fwd_kernel,
+        out_shape=[wide] * 3 + [jax.ShapeDtypeStruct((tokens, D), BF), jax.ShapeDtypeStruct((tokens, LANE), F32)],
+        in_specs=[vmem] * 3, out_specs=[vmem] * 5,
+        scratch_shapes=[pltpu.VMEM((tokens, D), BF), pltpu.VMEM((1, D), F32), pltpu.VMEM((1, D), F32), pltpu.VMEM((1, 2 * D), F32)],
+        compiler_params=pltpu.CompilerParams(vmem_limit_bytes=40 << 20),
+        name="forward",
+    )(clip, wq, smalls)
+
+
+def mid_kernel(attended, fr, ct, wo_h, wu_h, wd_h, sm, lse, out_frames, agrad, mgrad, stats, rows, go, gu, gd, image,
+               wo, wu, wd, middle, normal, normed, act, pre, half, turned, wide, gain, shift, obias, ubias, dbias,
+               v_gain, v_shift, v_out, v_up, v_down, sem):
+    tokens = attended.shape[0]
+    loads = [pltpu.make_async_copy(a, b, sem.at[i]) for i, (a, b) in enumerate(((wo_h, wo), (wu_h, wu), (wd_h, wd)))]
+    for cp in loads:
+        cp.start()
+    assemble(sm, GAIN_TWO, gain)
+    assemble(sm, SHIFT_TWO, shift)
+    assemble(sm, OUT_BIAS, obias)
+    assemble(sm, UP_BIAS, ubias)
+    assemble(sm, DOWN_BIAS, dbias)
+    loads[0].wait()
+
+    def out_block(n):
+        col = pl.ds(mo(n * 256, 256), 256)
+        middle[:, col] = nn(attended[...], wo[:, col]) + obias[0:1, col] + fr[:, col].astype(F32)
+    loop(D // 256, out_block)
+    value, inverse = normalize(middle[...])
+    normal[...] = value
+    normed[...] = (value * gain[...] + shift[...]).astype(BF)
+    loads[1].wait()
+    loads[2].wait()
+
+    def hidden_block(n):
+        col = pl.ds(mo(n * 256, 256), 256)
+        hidden = nn(normed[...], wu[:, col]) + ubias[0:1, col]
+        bell = 0.5 * (1.0 + lax.erf(hidden * ROOT_HALF))
+        act[:, col] = (hidden * bell).astype(BF)
+        slope = bell + hidden * jnp.exp(-0.5 * hidden * hidden) * ROOT_TWO_PI
+        grad = nt(ct[...], wd[pl.ds(mo(n * 256, 256), 256), :]) * slope
+        v_up[0:1, col] = jnp.sum(grad, axis=0, keepdims=True)
+        pre[:, col] = grad.astype(BF)
+    loop(FF // 256, hidden_block)
+
+    def down_block(n):
+        col = pl.ds(mo(n * 256, 256), 256)
+        out_frames[:, col] = (nn(act[...], wd[:, col]) + dbias[0:1, col] + middle[:, col]).astype(BF)
+    loop(D // 256, down_block)
+
+    def back_block(n):
+        col = pl.ds(mo(n * 256, 256), 256)
+        wide[:, col] = nt(pre[...], wu[pl.ds(mo(n * 256, 256), 256), :])
+    loop(D // 256, back_block)
+    upstream = wide[...]
+    v_gain[...] = jnp.sum(upstream * normal[...], axis=0, keepdims=True)
+    v_shift[...] = jnp.sum(upstream, axis=0, keepdims=True)
+    total = ct[...].astype(F32) + norm_back(upstream, normal[...], inverse, gain[...])
+    mgrad[...] = total
+    half[...] = total.astype(BF)
+    v_out[...] = jnp.sum(total, axis=0, keepdims=True)
+    v_down[...] = jnp.sum(ct[...].astype(F32), axis=0, keepdims=True)
+
+    def attended_block(n):
+        col = pl.ds(mo(n * 256, 256), 256)
+        agrad[:, col] = nt(half[...], wo[pl.ds(mo(n * 256, 256), 256), :]).astype(BF)
+    loop(D // 256, attended_block)
+    lanes = lax.broadcasted_iota(jnp.int32, (tokens, LANE), 1)
+    mask = head_mask(tokens)
+    both = lse[...]
+    for p in range(HEADS // 2):
+        product = agrad[:, p * LANE:(p + 1) * LANE].astype(F32) * attended[:, p * LANE:(p + 1) * LANE].astype(F32)
+        for side in range(2):
+            mine = jnp.where(mask if side == 0 else jnp.logical_not(mask), product, 0.0)
+            both = jnp.where(lanes == HEADS + 2 * p + side, jnp.sum(mine, axis=-1, keepdims=True), both)
+    stats[...] = both
+    rows[...] = both.T[0:2 * HEADS, :]
+
+    def weight(left, right, out):
+        count = left.shape[1]
+        turned[0:count, :] = left[...].T
+
+        def block(i):
+            def inner(n):
+                r, c = pl.ds(mo(i * 256, 256), 256), pl.ds(mo(n * 256, 256), 256)
+                out[r, c] = nn(turned[r, :], right[:, c]).astype(BF)
+            loop(right.shape[1] // 256, inner)
+        loop(count // 256, block)
+    weight(act, ct, gd)
+    weight(normed, pre, gu)
+    weight(attended, half, go)
+    fill_image(image, range(6, SROWS), ((OUT_BIAS, v_out), (GAIN_TWO, v_gain), (SHIFT_TWO, v_shift), (UP_BIAS, v_up), (DOWN_BIAS, v_down)))
+
+
+def middle_step(attended, frames, cotangent, weights, smalls, lse):
+    vmem, hbm = pl.BlockSpec(memory_space=pltpu.VMEM), pl.BlockSpec(memory_space=pl.ANY)
+    tokens = frames.shape[0]
+    groups = smalls.shape[0]
+    sds = jax.ShapeDtypeStruct
+    vec = [pltpu.VMEM((1, n), F32) for n in (D, D, D, FF, D)]
+    return pl.pallas_call(
+        mid_kernel,
+        out_shape=[sds((tokens, D), BF), sds((tokens, D), BF), sds((tokens, D), F32), sds((tokens, LANE), F32),
+                   sds((2 * HEADS, tokens), F32), sds((D, D), BF), sds((D, FF), BF), sds((FF, D), BF),
+                   sds((groups, SROWS, LANE), F32)],
+        in_specs=[vmem] * 3 + [hbm] * 3 + [vmem] * 2, out_specs=[vmem] * 9,
+        scratch_shapes=[pltpu.VMEM((D, D), BF), pltpu.VMEM((D, FF), BF), pltpu.VMEM((FF, D), BF),
+                        pltpu.VMEM((tokens, D), F32), pltpu.VMEM((tokens, D), F32), pltpu.VMEM((tokens, D), BF),
+                        pltpu.VMEM((tokens, FF), BF), pltpu.VMEM((tokens, FF), BF), pltpu.VMEM((tokens, D), BF),
+                        pltpu.VMEM((FF, tokens), BF), pltpu.VMEM((tokens, D), F32)] + vec + vec[:3] + [vec[3], vec[4]]
+                       + [pltpu.SemaphoreType.DMA((3,))],
+        compiler_params=pltpu.CompilerParams(vmem_limit_bytes=56 << 20),
+        name="middle",
+    )(attended, frames, cotangent, *weights, smalls, lse)
+
+
+def query_back(p, g, q_all, k_all, v_all, a_all, stats, grad, tokens):
+    col = pl.ds(mo(p * LANE, LANE), LANE)
+    own = pl.ds(mo(g * tokens, 16), tokens)
+    scale = jnp.asarray(HDIM**-0.5, BF)
+    query, upstream = q_all[own, col] * scale, a_all[own, col]
+    keys, values = k_all[:, col], v_all[:, col]
+    mask = head_mask(tokens)
+    zero = jnp.zeros_like(query)
+    lanes = lax.broadcasted_iota(jnp.int32, (tokens, LANE), 1)
+    results = []
+    for side in range(2):
+        def pick(v):
+            return jnp.where(mask, v, zero) if side == 0 else jnp.where(mask, zero, v)
+        total = jnp.sum(jnp.where(lanes == 2 * p + side, stats[...], 0.0), axis=-1, keepdims=True)
+        centre = jnp.sum(jnp.where(lanes == HEADS + 2 * p + side, stats[...], 0.0), axis=-1, keepdims=True)
+        shares = jnp.exp(nt(pick(query), keys) - total)
+        back = (shares * (nt(pick(upstream), values) - centre)).astype(BF) * scale
+        results.append(nn(back, keys))
+    grad[:, col] = jnp.where(mask, results[0], results[1])
+
+
+def key_back(p, g, q_all, k_all, v_all, a_all, rows, kgrad, vgrad, tokens):
+    col = pl.ds(mo(p * LANE, LANE), LANE)
+    own = pl.ds(mo(g * tokens, 16), tokens)
+    scale = jnp.asarray(HDIM**-0.5, BF)
+    keys, values = k_all[own, col] * scale, v_all[own, col]
+    queries, upstream = q_all[:, col], a_all[:, col]
+    mask = head_mask(tokens)
+    zero = jnp.zeros_like(keys)
+    ks, vs = [], []
+    for side in range(2):
+        def pick(v):
+            return jnp.where(mask, v, zero) if side == 0 else jnp.where(mask, zero, v)
+        total = rows[pl.ds(2 * p + side, 1), :]
+        centre = rows[pl.ds(HEADS + 2 * p + side, 1), :]
+        shares = jnp.exp(nt(pick(keys), queries) - total)
+        vs.append(nn(shares.astype(BF), upstream))
+        back = (shares * (nt(pick(values), upstream) - centre)).astype(BF) * scale
+        ks.append(nn(back, queries))
+    kgrad[:, col] = jnp.where(mask, ks[0], ks[1])
+    vgrad[:, col] = jnp.where(mask, vs[0], vs[1])
+
+
+def input_back(wq, fr, mgrad, gain, shift, qg, kg, vg, pgrad, normed, turned, wide, frames_grad, gq, v_gain, v_shift, v_qv):
+    for i, ref in enumerate((qg, kg, vg)):
+        pgrad[:, i * D:(i + 1) * D] = ref[...].astype(BF)
+    v_qv[0:1, 0:D] = jnp.sum(qg[...], axis=0, keepdims=True)
+    v_qv[0:1, D:2 * D] = jnp.sum(vg[...], axis=0, keepdims=True)
+
+    def block(n):
+        col = pl.ds(mo(n * 256, 256), 256)
+        wide[:, col] = nt(pgrad[...], wq[pl.ds(mo(n * 256, 256), 256), :])
+    loop(D // 256, block)
+    normal, inverse = normalize(fr[...].astype(F32))
+    normed[...] = (normal * gain[...] + shift[...]).astype(BF)
+    upstream = wide[...]
+    v_gain[...] = jnp.sum(upstream * normal, axis=0, keepdims=True)
+    v_shift[...] = jnp.sum(upstream, axis=0, keepdims=True)
+    frames_grad[...] = (mgrad[...] + norm_back(upstream, normal, inverse, gain[...])).astype(BF)
+    turned[...] = normed[...].T
+
+    def outer(i):
+        def inner(n):
+            r, c = pl.ds(mo(i * 256, 256), 256), pl.ds(mo(n * 256, 256), 256)
+            gq[r, c] = nn(turned[r, :], pgrad[:, c]).astype(BF)
+        loop(3 * D // 256, inner)
+    loop(D // 256, outer)
+
+
+ORDER = (3, 2, 1, 0)
+
+
+def finish_kernel(groups, highs, go, gu, gd, q_all, k_all, v_all, agrad, rows_own, stats, wq, fr, mgrad, sm, image_in,
+                  oq, oo, ou, od, osm, frames_grad, *scratch):
+    (a_all, rows3, rows, gq, gain, shift, qg, kg, vg, pgrad, normed, turned, wide, v_gain, v_shift, v_qv, sm_ref,
+     ksem, szs, szr, rs, rr), scratch = scratch[:22], scratch[22:]
     own, scratch = scratch[:4], scratch[4:]
     buf1, scratch = scratch[:4], scratch[4:]
     buf2, scratch = scratch[:4], scratch[4:]
@@ -342,9 +654,61 @@
     core, xn, yn = flip(rep, 1), flip(rep, 2), flip(rep, 4)
     grads = (gq, go, gu, gd)
     outs = (oq, oo, ou, od)
+    tokens = fr.shape[0]
     barrier, peers = greet(rep, g, groups)
     peers += [(flip(rep, 8 << b), g) for b in range(highs)]
     do_barrier(barrier, peers)
+
+    def place(r):
+        return a_all.at[pl.ds(mo(r * tokens, 16), tokens), :]
+
+    def acopy_z(d, step, src, dst):
+        target = lax.rem(g + (1 if d == 0 else groups - 1), groups)
+        return remote(src, dst, szs.at[d, step], szr.at[d, step], rep, target)
+
+    def has_next(d):
+        return g < groups - 1 if d == 0 else g > 0
+
+    def share_start():
+        for d in range(2):
+            @pl.when(has_next(d))
+            def _():
+                acopy_z(d, 0, agrad, place(g)).start()
+        pltpu.make_async_copy(agrad, place(g), ksem.at[0]).start()
+        for i in range(1, groups):
+            remote(rows_own, rows3.at[g], rs.at[i - 1], rr.at[i - 1], rep, lax.rem(g + i, groups)).start()
+        rows3[g] = rows_own[...]
+        pltpu.make_async_copy(agrad, place(g), ksem.at[0]).wait()
+
+    def share_step(step):
+        for d in range(2):
+            r = g - 1 - step if d == 0 else g + 1 + step
+
+            @pl.when(r >= 0 if d == 0 else r <= groups - 1)
+            def _():
+                acopy_z(d, step, place(r), place(r)).wait_recv()
+                if step < groups - 2:
+                    @pl.when(has_next(d))
+                    def _():
+                        acopy_z(d, step + 1, place(r), place(r)).start()
+
+    def share_rows():
+        for i in range(1, groups):
+            remote(rows_own, rows3.at[lax.rem(g + groups - i, groups)], rs.at[i - 1], rr.at[i - 1], rep,
+                   lax.rem(g + i, groups)).wait_recv()
+        for i in range(groups):
+            rows[:, i * tokens:(i + 1) * tokens] = rows3[i]
+
+    def share_sent():
+        for step in range(groups - 1):
+            for d in range(2):
+                r = g - step if d == 0 else g + step
+
+                @pl.when(jnp.logical_and(r >= 0 if d == 0 else r <= groups - 1, has_next(d)))
+                def _():
+                    acopy_z(d, step, place(g), place(g)).wait_send()
+        for i in range(1, groups):
+            remote(rows_own, rows3.at[g], rs.at[i - 1], rr.at[i - 1], rep, lax.rem(g + i, groups)).wait_send()
 
     def row(i):
         return lax.rem(g + 1 + i, groups)
@@ -381,10 +745,14 @@
 
     def r1(t, i):
         m = MATS[t]
-        load(t, i).wait()
         first(t, i).wait_recv()
         at = pl.ds(mo(row(i) * m.block, 16), m.block)
-        add_rows(buf1[t].at[at, :], own[t].at[at, :], buf1[t].at[at, :], m.block)
+        if t:
+            load(t, i).wait()
+            mine = own[t].at[at, :]
+        else:
+            mine = gq.at[at, pl.ds(mo(h * m.half, LANE), m.half)]
+        add_rows(buf1[t].at[at, :], mine, buf1[t].at[at, :], m.block)
         for j in range(2):
             acopy(t, i, j, 2 * j + (1 - x)).start()
             bcopy(t, i, j, 2 * (1 - y) + j).start()
@@ -498,11 +866,31 @@
             osm[...] = smacc[j, g]
 
     chunks = [(t, i) for t in ORDER for i in range(groups)]
-    small(0)
+    share_start()
     for t, i in chunks:
-        first(t, i).start()
-        load(t, i).start()
-    done4 = {}
+        if t:
+            first(t, i).start()
+            load(t, i).start()
+    assemble(sm, GAIN_ONE, gain)
+    assemble(sm, SHIFT_ONE, shift)
+
+    def queries(p):
+        loop(2, lambda i: query_back(p + i, g, q_all, k_all, v_all, a_all, stats, qg, tokens))
+
+    def keys(p):
+        loop(2, lambda i: key_back(p + i, g, q_all, k_all, v_all, a_all, rows, kg, vg, tokens))
+
+    def inputs():
+        input_back(wq, fr, mgrad, gain, shift, qg, kg, vg, pgrad, normed, turned, wide, frames_grad, gq, v_gain, v_shift, v_qv)
+        sm_ref[...] = image_in[...]
+        fill_image(sm_ref, range(6), ((GAIN_ONE, v_gain), (SHIFT_ONE, v_shift), (QV_BIAS, v_qv)))
+        for i in range(groups):
+            first(0, i).start()
+        small(0)
+
+    work = {0: [lambda: queries(0)], 1: [lambda: queries(2), lambda: share_step(0)],
+            2: [lambda: queries(4)], 3: [lambda: share_step(1)], 5: [lambda: share_step(2), share_rows, lambda: keys(0)],
+            6: [lambda: keys(2)], 7: [lambda: keys(4)], 8: [inputs]}
     total = len(chunks)
     smalls = 1
     for n in range(total + 16):
@@ -510,7 +898,7 @@
             r1(*chunks[n])
         if 0 <= n - 2 < total:
             r2(*chunks[n - 2])
-        if n % 2 and smalls <= len(partners):
+        if n > 9 and smalls <= len(partners):
             small(smalls)
             smalls += 1
         if 0 <= n - 4 < total:
@@ -523,6 +911,9 @@
                 r5(t)
             if n == last + 6:
                 r6(t)
+        for piece in work.get(n, ()):
+            piece()
+    share_sent()
     for t in ORDER:
         r7(t)
     for t, i in chunks:
@@ -544,26 +935,38 @@
         smcopy(j).wait_send()
 
 
-def reduce_grads(grads, smalls, groups, reps):
+def finish(grads, q_all, k_all, v_all, agrad, rows, stats, wq, frames, mgrad, smalls, image, reps):
     dma = pltpu.SemaphoreType.DMA
+    groups = smalls.shape[0]
+    tokens = frames.shape[0]
+    clip = q_all.shape[0]
     highs = (reps // 8).bit_length() - 1
     steps = 3 + highs + groups.bit_length() - 1
+    vmem, hbm = pl.BlockSpec(memory_space=pltpu.VMEM), pl.BlockSpec(memory_space=pl.ANY)
     wide = [pltpu.VMEM((m.block * groups, m.half), BF) for m in MATS]
-    scratch = wide * 4
+    scratch = [pltpu.VMEM((clip, D), BF), pltpu.VMEM((groups, 2 * HEADS, tokens), F32), pltpu.VMEM((2 * HEADS, clip), F32),
+               pltpu.VMEM((D, 3 * D), BF), pltpu.VMEM((1, D), F32), pltpu.VMEM((1, D), F32)]
+    scratch += [pltpu.VMEM((tokens, D), F32)] * 3
+    scratch += [pltpu.VMEM((tokens, 3 * D), BF), pltpu.VMEM((tokens, D), BF), pltpu.VMEM((D, tokens), BF),
+                pltpu.VMEM((tokens, D), F32), pltpu.VMEM((1, D), F32), pltpu.VMEM((1, D), F32), pltpu.VMEM((1, 2 * D), F32),
+                pltpu.VMEM(image.shape, F32), dma((1,)), dma((2, groups)), dma((2, groups)), dma((groups,)), dma((groups,))]
+    scratch += [pltpu.VMEM((16, LANE), BF)] + wide[1:]
+    scratch += wide * 3
     scratch += [pltpu.VMEM((groups, m.quarter, m.half), BF) for m in MATS]
     scratch += [pltpu.VMEM((2 * highs + 1, m.quarter, m.half), BF) for m in MATS]
     scratch += [pltpu.VMEM((steps + 1, groups, SROWS, LANE), F32), pltpu.VMEM((steps, groups, SROWS, LANE), F32)]
     scratch += [dma((4, groups))] * 3 + [dma((4, groups, 2))] * 4 + [dma((4, groups))] * 6
     scratch += [dma((4, max(highs, 1)))] * 2 + [dma((4,))] * 11 + [dma((steps,))] * 2
     return pl.pallas_call(
-        functools.partial(reduce_kernel, groups, highs),
-        out_shape=[jax.ShapeDtypeStruct((m.block, m.cols), BF) for m in MATS] + [jax.ShapeDtypeStruct((SROWS, LANE), F32)],
-        in_specs=[pl.BlockSpec(memory_space=pl.ANY)] * 4 + [pl.BlockSpec(memory_space=pltpu.VMEM)],
-        out_specs=[pl.BlockSpec(memory_space=pl.ANY)] * 4 + [pl.BlockSpec(memory_space=pltpu.VMEM)],
+        functools.partial(finish_kernel, groups, highs),
+        out_shape=[jax.ShapeDtypeStruct((m.block, m.cols), BF) for m in MATS]
+        + [jax.ShapeDtypeStruct((SROWS, LANE), F32), jax.ShapeDtypeStruct((tokens, D), BF)],
+        in_specs=[hbm] * 3 + [vmem] * 11,
+        out_specs=[hbm] * 4 + [vmem] * 2,
         scratch_shapes=scratch,
-        compiler_params=pltpu.CompilerParams(collective_id=1, has_side_effects=True, vmem_limit_bytes=44 << 20),
-        name="reduce",
-    )(*grads, smalls)
+        compiler_params=pltpu.CompilerParams(collective_id=1, has_side_effects=True, vmem_limit_bytes=62 << 20),
+        name="finish",
+    )(*grads, q_all, k_all, v_all, agrad, rows, stats, wq, frames, mgrad, smalls, image)
 
 
 BETA_ONE = 0.9
@@ -641,175 +1044,14 @@
     )(*blocks, smalls, params, first, second)
 
 
-EPS_NORM = 1e-05
-
-
-def norm_forward(values):
-    center = values - jnp.mean(values, axis=-1, keepdims=True)
-    inverse = lax.rsqrt(jnp.mean(center * center, axis=-1, keepdims=True) + EPS_NORM)
-    return (center * inverse, inverse)
-
-
-def norm_backward(upstream, normalized, inverse, gain):
-    scaled = upstream * gain
-    return inverse * (
-        scaled
-        - jnp.mean(scaled, axis=-1, keepdims=True)
-        - normalized * jnp.mean(scaled * normalized, axis=-1, keepdims=True)
-    )
-
-
-def gelu(values):
-    return 0.5 * values * (1.0 + lax.erf(values * 0.7071067811865476))
-
-
-def gelu_slope(values):
-    return (
-        0.5 * (1.0 + lax.erf(values * 0.7071067811865476))
-        + values * jnp.exp(-0.5 * values * values) * 0.3989422804014327
-    )
-
-
-def to_pairs(matrix):
-    heads = matrix.shape[1] // HDIM
-    return matrix.reshape(matrix.shape[0], heads // 2, 2, HDIM).transpose(1, 0, 2, 3)
-
-
-def from_pairs(stacked):
-    return stacked.transpose(1, 0, 2, 3).reshape(stacked.shape[1], -1)
-
-
-def attend(query, keys, values):
-    scale = HDIM ** (-0.5)
-
-    def attend_one_pair(items):
-        query_pair, key_pair, value_pair = items
-        scores = (
-            jnp.einsum("qhd,khd->hqk", query_pair, key_pair, preferred_element_type=jnp.float32)
-            * scale
-        )
-        highest = jnp.max(scores, axis=-1, keepdims=True)
-        log_total = highest + jnp.log(jnp.sum(jnp.exp(scores - highest), axis=-1, keepdims=True))
-        shares = jnp.exp(scores - log_total).astype(jnp.bfloat16)
-        mixed = jnp.einsum("hqk,khd->qhd", shares, value_pair, preferred_element_type=jnp.float32)
-        return (mixed, log_total[..., 0])
-
-    mixed, log_total = lax.map(attend_one_pair, (to_pairs(query), to_pairs(keys), to_pairs(values)))
-    return (from_pairs(mixed).astype(jnp.bfloat16), log_total)
-
-
-def row_centre(upstream, attended):
-    product = to_pairs(upstream).astype(jnp.float32) * to_pairs(attended).astype(jnp.float32)
-    return jnp.sum(product, axis=-1).transpose(0, 2, 1)
-
-
-def back_blocks(query, keys, values, upstream, log_total, centre):
-    scale = HDIM ** (-0.5)
-
-    def back_one_pair(items):
-        query_pair, key_pair, value_pair, upstream_pair, log_pair, centre_pair = items
-        scores = (
-            jnp.einsum("qhd,khd->hqk", query_pair, key_pair, preferred_element_type=jnp.float32)
-            * scale
-        )
-        shares = jnp.exp(scores - log_pair[..., None])
-        share_grad = jnp.einsum(
-            "qhd,khd->hqk", upstream_pair, value_pair, preferred_element_type=jnp.float32
-        )
-        score_grad = (shares * (share_grad - centre_pair[..., None]) * scale).astype(jnp.bfloat16)
-        result = []
-        result.append(
-            jnp.einsum("hqk,khd->qhd", score_grad, key_pair, preferred_element_type=jnp.float32)
-        )
-        result.append(
-            jnp.einsum("hqk,qhd->khd", score_grad, query_pair, preferred_element_type=jnp.float32)
-        )
-        result.append(
-            jnp.einsum(
-                "hqk,qhd->khd",
-                shares.astype(jnp.bfloat16),
-                upstream_pair,
-                preferred_element_type=jnp.float32,
-            )
-        )
-        return tuple(result)
-
-    stacked = (
-        to_pairs(query),
-        to_pairs(keys),
-        to_pairs(values),
-        to_pairs(upstream),
-        log_total,
-        centre,
-    )
-    outputs = lax.map(back_one_pair, stacked)
-    return tuple((from_pairs(item) for item in outputs))
-
-
-def vectors(smalls, groups):
-    rows = smalls.reshape(groups, SROWS * LANE)
-
-    def pick(first, count):
-        return rows[:, first:first + count].reshape(1, groups * count)
-    qv = pick(384, 384)
-    return (pick(0, 192), pick(192, 192), qv, pick(768, 192), pick(960, 192), pick(1152, 192), pick(1472, 768), pick(2368, 192))
-
-
-def small_image(gain_one, shift_one, qv, out_bias, gain_two, shift_two, up_bias, down_bias, groups):
-    def rows(item):
-        return item.reshape(groups, -1)
-    gap = jnp.zeros((groups, 64), F32)
-    pieces = [rows(gain_one), rows(shift_one), rows(qv), rows(out_bias), rows(gain_two), rows(shift_two), gap,
-              gap, rows(up_bias), gap, gap, rows(down_bias), jnp.zeros((groups, 512), F32)]
-    return jnp.concatenate(pieces, axis=1).reshape(groups, SROWS, LANE)
-
-
 def on_device(frames, cotangent, params, first_moment, second_moment):
     groups, reps = lax.axis_size("grp"), lax.axis_size("rep")
-    qkv_weight, out_weight, up_weight, down_weight, clip, smalls = gather(params, frames, groups)
-    gain_one, shift_one, qv_bias, out_bias, gain_two, shift_two, up_bias, down_bias = vectors(smalls, groups)
-    width = frames.shape[1]
-    tokens = frames.shape[0]
-    wide = clip.astype(F32)
-    normal_all, inverse_all = norm_forward(wide)
-    normed_all = (normal_all * gain_one + shift_one).astype(BF)
-    start = lax.axis_index("grp") * tokens
-    inputs = frames.astype(F32)
-    normal_one, inverse_one = norm_forward(inputs)
-    normed_one = (normal_one * gain_one + shift_one).astype(BF)
-    query = (jnp.dot(normed_one, qkv_weight[:, :width], preferred_element_type=F32) + qv_bias[:, :width]).astype(BF)
-    kv_bias = jnp.concatenate([jnp.zeros((1, width), F32), qv_bias[:, width:]], axis=1)
-    key_value = (jnp.dot(normed_all, qkv_weight[:, width:], preferred_element_type=F32) + kv_bias).astype(BF)
-    keys = key_value[:, :width]
-    values = key_value[:, width:]
-    attended, log_total = attend(query, keys, values)
-    middle = jnp.dot(attended, out_weight, preferred_element_type=F32) + out_bias + inputs
-    normal_two, inverse_two = norm_forward(middle)
-    normed_two = (normal_two * gain_two + shift_two).astype(BF)
-    hidden_pre = jnp.dot(normed_two, up_weight, preferred_element_type=F32) + up_bias
-    activated = gelu(hidden_pre).astype(BF)
-    out_frames = (jnp.dot(activated, down_weight, preferred_element_type=F32) + down_bias + middle).astype(BF)
-    upstream = cotangent.astype(F32)
-    pre_grad = jnp.dot(cotangent, down_weight.T, preferred_element_type=F32) * gelu_slope(hidden_pre)
-    pre_grad_half = pre_grad.astype(BF)
-    normed_two_grad = jnp.dot(pre_grad_half, up_weight.T, preferred_element_type=F32)
-    middle_grad = upstream + norm_backward(normed_two_grad, normal_two, inverse_two, gain_two)
-    middle_half = middle_grad.astype(BF)
-    attended_grad = jnp.dot(middle_half, out_weight.T, preferred_element_type=F32).astype(BF)
-    centre = row_centre(attended_grad, attended)
-    query_grad, key_grad, value_grad = back_blocks(query, keys, values, attended_grad, log_total, centre)
-    owned = lax.psum_scatter(jnp.concatenate([key_grad, value_grad], axis=1), "grp", scatter_dimension=0, tiled=True)
-    projected_grad = jnp.concatenate([query_grad, owned], axis=1).astype(BF)
-    normed_one_grad = jnp.dot(projected_grad, qkv_weight.T, preferred_element_type=F32)
-    frames_grad = (middle_grad + norm_backward(normed_one_grad, normal_one, inverse_one, gain_one)).astype(BF)
-    grads = [jnp.dot(a.T, b, preferred_element_type=F32).astype(BF) for a, b in (
-        (normed_one, projected_grad), (attended, middle_half), (normed_two, pre_grad_half), (activated, cotangent))]
-    image = small_image(
-        jnp.sum(normed_one_grad * normal_one, axis=0), jnp.sum(normed_one_grad, axis=0),
-        jnp.concatenate([jnp.sum(query_grad, axis=0), jnp.sum(owned[:, width:], axis=0)]),
-        jnp.sum(middle_grad, axis=0), jnp.sum(normed_two_grad * normal_two, axis=0), jnp.sum(normed_two_grad, axis=0),
-        jnp.sum(pre_grad, axis=0), jnp.sum(upstream, axis=0), groups)
-    *blocks, small = reduce_grads(grads, image, groups, reps)
+    wq, wo, wu, wd, clip, smalls = gather(params, frames, groups)
+    q_all, k_all, v_all, attended, lse = forward(clip, wq, smalls, frames.shape[0])
+    out_frames, agrad, mgrad, stats, rows, go, gu, gd, image = middle_step(
+        attended, frames, cotangent, (wo, wu, wd), smalls, lse)
+    *blocks, small, frames_grad = finish(
+        (go, gu, gd), q_all, k_all, v_all, agrad, rows, stats, wq, frames, mgrad, smalls, image, reps)
     param_grad, new_params, new_first, new_second = adam(blocks, small, params, first_moment, second_moment, reps)
     return (out_frames, frames_grad, param_grad, new_params, new_first, new_second)
 

time: 472 us -> 287 us (0.61)
  matrix products: 105 us -> 0 us
  waiting for transfers between devices: 88 us -> 0 us
  Pallas kernels: 188 us -> 265 us
  other arithmetic: 29.7 us -> 0 us
  local copies, waits for them, and re-layouts: 40.4 us -> 17.1 us
  between operations: 14.4 us -> 0.7 us
    dot_general x55 -> x0, matrix products: 105 us -> none  [the longest x6 11.6 us: back_one_pair(): jnp.einsum('hqk,qhd->khd', score_grad, query_pair, preferred_element_type...]
    reduce_scatter x1 -> x0, waiting for transfers between devices: 88 us -> none  [on_device(): lax.psum_scatter(jnp.concatenate([key_grad, value_grad], axis=1), 'grp',...]
    pallas_call x1 -> x3, Pallas kernels: 91.1 us -> 168 us  [the longest x1 112 us: finish(): pl.pallas_call(functools.partial(finish_kernel, groups, highs), out_shape...]
    unnamed x68 -> x33, local copies, waits for them, and re-layouts: 6.58 us -> 17.1 us
    reshape x7 -> x0, local copies, waits for them, and re-layouts: 9.37 us -> none  [rows(): return item.reshape(groups, -1)]
    reduce_sum x15 -> x0, other arithmetic: 9.02 us -> none  [the longest x6 3.04 us: attend_one_pair(): jnp.sum(jnp.exp(scores - highest), axis=-1, keepdims=True)]
    concatenate x2 -> x0, other arithmetic: 7.94 us -> none  [the longest x1 6.67 us: on_device(): jnp.concatenate([key_grad, value_grad], axis=1)]
    slice x6 -> x0, local copies, waits for them, and re-layouts: 7.57 us -> none  [the longest x2 3.58 us: on_device(): keys = key_value[:, :width]]
  transfers between devices with their start and end apart: 1 -> 0, of which waited for: 1 -> 0; matrix products, arithmetic and copies ran while one was open for 5% -> 0% of each run, Pallas kernels for 0% -> 0%
where the time goes in v3:
time: 287 us; the launch traced here: 282 us
  Pallas kernels  265 us (92%)
  local copies, waits for them, and re-layouts  17.1 us (6%)
    pallas_call x1, Pallas kernels, finish(): pl.pallas_call(functools.partial(finish_kernel, groups, highs), out_shape...  112 us
    pallas_call x1, Pallas kernels, gather(): pl.pallas_call(functools.partial(gather_kernel, groups), out_shape=shapes...  72.2 us
    pallas_call x1, Pallas kernels, middle_step(): pl.pallas_call(mid_kernel, out_shape=[sds((tokens, D), BF), sds((tokens,...  37.8 us
    pallas_call x1, Pallas kernels, adam(): pl.pallas_call(functools.partial(adam_kernel, 1.0 / reps), grid=(STEPS,),...  24.7 us
    pallas_call x1, Pallas kernels, forward(): pl.pallas_call(fwd_kernel, out_shape=[wide] * 3 + [jax.ShapeDtypeStruct((...  18.2 us
    unnamed x33, local copies, waits for them, and re-layouts  17.1 us

profile of v3, /device:TPU:28, one launch (start us, length us, event | category | flops | bytes accessed | tf_op | source)
XLA Modules:
  0.0 282.3 jit_solution(7162498871926702512)
XLA Ops:
  0.6 0.0 copy-start.2
  0.6 1.0 copy-done.2
  1.6 72.2 %gather.1 = (bf16[768,2304]{1,0:T(8,128)(2,1)S(1)}, bf16[768,768]{1,0:T(8,128)(2,1)S(1)}, bf16[768,3072]{1,0:T(8,128)(2,1)S(1)}, bf16[3072,768]{1,0:T(8,128)(2,1...) custom-call(bf16[1,1771776]{1,0:T(2,128)(2,1)} %p_ref.3, bf16[256,768]{1,0:T(8,128)(2,1)S(1)} %copy-done.2), custom_call_target="tpu_custom_call" | custom-call | tf_op jit(solution)/shard_map/gather/pallas_call | solution.py:292
  73.8 0.0 copy-start.1
  73.8 2.2 copy-done.1
  76.0 0.0 copy-start.8
  76.0 1.0 copy-done.8
  77.0 0.0 copy-start.10
  77.0 18.2 %forward.1 = (bf16[1024,768]{1,0:T(8,128)(2,1)S(1)}, bf16[1024,768]{1,0:T(8,128)(2,1)S(1)}, bf16[1024,768]{1,0:T(8,128)(2,1)S(1)}, bf16[256,768]{1,0:T(8,128)(2,1)S(1)}, f32[256,128]{1,0:T(8,128)S(1)}) custom-call(bf16[1024,768]{1,0:T(8,128)(2,1)S(1)} %get-tuple-element.36.fa, bf16[768,2304]{1,0:T(8,128)(2,1)S(1)} %get-tuple-element.37.wq, ...), custom_call_target="tpu_custom_call" | custom-call | tf_op jit(solution)/shard_map/forward/pallas_call | solution.py:448
  95.3 0.0 copy-start
  95.3 1.8 copy-done
  97.1 0.0 copy-start.3
  97.1 1.2 copy-done.3
  98.2 0.0 copy-start.4
  98.3 1.1 copy-done.4
  99.4 0.0 copy-start.5
  99.4 1.3 copy-done.5
  100.7 0.0 copy-start.11
  100.7 0.7 copy-done.11
  101.4 0.0 copy-start.13
  101.4 0.6 copy-done.13
  102.0 0.0 copy-done.10
  102.0 37.8 %middle.1 = (bf16[256,768]{1,0:T(8,128)(2,1)}, bf16[256,768]{1,0:T(8,128)(2,1)}, f32[256,768]{1,0:T(8,128)}, f32[256,128]{1,0:T(8,128)}, f32[24,256]{1,0:T(8,128...) custom-call(bf16[256,768]{1,0:T(8,128)(2,1)} %copy-done.11, ...), custom_call_target="tpu_custom_call" | custom-call | tf_op jit(solution)/shard_map/middle/pallas_call | solution.py:548
  139.8 111.7 %finish.1 = (bf16[192,2304]{1,0:T(8,128)(2,1)}, bf16[192,768]{1,0:T(8,128)(2,1)}, bf16[192,3072]{1,0:T(8,128)(2,1)}, bf16[768,768]{1,0:T(8,128)(2,1)}, f32[24,128]{1,0:T(8,128)}, /*index=5*/bf16[256,768]{1,0:T(8,128)(2,1)}) custom-call(bf16[768,768]{1,0:T(8,128)(2,1)} %get-tuple-element.45.go, bf16[768,3072]{1,0:T(8,128)(2,1)} %get-tuple-element.46.gu, ...), custom_call_target="tpu_custom_call" | custom-call | tf_op jit(solution)/shard_map/finish/pallas_call | solution.py:960
  251.5 0.0 copy-start.6
  251.5 1.3 copy-done.6
  252.8 0.0 copy-start.7
  252.8 1.3 copy-done.7
  254.1 0.0 copy-start.9
  254.1 1.2 copy-done.9
  255.3 0.0 copy-start.12
  255.3 1.0 copy-done.12
  256.2 0.0 copy-start.14
  256.2 0.7 copy-done.14
  256.9 0.0 copy-start.15
  256.9 24.7 %adam.1 = (f32[1,1771776]{1,0:T(1,128)}, f32[1,1771776]{1,0:T(1,128)}, f32[1,1771776]{1,0:T(1,128)}, f32[1,1771776]{1,0:T(1,128)}) custom-call(bf16[192,2304]{1,0:T(8,128)(2,1)S(1)} %copy-done.9, bf16[192,768]{1,0:T(8,128)(2,1)S(1)} %copy-done.12, bf16[192,3072]{1,0:T(8,128)(2,1)S(1)} %copy-done.6, bf16[768,768]{1,0:T(8,128)(2,1)S(1)} %copy-done.7, ...), custom_call_target="tpu_custom_call" | custom-call | tf_op jit(solution)/shard_map/adam/pallas_call | solution.py:1035
  281.6 0.0 copy-done.15
  281.6 0.7 copy.12
Async XLA Ops:
  0.6 1.0 copy-start.2
  73.8 2.2 copy-start.1
  76.0 1.0 copy-start.8
  77.0 25.0 %copy-start.10 = (f32[4,24,128]{2,1,0:T(8,128)}, f32[4,24,128]{2,1,0:T(8,128)S(1)}, u32[]{:S(2)}) copy-start(f32[4,24,128]{2,1,0:T(8,128)S(1)} %get-tuple-element.38.sm) | copy-start | bytes 147460
  95.3 1.8 copy-start
  97.1 1.2 copy-start.3
  98.2 1.1 copy-start.4
  99.4 1.3 copy-start.5
  100.7 0.7 copy-start.11
  101.4 0.6 copy-start.13
  251.5 1.3 copy-start.6
  252.8 1.3 copy-start.7
  254.1 1.2 copy-start.9
  255.3 1.0 copy-start.12
  256.2 0.7 copy-start.14
  256.9 24.7 %copy-start.15 = (bf16[256,768]{1,0:T(8,128)(2,1)S(1)}, bf16[256,768]{1,0:T(8,128)(2,1)}, u32[]{:S(2)}) copy-start(bf16[256,768]{1,0:T(8,128)(2,1)} %get-tuple-element.73) | copy-start | bytes 1179652

commit v4 on v3

v4 whole, which is shorter than its diff:
```python
import functools
import types

import jax
import jax.numpy as jnp
from jax import lax
from jax.sharding import PartitionSpec as P
from jax.experimental import pallas as pl
from jax.experimental.pallas import tpu as pltpu

MESH = pl.DeviceIdType.MESH
BF = jnp.bfloat16
F32 = jnp.float32
D = 768
FF = 3072
HDIM = 64
LANE = 128
FLAT = 1771776
FROWS = FLAT // LANE


class Mat:
    def __init__(self, offset, block, cols, suba, subb):
        self.offset, self.block, self.cols = offset, block, cols
        self.tiles = cols // LANE
        self.row0 = offset // LANE
        self.shifted = offset % LANE != 0
        self.quarter = block // 4
        self.half = cols // 2
        self.sub = (suba, subb)


QKV = Mat(384, 192, 2304, (0, 48, 0, 640), (0, 48, 640, 512))
OUT = Mat(443136, 192, 768, (0, 48, 0, 128), (0, 48, 128, 256))
UP = Mat(591168, 192, 3072, (0, 48, 0, 768), (0, 48, 768, 768))
DOWN = Mat(1181760, 768, 768, (0, 96, 0, 384), (96, 96, 0, 384))
MATS = (QKV, OUT, UP, DOWN)
SMALL = ((0, 3), (3459, 3), (4614, 5), (9226, 7), (13840, 2))
SROWS = 24


def flip(index, bit):
    return index + bit - 2 * bit * ((index // bit) % 2)


def mo(value, by):
    return pl.multiple_of(value, by)


def part(ref, m, r, k, h, sub=None):
    r0, rn, c0, cn = m.sub[sub] if sub is not None else (0, m.quarter, 0, m.half)
    row = mo(r * m.block + k * m.quarter + r0, 16)
    col = mo(h * m.half + c0, LANE)
    return ref.at[pl.ds(row, rn), pl.ds(col, cn)]


def slab(ref, m, r, h):
    return ref.at[pl.ds(mo(r * m.block, 16), m.block), pl.ds(mo(h * m.half, LANE), m.half)]


def remote(src, dst, send, recv, rep, grp):
    return pltpu.make_async_remote_copy(
        src_ref=src, dst_ref=dst, send_sem=send, recv_sem=recv,
        device_id={"rep": rep, "grp": grp}, device_id_type=MESH)


def greet(rep, g, groups):
    barrier = pltpu.get_barrier_semaphore()
    peers = [(flip(rep, b), g) for b in (1, 2, 4)]
    peers += [(rep, lax.rem(g + i, groups)) for i in range(1, groups)]
    return barrier, peers


def do_barrier(barrier, peers):
    for r, gg in peers:
        pl.semaphore_signal(barrier, inc=1, device_id={"rep": r, "grp": gg}, device_id_type=MESH)
    pl.semaphore_wait(barrier, len(peers))


def add_rows(dst, a, b, rows, step=16):
    def body(i, c):
        at = pl.ds(mo(i * step, 16), step)
        dst[at, :] = (a[at, :].astype(F32) + b[at, :].astype(F32)).astype(dst.dtype)
        return c
    lax.fori_loop(0, rows // step, body, 0)


EPS_NORM = 1e-05
ROOT_HALF = 0.7071067811865476
ROOT_TWO_PI = 0.3989422804014327
HEADS = D // HDIM
GAIN_ONE, SHIFT_ONE, QV_BIAS, OUT_BIAS, GAIN_TWO, SHIFT_TWO, UP_BIAS, DOWN_BIAS = (
    (0, 3), (3, 3), (6, 6), (12, 3), (15, 3), (18, 3), (23, 12), (37, 3))


def low_lanes():
    return lax.broadcasted_iota(jnp.int32, (1, LANE), 1) < 64


def assemble(sm, place, out):
    first, count = place
    halves = [(gi, first + i) for gi in range(sm.shape[0]) for i in range(count)]
    for t in range(len(halves) // 2):
        (g0, h0), (g1, h1) = halves[2 * t], halves[2 * t + 1]
        a = sm[g0, h0 // 2:h0 // 2 + 1, :]
        b = sm[g1, h1 // 2:h1 // 2 + 1, :]
        a = pltpu.roll(a, 64, 1) if h0 % 2 else a
        b = b if h1 % 2 else pltpu.roll(b, 64, 1)
        out[0:1, t * LANE:(t + 1) * LANE] = jnp.where(low_lanes(), a, b)


def fill_image(image, rows, vectors):
    where = {}
    for place, ref in vectors:
        for i in range(place[1]):
            where[place[0] + i] = (place[1], i, ref)
    for gi in range(image.shape[0]):
        for r in rows:
            parts = []
            for side in range(2):
                spot = where.get(2 * r + side)
                if spot is None:
                    parts.append(jnp.zeros((1, LANE), F32))
                    continue
                count, i, ref = spot
                q = gi * count + i
                v = ref[0:1, q // 2 * LANE:(q // 2 + 1) * LANE]
                parts.append(v if q % 2 == side else pltpu.roll(v, 64, 1))
            image[gi, r:r + 1, :] = jnp.where(low_lanes(), parts[0], parts[1])


def mean(v):
    return jnp.sum(v, axis=-1, keepdims=True) * (1.0 / D)


def normalize(v):
    centered = v - mean(v)
    inverse = lax.rsqrt(mean(centered * centered) + EPS_NORM)
    return centered * inverse, inverse


def norm_back(upstream, normal, inverse, gain):
    s = upstream * gain
    return inverse * (s - mean(s) - normal * mean(s * normal))


def nn(a, b):
    return lax.dot_general(a, b, (((1,), (0,)), ((), ())), preferred_element_type=F32)


def nt(a, b):
    return lax.dot_general(a, b, (((1,), (1,)), ((), ())), preferred_element_type=F32)


def loop(count, body):
    def step(i, c):
        body(i)
        return c
    lax.fori_loop(0, count, step, 0)


def head_mask(rows):
    return lax.broadcasted_iota(jnp.int32, (rows, LANE), 1) < HDIM


def project_block(j, fa, gain, shift, bias, wq, q_all, k_all, v_all, normed, tokens):
    at = pl.ds(mo(j * tokens, 16), tokens)
    normal, _ = normalize(fa[at, :].astype(F32))
    normed[...] = (normal * gain[...] + shift[...]).astype(BF)
    for third, out in enumerate((q_all, k_all, v_all)):
        def body(n):
            col = pl.ds(mo(n * 256, 256), 256)
            wide = nn(normed[...], wq[:, pl.ds(mo(third * D + n * 256, 256), 256)])
            if third != 1:
                wide = wide + bias[0:1, pl.ds(mo((third // 2) * D + n * 256, 256), 256)]
            out[at, col] = wide.astype(BF)
        loop(D // 256, body)


def attend_pair(p, g, q_all, k_all, v_all, attended, stats, tokens):
    col = pl.ds(mo(p * LANE, LANE), LANE)
    query = q_all[pl.ds(mo(g * tokens, 16), tokens), col] * jnp.asarray(HDIM**-0.5, BF)
    keys, values = k_all[:, col], v_all[:, col]
    mask = head_mask(tokens)
    zero = jnp.zeros_like(query)
    lanes = lax.broadcasted_iota(jnp.int32, (tokens, LANE), 1)
    results = []
    for side in range(2):
        scores = nt(jnp.where(mask, query, zero) if side == 0 else jnp.where(mask, zero, query), keys)
        highest = jnp.max(scores, axis=-1, keepdims=True)
        shares = jnp.exp(scores - highest)
        total = jnp.sum(shares, axis=-1, keepdims=True)
        results.append(nn(shares.astype(BF), values) * (1.0 / total))
        stats[...] = jnp.where(lanes == 2 * p + side, highest + jnp.log(total), stats[...])
    attended[:, col] = jnp.where(mask, results[0], results[1]).astype(BF)


def query_back(p, g, q_all, k_all, v_all, a_all, stats, pgrad, v_qv, tokens):
    col = pl.ds(mo(p * LANE, LANE), LANE)
    own = pl.ds(mo(g * tokens, 16), tokens)
    scale = jnp.asarray(HDIM**-0.5, BF)
    query, upstream = q_all[own, col] * scale, a_all[own, col]
    keys, values = k_all[:, col], v_all[:, col]
    mask = head_mask(tokens)
    zero = jnp.zeros_like(query)
    lanes = lax.broadcasted_iota(jnp.int32, (tokens, LANE), 1)
    results = []
    for side in range(2):
        def pick(v):
            return jnp.where(mask, v, zero) if side == 0 else jnp.where(mask, zero, v)
        total = jnp.sum(jnp.where(lanes == 2 * p + side, stats[...], 0.0), axis=-1, keepdims=True)
        centre = jnp.sum(jnp.where(lanes == HEADS + 2 * p + side, stats[...], 0.0), axis=-1, keepdims=True)
        shares = jnp.exp(nt(pick(query), keys) - total)
        back = (shares * (nt(pick(upstream), values) - centre)).astype(BF) * scale
        results.append(nn(back, keys))
    grad = jnp.where(mask, results[0], results[1])
    pgrad[:, col] = grad.astype(BF)
    v_qv[0:1, col] = jnp.sum(grad, axis=0, keepdims=True)


def key_back(p, g, q_all, k_all, v_all, a_all, rows, pgrad, v_qv, tokens):
    col = pl.ds(mo(p * LANE, LANE), LANE)
    own = pl.ds(mo(g * tokens, 16), tokens)
    scale = jnp.asarray(HDIM**-0.5, BF)
    keys, values = k_all[own, col] * scale, v_all[own, col]
    queries, upstream = q_all[:, col], a_all[:, col]
    mask = head_mask(tokens)
    zero = jnp.zeros_like(keys)
    ks, vs = [], []
    for side in range(2):
        def pick(v):
            return jnp.where(mask, v, zero) if side == 0 else jnp.where(mask, zero, v)
        total = rows[pl.ds(2 * p + side, 1), :]
        centre = rows[pl.ds(HEADS + 2 * p + side, 1), :]
        shares = jnp.exp(nt(pick(keys), queries) - total)
        vs.append(nn(shares.astype(BF), upstream))
        back = (shares * (nt(pick(values), upstream) - centre)).astype(BF) * scale
        ks.append(nn(back, queries))
    pgrad[:, pl.ds(mo(D + p * LANE, LANE), LANE)] = jnp.where(mask, ks[0], ks[1]).astype(BF)
    grad = jnp.where(mask, vs[0], vs[1])
    pgrad[:, pl.ds(mo(2 * D + p * LANE, LANE), LANE)] = grad.astype(BF)
    v_qv[0:1, pl.ds(mo(D + p * LANE, LANE), LANE)] = jnp.sum(grad, axis=0, keepdims=True)


def cell(ref, m, row, sub=None):
    r0, rn, c0, cn = m.sub[sub] if sub is not None else (0, m.quarter, 0, m.half)
    return ref.at[pl.ds(mo(row + r0, 16), rn), pl.ds(c0, cn)]


ORDER = (3, 2, 1, 0)


def layer_kernel(groups, highs, names, fr, ct, p_ref, oq, oo, ou, od, osm, out_frames, frames_grad, *scratch):
    s = types.SimpleNamespace(**dict(zip(names, scratch)))
    rep, g = lax.axis_index("rep"), lax.axis_index("grp")
    tokens = fr.shape[0]
    share_of = lax.rem(rep, 8)
    h = lax.rem(share_of, 2)
    k = share_of // 2
    x, y = lax.rem(k, 2), k // 2
    kx, ky, kd = flip(k, 1), flip(k, 2), 3 - k
    core, xn, yn = flip(rep, 1), flip(rep, 2), flip(rep, 4)
    full = (s.wq, s.wo, s.wu, s.wd)
    outs = (oq, oo, ou, od)
    grads = (s.wu, s.go, s.gu, s.gd)
    last = groups - 1

    def has_next(d):
        return g < last if d == 0 else g > 0

    def toward(d):
        return lax.rem(g + (1 if d == 0 else last), groups)

    def row_of(d, step):
        return g - 1 - step if d == 0 else g + 1 + step

    def valid(d, step):
        return row_of(d, step) >= 0 if d == 0 else row_of(d, step) <= last

    slots = [(d, step) for step in range(last) for d in range(2)]

    order = [(0, 0), (0, 1), (0, 2), (0, 3), (1, 0), (2, 0), (3, 0)] + [(t, i) for t in (1, 2, 3) for i in (1, 2, 3)]

    def piece_load(n):
        t, i = order[n]
        m = MATS[t]
        count = (m.quarter * m.tiles + (2 if m.shifted else 0)) * LANE
        start = mo((m.row0 + lax.rem(k + i, 4) * (m.quarter * m.tiles)) * LANE, LANE)
        return pltpu.make_async_copy(p_ref.at[:, pl.ds(start, count)], s.pbuf.at[n % 3, :, pl.ds(0, count)], s.lsem.at[n % 3])

    def relayout(n):
        t, i = order[n]
        m = MATS[t]
        piece_load(n).wait()
        count = m.quarter * m.tiles + (8 if m.shifted else 0)
        s.fbuf[0:count, :] = s.pbuf[n % 3, :, 0:count * LANE].astype(F32).reshape(count, LANE)
        if n + 3 < len(order):
            piece_load(n + 3).start()
        at = pl.ds(mo(g * m.block + lax.rem(k + i, 4) * m.quarter, 16), m.quarter)
        low = lax.broadcasted_iota(jnp.int32, (m.quarter, LANE), 1) < 64
        for c in range(m.tiles):
            a = s.fbuf[pl.ds(c, m.quarter, stride=m.tiles), :]
            if m.shifted:
                b = s.fbuf[pl.ds(c + 1, m.quarter, stride=m.tiles), :]
                a = pltpu.roll(jnp.where(low, b, a), 64, 1)
            full[t][at, c * LANE:(c + 1) * LANE] = a.astype(BF)

    def small_loads():
        at, result = 0, []
        for n, (first, count) in enumerate(SMALL):
            result.append(pltpu.make_async_copy(
                p_ref.at[:, pl.ds(first * LANE, count * LANE)], s.spbuf.at[:, pl.ds(at * LANE, count * LANE)], s.ssem.at[n]))
            at += count
        return result

    def zregion(t, r):
        if t == 4:
            return s.fa.at[pl.ds(mo(r * tokens, 16), tokens), :]
        return part(full[t], MATS[t], r, k, h)

    def zcopy(t, d, step, r):
        reg = zregion(t, r)
        return remote(reg, reg, s.zs.at[t, d, step], s.zr.at[t, d, step], rep, toward(d))

    def own_send(t):
        for d in range(2):
            @pl.when(has_next(d))
            def _():
                zcopy(t, d, 0, g).start()

    def xcopy(t, i, r, kk):
        reg = part(full[t], MATS[t], r, kk, h)
        return remote(reg, reg, s.xs.at[t, i], s.xr.at[t, i], xn, g)

    def ycopy(t, i, r, kk):
        reg = part(full[t], MATS[t], r, kk, h)
        return remote(reg, reg, s.ys.at[t, i], s.yr.at[t, i], yn, g)

    def acopy(t, i, r, kk):
        reg = part(full[t], MATS[t], r, kk, h, 0)
        return remote(reg, reg, s.fas.at[t, i], s.far.at[t, i], yn, g)

    def bcopy(t, i, r, kk):
        reg = part(full[t], MATS[t], r, kk, h, 1)
        return remote(reg, reg, s.fbs.at[t, i], s.fbr.at[t, i], xn, g)

    def ccopy(t, i, r, hh):
        reg = slab(full[t], MATS[t], r, hh)
        return remote(reg, reg, s.cs.at[t, i], s.cr.at[t, i], core, g)

    def stage(number, t, d, step):
        i = d * last + step

        @pl.when(valid(d, step))
        def _():
            r = row_of(d, step)
            if number == 0:
                zcopy(t, d, step, r).wait_recv()
                if step < last - 1:
                    @pl.when(has_next(d))
                    def _():
                        zcopy(t, d, step + 1, r).start()
                if t < 4:
                    xcopy(t, i, r, k).start()
                    ycopy(t, i, r, k).start()
            if number == 1:
                xcopy(t, i, r, kx).wait_recv()
                acopy(t, i, r, kx).start()
                ycopy(t, i, r, ky).wait_recv()
                bcopy(t, i, r, ky).start()
            if number == 2:
                acopy(t, i, r, kd).wait_recv()
                bcopy(t, i, r, kd).wait_recv()
                ccopy(t, i, r, h).start()
            if number == 3:
                ccopy(t, i, r, 1 - h).wait_recv()

    def both(number, t, step):
        for d in range(2):
            stage(number, t, d, step)

    def gather_sent():
        for t in range(5):
            for d in range(2):
                @pl.when(has_next(d))
                def _():
                    zcopy(t, d, 0, g).wait_send()
            for (d, step) in slots:
                i = d * last + step

                @pl.when(valid(d, step))
                def _():
                    r = row_of(d, step)
                    if step < last - 1:
                        @pl.when(has_next(d))
                        def _():
                            zcopy(t, d, step + 1, r).wait_send()
                    if t < 4:
                        xcopy(t, i, r, k).wait_send()
                        ycopy(t, i, r, k).wait_send()
                        acopy(t, i, r, kx).wait_send()
                        bcopy(t, i, r, ky).wait_send()
                        ccopy(t, i, r, h).wait_send()

    def vcopy(i, owner):
        return remote(s.smb, s.sm.at[owner], s.ms.at[i - 1], s.mr.at[i - 1], rep, lax.rem(g + i, groups))

    def place(r):
        return s.a_all.at[pl.ds(mo(r * tokens, 16), tokens), :]

    def scopy(d, step, r):
        return remote(place(r), place(r), s.szs.at[d, step], s.szr.at[d, step], rep, toward(d))

    def rcopy(i, owner):
        return remote(s.rows3.at[groups], s.rows3.at[owner], s.rs.at[i - 1], s.rr.at[i - 1], rep, lax.rem(g + i, groups))

    def share_start():
        for d in range(2):
            @pl.when(has_next(d))
            def _():
                scopy(d, 0, g).start()
        for i in range(1, groups):
            rcopy(i, g).start()

    def share_step(step):
        for d in range(2):
            @pl.when(valid(d, step))
            def _():
                r = row_of(d, step)
                scopy(d, step, r).wait_recv()
                if step < last - 1:
                    @pl.when(has_next(d))
                    def _():
                        scopy(d, step + 1, r).start()

    def share_rows():
        for i in range(1, groups):
            rcopy(i, lax.rem(g + groups - i, groups)).wait_recv()
        for i in range(groups):
            s.rows[:, i * tokens:(i + 1) * tokens] = s.rows3[i]
        s.rows[:, pl.ds(mo(g * tokens, LANE), tokens)] = s.rows3[groups]

    def share_sent():
        for d in range(2):
            @pl.when(has_next(d))
            def _():
                scopy(d, 0, g).wait_send()
            for step in range(last - 1):
                @pl.when(jnp.logical_and(valid(d, step), has_next(d)))
                def _():
                    scopy(d, step + 1, g).wait_send()
        for i in range(1, groups):
            rcopy(i, g).wait_send()

    def row(i):
        return lax.rem(g + 1 + i, groups)

    def first(t, i):
        m = MATS[t]
        at = pl.ds(mo(row(i) * m.block, 16), m.block)
        return remote(grads[t].at[at, pl.ds(mo((1 - h) * m.half, LANE), m.half)], s.buf1[t].at[at, :],
                      s.c1s.at[t, i], s.c1r.at[t, i], core, g)

    def cell1(t, i, kk, sub=None):
        return cell(s.buf1[t], MATS[t], row(i) * MATS[t].block + kk * MATS[t].quarter, sub)

    def cell2(t, i, j, sub):
        return cell(s.buf2[t], MATS[t], (row(i) * 2 + j) * MATS[t].quarter, sub)

    def cell3(t, i, sub=None):
        return cell(s.buf3[t], MATS[t], row(i) * MATS[t].quarter, sub)

    def a1(t, i, j, kk):
        return remote(cell1(t, i, kk, 0), cell2(t, i, j, 0), s.a1s.at[t, i, j], s.a1r.at[t, i, j], xn, g)

    def b1(t, i, j, kk):
        return remote(cell1(t, i, kk, 1), cell2(t, i, j, 1), s.b1s.at[t, i, j], s.b1r.at[t, i, j], yn, g)

    def a2(t, i, j):
        return remote(cell2(t, i, j, 0), cell3(t, i, 0), s.a2s.at[t, i], s.a2r.at[t, i], yn, g)

    def b2(t, i, j):
        return remote(cell2(t, i, j, 1), cell3(t, i, 1), s.b2s.at[t, i], s.b2r.at[t, i], xn, g)

    def z2(t, i):
        return remote(cell3(t, i), s.zbuf[t].at[i], s.z2s.at[t, i], s.z2r.at[t, i], rep, row(i))

    def r1(t, i):
        m = MATS[t]
        first(t, i).wait_recv()
        at = pl.ds(mo(row(i) * m.block, 16), m.block)
        mine = grads[t].at[at, pl.ds(mo(h * m.half, LANE), m.half)]
        add_rows(s.buf1[t].at[at, :], mine, s.buf1[t].at[at, :], m.block)
        for j in range(2):
            a1(t, i, j, 2 * j + (1 - x)).start()
            b1(t, i, j, 2 * (1 - y) + j).start()

    def r2(t, i):
        m = MATS[t]
        for j in range(2):
            a1(t, i, j, 2 * j + x).wait_recv()
            add_rows(cell2(t, i, j, 0), cell1(t, i, 2 * j + x, 0), cell2(t, i, j, 0), m.sub[0][1])
        a2(t, i, 1 - y).start()
        for j in range(2):
            b1(t, i, j, 2 * y + j).wait_recv()
            add_rows(cell2(t, i, j, 1), cell1(t, i, 2 * y + j, 1), cell2(t, i, j, 1), m.sub[1][1])
        b2(t, i, 1 - x).start()

    def r3(t, i):
        m = MATS[t]
        a2(t, i, y).wait_recv()
        b2(t, i, x).wait_recv()
        add_rows(cell3(t, i, 0), cell2(t, i, y, 0), cell3(t, i, 0), m.sub[0][1])
        add_rows(cell3(t, i, 1), cell2(t, i, x, 1), cell3(t, i, 1), m.sub[1][1])
        if i < last:
            z2(t, i).start()

    def fpart(t, kk, hh, sub=None):
        return part(outs[t], MATS[t], 0, kk, hh, sub)

    def keep(t):
        return pltpu.make_async_copy(s.fin[t].at[0], fpart(t, k, h), s.os.at[t])

    def xsend(t):
        return remote(s.fin[t].at[0], fpart(t, k, h), s.oxs.at[t], s.oxr.at[t], xn, g)

    def ysend(t):
        return remote(s.fin[t].at[0], fpart(t, k, h), s.oys.at[t], s.oyr.at[t], yn, g)

    def xgot(t):
        return remote(fpart(t, kx, h), fpart(t, kx, h), s.oxs.at[t], s.oxr.at[t], xn, g)

    def ygot(t):
        return remote(fpart(t, ky, h), fpart(t, ky, h), s.oys.at[t], s.oyr.at[t], yn, g)

    def fwd(t, sub, kk):
        reg = fpart(t, kk, h, sub)
        return remote(reg, reg, (s.oas, s.obs)[sub].at[t], (s.oar, s.obr)[sub].at[t], (yn, xn)[sub], g)

    def cross(t, hh):
        reg = slab(outs[t], MATS[t], 0, hh)
        return remote(reg, reg, s.ocs.at[t], s.ocr.at[t], core, g)

    def r4(t):
        m = MATS[t]
        for i in range(last):
            z2(t, i).wait_recv()
        mine = cell3(t, last)

        def body(n):
            at = pl.ds(mo(n * 16, 16), 16)
            total = mine[at, :].astype(F32)
            for i in range(last):
                total = total + s.zbuf[t][i, at, :].astype(F32)
            s.fin[t][0, at, :] = total.astype(BF)
        loop(m.quarter // 16, body)
        for b in range(highs):
            cp = remote(s.fin[t].at[0], s.fin[t].at[1 + b], s.fxs.at[t, b], s.fxr.at[t, b], flip(rep, 8 << b), g)
            cp.start()
            cp.wait()
            add_rows(s.fin[t].at[0], s.fin[t].at[0], s.fin[t].at[1 + b], m.quarter)
        keep(t).start()
        xsend(t).start()
        ysend(t).start()

    def r5(t):
        xgot(t).wait_recv()
        fwd(t, 0, kx).start()
        ygot(t).wait_recv()
        fwd(t, 1, ky).start()

    def r6(t):
        fwd(t, 0, kd).wait_recv()
        fwd(t, 1, kd).wait_recv()
        keep(t).wait()
        cross(t, h).start()

    partners = [(core, g), (xn, g), (yn, g)] + [(flip(rep, 8 << b), g) for b in range(highs)]
    bit = 1
    while bit < groups:
        partners.append((rep, flip(g, bit)))
        bit *= 2

    def smcopy(j):
        return remote(s.smacc.at[j], s.smin.at[j], s.sms.at[j], s.smr.at[j], *partners[j])

    def small(j):
        if j:
            smcopy(j - 1).wait_recv()
            s.smacc[j] = s.smacc[j - 1] + s.smin[j - 1]
        if j < len(partners):
            smcopy(j).start()
        else:
            osm[...] = s.smacc[j, g]

    def project(j):
        project_block(j, s.fa, s.gain1, s.shift1, s.qvbias, s.wq, s.q_all, s.k_all, s.v_all, s.normed, tokens)

    def attention(p):
        loop(2, lambda i: attend_pair(p + i, g, s.q_all, s.k_all, s.v_all, s.attended, s.stats, tokens))

    def block(n):
        return pl.ds(mo(n * 256, 256), 256)

    def to_middle():
        def body(n):
            c = block(n)
            s.middle[:, c] = nn(s.attended[...], s.wo[:, c]) + s.obias[0:1, c] + fr[:, c].astype(F32)
        loop(D // 256, body)
        value, inverse = normalize(s.middle[...])
        s.normal[...] = value
        s.inverse[...] = jnp.broadcast_to(inverse, (tokens, LANE))
        s.normed[...] = (value * s.gain2[...] + s.shift2[...]).astype(BF)

    def hidden():
        def body(n):
            c = block(n)
            u = nn(s.normed[...], s.wu[:, c]) + s.ubias[0:1, c]
            bell = 0.5 * (1.0 + lax.erf(u * ROOT_HALF))
            s.act[:, c] = (u * bell).astype(BF)
            slope = bell + u * jnp.exp(-0.5 * u * u) * ROOT_TWO_PI
            grad = nt(ct[...], s.wd[block(n), :]) * slope
            s.v_up[0:1, c] = jnp.sum(grad, axis=0, keepdims=True)
            s.pre[:, c] = grad.astype(BF)
        loop(FF // 256, body)

    def to_output():
        def body(n):
            c = block(n)
            out_frames[:, c] = (nn(s.act[...], s.wd[:, c]) + s.dbias[0:1, c] + s.middle[:, c]).astype(BF)
        loop(D // 256, body)

    def back_up():
        def body(n):
            s.wide[:, block(n)] = nt(s.pre[...], s.wu[block(n), :])
        loop(D // 256, body)

    def back_norm():
        upstream, normal = s.wide[...], s.normal[...]
        s.v_gain2[...] = jnp.sum(upstream * normal, axis=0, keepdims=True)
        s.v_shift2[...] = jnp.sum(upstream, axis=0, keepdims=True)
        total = ct[...].astype(F32) + norm_back(upstream, normal, s.inverse[:, 0:1], s.gain2[...])
        s.mgrad[...] = total
        s.half[...] = total.astype(BF)
        s.v_out[...] = jnp.sum(total, axis=0, keepdims=True)
        s.v_down[...] = jnp.sum(ct[...].astype(F32), axis=0, keepdims=True)

        def body(n):
            s.a_all[own, block(n)] = nt(s.half[...], s.wo[block(n), :]).astype(BF)
        own = pl.ds(mo(g * tokens, 16), tokens)
        loop(D // 256, body)
        lanes = lax.broadcasted_iota(jnp.int32, (tokens, LANE), 1)
        mask = head_mask(tokens)
        stats = s.stats[...]
        for p in range(HEADS // 2):
            c = slice(p * LANE, (p + 1) * LANE)
            product = s.a_all[own, c].astype(F32) * s.attended[:, c].astype(F32)
            for side in range(2):
                mine = jnp.where(mask if side == 0 else jnp.logical_not(mask), product, 0.0)
                stats = jnp.where(lanes == HEADS + 2 * p + side, jnp.sum(mine, axis=-1, keepdims=True), stats)
        s.stats[...] = stats
        s.rows3[groups] = stats.T[0:2 * HEADS, :]

    def weight(t, i, left, right):
        m = MATS[t]
        s.turned[0:m.block, :] = left[:, pl.ds(mo(row(i) * m.block, LANE if m.block % LANE == 0 else 64), m.block)].T

        def body(n):
            c = block(n)
            grads[t][pl.ds(mo(row(i) * m.block, 16), m.block), c] = nn(s.turned[0:m.block, :], right[:, c]).astype(BF)
        loop(m.cols // 256, body)
        first(t, i).start()

    def turn(left, out):
        out[...] = left[...].T

    def weight_from(t, i, left, right):
        m = MATS[t]
        at = pl.ds(mo(row(i) * m.block, 16), m.block)

        def body(n):
            c = block(n)
            grads[t][at, c] = nn(left[at, :], right[:, c]).astype(BF)
        loop(m.cols // 256, body)
        first(t, i).start()

    def queries(p):
        loop(2, lambda i: query_back(p + i, g, s.q_all, s.k_all, s.v_all, s.a_all, s.stats, s.pgrad, s.v_qv, tokens))

    def keys(p):
        loop(2, lambda i: key_back(p + i, g, s.q_all, s.k_all, s.v_all, s.a_all, s.rows, s.pgrad, s.v_qv, tokens))

    def to_inputs():
        normal, _ = normalize(fr[...].astype(F32))
        s.normed[...] = (normal * s.gain1[...] + s.shift1[...]).astype(BF)
        turn(s.normed, s.turned)

    def input_grad():
        def body(n):
            s.wide[:, block(n)] = nt(s.pgrad[...], s.wq[block(n), :])
        loop(D // 256, body)
        normal, inverse = normalize(fr[...].astype(F32))
        upstream = s.wide[...]
        s.v_gain1[...] = jnp.sum(upstream * normal, axis=0, keepdims=True)
        s.v_shift1[...] = jnp.sum(upstream, axis=0, keepdims=True)
        frames_grad[...] = (s.mgrad[...] + norm_back(upstream, normal, inverse, s.gain1[...])).astype(BF)
        fill_image(s.smacc.at[0], range(SROWS), (
            (GAIN_ONE, s.v_gain1), (SHIFT_ONE, s.v_shift1), (QV_BIAS, s.v_qv), (OUT_BIAS, s.v_out), (GAIN_TWO, s.v_gain2),
            (SHIFT_TWO, s.v_shift2), (UP_BIAS, s.v_up), (DOWN_BIAS, s.v_down)))
        small(0)

    barrier, peers = greet(rep, g, groups)
    peers += [(flip(rep, 8 << b), g) for b in range(highs)]
    for n in range(3):
        piece_load(n).start()
    for cp in small_loads():
        cp.start()
    own_frames = pltpu.make_async_copy(fr, zregion(4, g), s.ssem.at[len(SMALL)])
    own_frames.start()
    do_barrier(barrier, peers)
    relayout(0)
    own_send(0)
    for cp in small_loads():
        cp.wait()
    s.smb[...] = jnp.zeros_like(s.smb)
    count = sum(c for _, c in SMALL)
    s.smb[0:count, :] = s.spbuf[...].astype(F32).reshape(count, LANE)
    for i in range(1, groups):
        vcopy(i, g).start()
    own_frames.wait()
    both(0, 0, 0)
    both(0, 0, 1)
    own_send(4)
    for n in (1, 2, 3):
        relayout(n)
    both(0, 0, 2)
    for n in (4, 5, 6):
        relayout(n)
        own_send(n - 3)
    for step in range(last):
        both(1, 0, step)
    for n in (7, 8, 9):
        relayout(n)
    for step in range(last):
        both(2, 0, step)
    for i in range(1, groups):
        vcopy(i, lax.rem(g + groups - i, groups)).wait_recv()
    s.sm[g] = s.smb[...]
    for spot, ref in ((GAIN_ONE, s.gain1), (SHIFT_ONE, s.shift1), (QV_BIAS, s.qvbias), (GAIN_TWO, s.gain2), (SHIFT_TWO, s.shift2),
                      (OUT_BIAS, s.obias), (UP_BIAS, s.ubias), (DOWN_BIAS, s.dbias)):
        assemble(s.sm, spot, ref)
    s.stats[...] = jnp.zeros_like(s.stats)
    for n in (10, 11, 12):
        relayout(n)
    for step in range(last):
        both(3, 0, step)
    both(0, 4, 0)
    project(g)
    for n in (13, 14, 15):
        relayout(n)
    rest = [(t, step) for step in range(last) for t in (1, 2, 3)]
    for step in range(last):
        if step:
            both(0, 4, step)
        for t in (1, 2, 3):
            both(0, t, step)
        for d in range(2):
            @pl.when(valid(d, step))
            def _():
                project(row_of(d, step))
        for t in (1, 2, 3):
            both(1, t, step)
        if step:
            for t in (1, 2, 3):
                both(2, t, step - 1)
    attention(0)
    attention(2)
    for t in (1, 2, 3):
        both(2, t, last - 1)
    attention(4)
    for t, step in rest:
        both(3, t, step)
    to_middle()
    hidden()
    for i in range(groups):
        weight(3, i, s.act, ct)
    turn(s.normed, s.turned2)
    work = {
        0: [back_up], 1: [back_norm, share_start],
        2: [lambda: weight_from(2, 0, s.turned2, s.pre), lambda: weight_from(2, 1, s.turned2, s.pre)],
        3: [lambda: weight_from(2, 2, s.turned2, s.pre), lambda: weight_from(2, 3, s.turned2, s.pre), gather_sent],
        4: [lambda: share_step(0), lambda: turn(s.attended, s.turned2)]
        + [functools.partial(weight_from, 1, i, s.turned2, s.half) for i in range(groups)],
        5: [to_output, lambda: queries(0)],
        6: [lambda: share_step(1), lambda: queries(2)],
        7: [lambda: queries(4), to_inputs],
        8: [lambda: share_step(2), share_rows, lambda: keys(0)],
        9: [lambda: keys(2)],
        10: [lambda: keys(4)],
        11: [functools.partial(weight_from, 0, i, s.turned, s.pgrad) for i in range(groups)] + [input_grad],
    }
    chunks = [(t, i) for t in ORDER for i in range(groups)]
    total = len(chunks)
    smalls = 1
    for n in range(total + 16):
        if n < total:
            r1(*chunks[n])
        if 0 <= n - 2 < total:
            r2(*chunks[n - 2])
        if n > 12 and smalls <= len(partners):
            small(smalls)
            smalls += 1
        if 0 <= n - 4 < total:
            r3(*chunks[n - 4])
        for q, t in enumerate(ORDER):
            done = groups * q + groups - 1 + 4
            if n == done + 2:
                r4(t)
            if n == done + 4:
                r5(t)
            if n == done + 6:
                r6(t)
        for piece in work.get(n, ()):
            piece()
    for t in ORDER:
        cross(t, 1 - h).wait_recv()
    share_sent()
    for i in range(1, groups):
        vcopy(i, g).wait_send()
    for t, i in chunks:
        first(t, i).wait_send()
        for j in range(2):
            a1(t, i, j, 2 * j + x).wait_send()
            b1(t, i, j, 2 * y + j).wait_send()
        a2(t, i, y).wait_send()
        b2(t, i, x).wait_send()
        if i < last:
            z2(t, i).wait_send()
    for t in ORDER:
        xsend(t).wait_send()
        ysend(t).wait_send()
        fwd(t, 0, kx).wait_send()
        fwd(t, 1, ky).wait_send()
        cross(t, h).wait_send()
    for j in range(len(partners)):
        smcopy(j).wait_send()


def layer(frames, cotangent, params, groups, reps):
    dma = pltpu.SemaphoreType.DMA
    tokens = frames.shape[0]
    clip = tokens * groups
    highs = (reps // 8).bit_length() - 1
    steps = 3 + highs + groups.bit_length() - 1
    n = 2 * (groups - 1)

    def bf(*shape):
        return pltpu.VMEM(shape, BF)

    def wide(*shape):
        return pltpu.VMEM(shape, F32)

    scratch = {name: bf(m.block * groups, m.cols) for name, m in zip(("wq", "wo", "wu", "wd"), MATS)}
    scratch.update(go=bf(D, D), gu=bf(D, FF), gd=bf(FF, D))
    scratch.update(buf1=[bf(m.block * groups, m.half) for m in MATS], buf2=[bf(m.quarter * groups * 2, m.half) for m in MATS],
                   buf3=[bf(m.quarter * groups, m.half) for m in MATS], zbuf=[bf(groups - 1, m.quarter, m.half) for m in MATS],
                   fin=[bf(highs + 1, m.quarter, m.half) for m in MATS])
    scratch.update(fa=bf(clip, D), q_all=bf(clip, D), k_all=bf(clip, D), v_all=bf(clip, D), a_all=bf(clip, D))
    scratch.update(attended=bf(tokens, D), normed=bf(tokens, D), half=bf(tokens, D),
                   act=bf(tokens, FF), pre=bf(tokens, FF), pgrad=bf(tokens, 3 * D), turned=bf(D, tokens), turned2=bf(D, tokens))
    scratch.update(middle=wide(tokens, D), normal=wide(tokens, D), mgrad=wide(tokens, D), wide=wide(tokens, D),
                   inverse=wide(tokens, LANE), stats=wide(tokens, LANE))
    scratch.update(rows3=wide(groups + 1, 2 * HEADS, tokens), rows=wide(2 * HEADS, clip))
    scratch.update({name: wide(1, D) for name in ("gain1", "shift1", "gain2", "shift2", "obias", "dbias", "v_gain1", "v_shift1",
                                                  "v_gain2", "v_shift2", "v_out", "v_down")})
    scratch.update(qvbias=wide(1, 2 * D), v_qv=wide(1, 2 * D), ubias=wide(1, FF), v_up=wide(1, FF))
    piece = max(m.quarter * m.tiles + 8 for m in MATS)
    scratch.update(pbuf=bf(3, 1, piece * LANE), fbuf=wide(piece, LANE), spbuf=bf(1, sum(c for _, c in SMALL) * LANE),
                   smb=wide(SROWS, LANE), sm=wide(groups, SROWS, LANE),
                   smacc=wide(steps + 1, groups, SROWS, LANE), smin=wide(steps, groups, SROWS, LANE))
    scratch.update(lsem=dma((3,)), ssem=dma((len(SMALL) + 1,)), zs=dma((5, 2, groups)), zr=dma((5, 2, groups)))
    scratch.update({name: dma((4, n)) for name in ("xs", "xr", "ys", "yr", "fas", "far", "fbs", "fbr", "cs", "cr")})
    scratch.update({name: dma((groups,)) for name in ("ms", "mr", "rs", "rr")})
    scratch.update(szs=dma((2, groups)), szr=dma((2, groups)))
    scratch.update({name: dma((4, groups)) for name in ("c1s", "c1r", "a2s", "a2r", "b2s", "b2r", "z2s", "z2r")})
    scratch.update({name: dma((4, groups, 2)) for name in ("a1s", "a1r", "b1s", "b1r")})
    scratch.update({name: dma((4, max(highs, 1))) for name in ("fxs", "fxr")})
    scratch.update({name: dma((4,)) for name in ("os", "oxs", "oxr", "oys", "oyr", "oas", "oar", "obs", "obr", "ocs", "ocr")})
    scratch.update(sms=dma((steps,)), smr=dma((steps,)))
    vmem, hbm = pl.BlockSpec(memory_space=pltpu.VMEM), pl.BlockSpec(memory_space=pl.ANY)
    sds = jax.ShapeDtypeStruct
    names = tuple(scratch)
    flat, tree = jax.tree.flatten(list(scratch.values()))

    def body(*refs):
        fixed = 10
        layer_kernel(groups, highs, names, *refs[:fixed], *jax.tree.unflatten(tree, refs[fixed:]))

    return pl.pallas_call(
        body,
        out_shape=[sds((m.block, m.cols), BF) for m in MATS] + [sds((SROWS, LANE), F32), sds((tokens, D), BF), sds((tokens, D), BF)],
        in_specs=[vmem, vmem, hbm],
        out_specs=[hbm] * 4 + [vmem] * 3,
        scratch_shapes=flat,
        compiler_params=pltpu.CompilerParams(collective_id=0, has_side_effects=True, vmem_limit_bytes=67043328),
        name="layer",
    )(frames, cotangent, params)


BETA_ONE = 0.9
BETA_TWO = 0.98
ADAM_EPS = 1e-06
LEARN_RATE = 0.006
DECAY = 0.01
ADAM_STEP = 4
ROWS = 1736
STEPS = -(-FROWS // ROWS)


def flatten(m, block, flat, late):
    def body(i, carry):
        base = m.row0 + i * (48 * m.tiles)
        for c in range(m.tiles):
            tile = block[pl.ds(mo(i * 48, 16), 48), c * LANE:(c + 1) * LANE].astype(F32)
            if m.shifted:
                tile = pltpu.roll(tile, 64, 1)
                late[pl.ds(base + c + 1, 48, stride=m.tiles), :] = tile
            flat[pl.ds(base + c, 48, stride=m.tiles), :] = tile
        return carry
    lax.fori_loop(0, m.block // 48, body, 0)


def adam_kernel(scale, gq, go, gu, gd, sm, p_ref, m_ref, v_ref, o_g, o_p, o_m, o_v, flat, late):
    step = pl.program_id(0)

    @pl.when(step == 0)
    def _():
        flatten(QKV, gq, flat, late)
        flatten(OUT, go, flat, late)
        flatten(UP, gu, flat, late)
        flatten(DOWN, gd, flat, late)
        flat[0:3, :] = sm[0:3, :]
        flat[3459:3462, :] = sm[3:6, :]
        flat[4614:4618, :] = sm[6:10, :]
        flat[4618:4619, 0:64] = sm[10:11, 0:64]
        flat[9226:9227, 64:128] = sm[11:12, 64:128]
        flat[9227:9232, :] = sm[12:17, :]
        flat[9232:9233, 0:64] = sm[17:18, 0:64]
        flat[13840:13841, 64:128] = sm[18:19, 64:128]
        flat[13841:13842, :] = sm[19:20, :]
        late[9227:9232, :] = sm[12:17, :]
        late[9232:9233, 0:64] = sm[17:18, 0:64]
        late[13841:13842, :] = sm[19:20, :]

    at = pl.ds(mo(step * ROWS, 8), ROWS)
    number = step * ROWS + lax.broadcasted_iota(jnp.int32, (ROWS, LANE), 0)
    low = lax.broadcasted_iota(jnp.int32, (ROWS, LANE), 1) < 64
    grad = jnp.where(jnp.logical_and(number > UP.row0, low), late[at, :], flat[at, :]).reshape(1, ROWS * LANE) * scale
    first = BETA_ONE * m_ref[...] + (1.0 - BETA_ONE) * grad
    second = BETA_TWO * v_ref[...] + (1.0 - BETA_TWO) * grad * grad
    o_g[...] = grad
    o_m[...] = first
    o_v[...] = second
    first_hat = first * (1.0 / (1.0 - BETA_ONE**ADAM_STEP))
    second_hat = second * (1.0 / (1.0 - BETA_TWO**ADAM_STEP))
    current = p_ref[...].astype(F32)
    o_p[...] = current - LEARN_RATE * (first_hat / (jnp.sqrt(second_hat) + ADAM_EPS) + DECAY * current)


def adam(blocks, smalls, params, first, second, reps):
    spec = pl.BlockSpec((1, ROWS * LANE), lambda i: (0, i))
    vmem = pl.BlockSpec(memory_space=pltpu.VMEM)
    return pl.pallas_call(
        functools.partial(adam_kernel, 1.0 / reps),
        grid=(STEPS,),
        out_shape=[jax.ShapeDtypeStruct((1, FLAT), F32)] * 4,
        in_specs=[vmem] * 5 + [spec] * 3,
        out_specs=[spec] * 4,
        scratch_shapes=[pltpu.VMEM((STEPS * ROWS, LANE), F32)] * 2,
        compiler_params=pltpu.CompilerParams(vmem_limit_bytes=50 << 20),
        name="adam",
    )(*blocks, smalls, params, first, second)


def on_device(frames, cotangent, params, first_moment, second_moment):
    groups, reps = lax.axis_size("grp"), lax.axis_size("rep")
    *blocks, small, out_frames, frames_grad = layer(frames, cotangent, params, groups, reps)
    param_grad, new_params, new_first, new_second = adam(blocks, small, params, first_moment, second_moment, reps)
    return (out_frames, frames_grad, param_grad, new_params, new_first, new_second)


def solution(mesh):
    in_specs = (
        P(("rep", "grp"), None),
        P(("rep", "grp"), None),
        P("grp", None),
        P("grp", None),
        P("grp", None),
    )
    out_specs = (
        P(("rep", "grp"), None),
        P(("rep", "grp"), None),
        P("grp", None),
        P("grp", None),
        P("grp", None),
        P("grp", None),
    )
    return jax.shard_map(
        on_device, mesh=mesh, in_specs=in_specs, out_specs=out_specs, check_vma=False
    )
```

time: 287 us -> 237 us (0.83)
  Pallas kernels: 265 us -> 226 us
  local copies, waits for them, and re-layouts: 17.1 us -> 6.87 us
    pallas_call x4 -> x1, Pallas kernels: 240 us -> 201 us  [layer(): pl.pallas_call(body, out_shape=[sds((m.block, m.cols), BF) for m in MATS]...]
    unnamed x33 -> x16, local copies, waits for them, and re-layouts: 17.1 us -> 6.87 us
where the time goes in v4:
time: 237 us; the launch traced here: 233 us
  Pallas kernels  226 us (95%)
  local copies, waits for them, and re-layouts  6.87 us (3%)
    pallas_call x1, Pallas kernels, layer(): pl.pallas_call(body, out_shape=[sds((m.block, m.cols), BF) for m in MATS]...  201 us
    pallas_call x1, Pallas kernels, adam(): pl.pallas_call(functools.partial(adam_kernel, 1.0 / reps), grid=(STEPS,),...  24.7 us
    unnamed x16, local copies, waits for them, and re-layouts  6.87 us

profile of v4, /device:TPU:28, one launch (start us, length us, event | category | flops | bytes accessed | tf_op | source)
XLA Modules:
  0.0 233.4 jit_solution(15847617875614725494)
XLA Ops:
  0.6 201.2 %layer.1 = (bf16[192,2304]{1,0:T(8,128)(2,1)}, bf16[192,768]{1,0:T(8,128)(2,1)}, bf16[192,3072]{1,0:T(8,128)(2,1)}, bf16[768,768]{1,0:T(8,128)(2,1)}, f32[24,128...) custom-call(bf16[256,768]{1,0:T(8,128)(2,1)} %refs_0_.1, bf16[256,768]{1,0:T(8,128)(2,1)} %refs_1_.1, ...), custom_call_target="tpu_custom_call" | custom-call | tf_op jit(solution)/shard_map/layer/pallas_call | solution.py:899
  201.8 0.0 copy-start
  201.8 1.3 copy-done
  203.1 0.0 copy-start.1
  203.1 1.3 copy-done.1
  204.3 0.0 copy-start.2
  204.3 1.2 copy-done.2
  205.5 0.0 copy-start.3
  205.5 1.0 copy-done.3
  206.5 0.0 copy-start.4
  206.5 0.7 copy-done.4
  207.2 0.0 copy-start.6
  207.2 0.0 copy-start.5
  207.2 24.7 %adam.1 = (f32[1,1771776]{1,0:T(1,128)}, f32[1,1771776]{1,0:T(1,128)}, f32[1,1771776]{1,0:T(1,128)}, f32[1,1771776]{1,0:T(1,128)}) custom-call(bf16[192,2304]{1,0:T(8,128)(2,1)S(1)} %copy-done.2, bf16[192,768]{1,0:T(8,128)(2,1)S(1)} %copy-done.3, bf16[192,3072]{1,0:T(8,128)(2,1)S(1)} %copy-done, bf16[768,768]{1,0:T(8,128)(2,1)S(1)} %copy-done.1, ...), custom_call_target="tpu_custom_call" | custom-call | tf_op jit(solution)/shard_map/adam/pallas_call | solution.py:973
  231.9 0.0 copy-done.6
  231.9 0.7 copy.13
  232.6 0.0 copy-done.5
  232.6 0.7 copy.14
Async XLA Ops:
  201.8 1.3 copy-start
  203.1 1.3 copy-start.1
  204.3 1.2 copy-start.2
  205.5 1.0 copy-start.3
  206.5 0.7 copy-start.4
  207.2 24.7 %copy-start.6 = (bf16[256,768]{1,0:T(8,128)(2,1)S(1)}, bf16[256,768]{1,0:T(8,128)(2,1)}, u32[]{:S(2)}) copy-start(bf16[256,768]{1,0:T(8,128)(2,1)} %get-tuple-element.34) | copy-start | bytes 1179652
  207.2 25.4 %copy-start.5 = (bf16[256,768]{1,0:T(8,128)(2,1)S(1)}, bf16[256,768]{1,0:T(8,128)(2,1)}, u32[]{:S(2)}) copy-start(bf16[256,768]{1,0:T(8,128)(2,1)} %get-tuple-element.35) | copy-start | bytes 1179652
